TPU v7x, 32 devices: a whole 2x2x4 slice. The times are simulated.
32 devices in a mesh: dp: 4 (over x, y), fsdp: 8 (over z, core).
Axes of the slice: x: 2, y: 2, z: 4, core: 2. Of those that a mesh axis runs over, the one named last changes fastest.
Arguments:
- tokens: bfloat16 [256, 256, 2560], P(('dp', 'fsdp')), parts along dimension 0
- gain_in: bfloat16 [2560], P('fsdp')
- w_dq: bfloat16 [2560, 768], P('fsdp')
- gain_q: bfloat16 [768], P('fsdp')
- w_uq: bfloat16 [768, 3840], P('fsdp')
- w_dkv: bfloat16 [2560, 288], P('fsdp')
- gain_kv: bfloat16 [256], P('fsdp')
- w_ukv: bfloat16 [256, 5120], P('fsdp')
- w_out: bfloat16 [2560, 2560], P('fsdp')
Outputs:
- output 1: bfloat16 [256, 256, 2560], P(('dp', 'fsdp')), parts along dimension 0
- output 2: bfloat16 [256, 256, 256], P(('dp', 'fsdp')), parts along dimension 0
- output 3: bfloat16 [256, 256, 32], P(('dp', 'fsdp')), parts along dimension 0
There are 4 independent parts. A program takes and returns all parts, laid end to end along the dimension named above; an argument that names none is the same for every part.
All inputs are finite; a program needn't handle non-finite values.
Results may differ from a plain program's by a relative error of at most 0.00609399.
Values are sent between devices in bfloat16 or wider.
A program may use at most 1 GiB of HBM per device.

v0:
```python
import jax
import jax.numpy as jnp
from jax import lax
from jax.sharding import PartitionSpec as P, NamedSharding

EPSILON = 1e-6
ROPE_THETA = 10000.0


def rms_scale(values_in, gain_vec):
    values_f32 = values_in.astype(jnp.float32)
    inv_rms = lax.rsqrt(jnp.mean(values_f32 * values_f32, axis=-1, keepdims=True) + EPSILON)
    return values_f32 * inv_rms * gain_vec.astype(jnp.float32)


def rope_tables(seq_len, rope_dim):
    half_dim = rope_dim // 2
    inv_freq = ROPE_THETA ** (-2.0 * jnp.arange(half_dim, dtype=jnp.float32) / rope_dim)
    angles = jnp.arange(seq_len, dtype=jnp.float32)[:, None] * inv_freq[None, :]
    return jnp.cos(angles), jnp.sin(angles)


def apply_rope(values_in, cos_t, sin_t):
    half_dim = values_in.shape[-1] // 2
    lo_half = values_in[..., :half_dim]
    hi_half = values_in[..., half_dim:]
    return jnp.concatenate([lo_half * cos_t - hi_half * sin_t, hi_half * cos_t + lo_half * sin_t], axis=-1)


def head_dims(w_uq, w_dkv, gain_kv, w_ukv, w_out):
    rope_dim = w_dkv.shape[1] - gain_kv.shape[0]
    nope_total = w_ukv.shape[1] - w_out.shape[0]
    n_heads = (w_uq.shape[1] - nope_total) // rope_dim
    return n_heads, nope_total // n_heads, rope_dim, w_out.shape[0] // n_heads


def latents(tokens, gain_in, w_dq, gain_q, w_dkv, gain_kv, cos_t, sin_t):
    kv_rank = gain_kv.shape[0]
    normed = rms_scale(tokens, gain_in).astype(jnp.bfloat16)
    q_down = jnp.einsum('btd,dr->btr', normed, w_dq, preferred_element_type=jnp.float32)
    q_lat = rms_scale(q_down, gain_q).astype(jnp.bfloat16)
    kv_down = jnp.einsum('btd,dr->btr', normed, w_dkv, preferred_element_type=jnp.float32)
    latent = rms_scale(kv_down[:, :, :kv_rank], gain_kv).astype(jnp.bfloat16)
    k_pe = apply_rope(kv_down[:, :, kv_rank:], cos_t, sin_t).astype(jnp.bfloat16)
    return q_lat, latent, k_pe


def attend(q_lat, latent, k_pe, w_uq, w_ukv, w_out, head_info, cos_t, sin_t):
    n_heads, nope_dim, rope_dim, v_dim = head_info
    n_prompts = q_lat.shape[0]
    seq_len = q_lat.shape[1]
    q_full = jnp.einsum('btr,rc->btc', q_lat, w_uq, preferred_element_type=jnp.float32)
    q_full = q_full.reshape(n_prompts, seq_len, n_heads, nope_dim + rope_dim)
    q_nope = q_full[..., :nope_dim].astype(jnp.bfloat16)
    q_pe = apply_rope(q_full[..., nope_dim:], cos_t[:, None, :], sin_t[:, None, :]).astype(jnp.bfloat16)
    kv_up = jnp.einsum('btr,rc->btc', latent, w_ukv, preferred_element_type=jnp.float32).astype(jnp.bfloat16)
    kv_up = kv_up.reshape(n_prompts, seq_len, n_heads, nope_dim + v_dim)
    k_nope = kv_up[..., :nope_dim]
    values = kv_up[..., nope_dim:]
    score_scale = (nope_dim + rope_dim) ** -0.5
    scores = jnp.einsum('bqhd,bkhd->bhqk', q_nope, k_nope, preferred_element_type=jnp.float32)
    scores = scores + jnp.einsum('crie,cle->cirl', q_pe, k_pe, preferred_element_type=jnp.float32)
    causal = jnp.arange(seq_len)[:, None] >= jnp.arange(seq_len)[None, :]
    scores = jnp.where(causal, scores * score_scale, -1e30)
    attn_probs = jax.nn.softmax(scores, axis=-1).astype(jnp.bfloat16)
    attn_out = jnp.einsum('bhqk,bkhd->bqhd', attn_probs, values, preferred_element_type=jnp.float32).astype(jnp.bfloat16)
    attn_out = attn_out.reshape(n_prompts, seq_len, n_heads * v_dim)
    return jnp.einsum('btc,cd->btd', attn_out, w_out, preferred_element_type=jnp.float32)


def attend_each(q_lat, latent, k_pe, w_uq, w_ukv, w_out, head_info, cos_t, sin_t):
    def one_prompt(operands):
        q_one, lat_one, pe_one = operands
        return attend(q_one[None], lat_one[None], pe_one[None], w_uq, w_ukv, w_out, head_info, cos_t, sin_t)[0]

    return lax.map(one_prompt, (q_lat, latent, k_pe))


def solution(mesh):
    batch_spec = P(('dp', 'fsdp'))
    row_spec = P('fsdp')
    mat_spec = P('fsdp', None)

    def run_block(tokens, gain_in, w_dq, gain_q, w_uq, w_dkv, gain_kv, w_ukv, w_out):
        head_info = head_dims(w_uq, w_dkv, gain_kv, w_ukv, w_out)
        seq_len = tokens.shape[1]

        def local_block(tok_blk, gain_in_s, w_dq_s, gain_q_s, w_uq_s, w_dkv_s, gain_kv_s, w_ukv_s, w_out_s):
            cos_t, sin_t = rope_tables(seq_len, head_info[2])
            gain_in_all = lax.all_gather(gain_in_s, 'fsdp', tiled=True)
            w_dq_all = lax.all_gather(w_dq_s, 'fsdp', tiled=True)
            gain_q_all = lax.all_gather(gain_q_s, 'fsdp', tiled=True)
            w_dkv_all = lax.all_gather(w_dkv_s, 'fsdp', tiled=True)
            gain_kv_all = lax.all_gather(gain_kv_s, 'fsdp', tiled=True)
            q_lat, latent, k_pe = latents(tok_blk, gain_in_all, w_dq_all, gain_q_all, w_dkv_all, gain_kv_all, cos_t, sin_t)
            w_uq_all = lax.all_gather(w_uq_s, 'fsdp', tiled=True)
            w_ukv_all = lax.all_gather(w_ukv_s, 'fsdp', tiled=True)
            w_out_all = lax.all_gather(w_out_s, 'fsdp', tiled=True)
            proj_out = attend_each(q_lat, latent, k_pe, w_uq_all, w_ukv_all, w_out_all, head_info, cos_t, sin_t)
            y_blk = (tok_blk.astype(jnp.float32) + proj_out).astype(jnp.bfloat16)
            return y_blk, latent, k_pe

        mapped = jax.shard_map(
            local_block,
            mesh=mesh,
            in_specs=(batch_spec, row_spec, mat_spec, row_spec, mat_spec, mat_spec, row_spec, mat_spec, mat_spec),
            out_specs=(batch_spec, batch_spec, batch_spec),
            check_vma=False,
        )
        return mapped(tokens, gain_in, w_dq, gain_q, w_uq, w_dkv, gain_kv, w_ukv, w_out)

    return run_block
```

profile of v0, /device:TPU:0, one launch (start us, length us, event | category | flops | bytes accessed | tf_op | source)
XLA Modules:
  0.0 541.8 jit_solution(13997349392531779493)
XLA Ops:
  16.3 19.7 %all-reduce.3 = (bf16[2560]{0:T(1024)(128)(2,1)S(1)}, bf16[256]{0:T(256)(128)(2,1)S(1)}, bf16[768]{0:T(1024)(128)(2,1)S(1)}) all-reduce(bf16[2560]{0:T(1024)(128)(2,1)S(1)} %dynamic-update-slice, bf16[256]{0:T(256)(128)(2,1)S(1)} %dynamic-update-slice.1, bf16[768]{0:T(1024)(128)(2,1)S(1)} %dynamic-update-slice.2), channel_id=1, replica_groups=mesh['dp'=4,'fsdp'=8] {'fsdp'}, use_global_device_ids=true, to_apply=%add | all-reduce | flops 3584 | bytes 14336
  36.0 6.1 %fusion.33 = f32[8,256]{1,0:T(8,128)S(1)} fusion(bf16[8,256,2560]{2,1,0:T(8,128)(2,1)} %param.11), kind=kLoop, calls=%fused_computation.44 | loop fusion | flops 15726592 | bytes 10493952 | tf_op jit(solution)/shard_map/reduce_sum | solution.py:12
  46.7 6.6 %fusion.39 = f32[8,256,288]{1,2,0:T(8,128)S(1)} fusion(bf16[2560,288,1]{0,1,2:T(8,128)(2,1)} %reshape.199, bf16[8,256,2560]{2,1,0:T(8,128)(2,1)} %param.11, f32[2560]{0:T(1024)S(1)} %convert_element_type.48, f32[8,256]{1,0:T(8,128)S(1)} %add_rsqrt_fusion.2), kind=kOutput, calls=%fused_computation.49 | convolution fusion | flops 3040870400 | bytes 14338048 | tf_op jit(solution)/shard_map/btd,dr->btr/dot_general | solution.py:42
  55.1 30.1 %all-gather.9.cloned.1.call-done = bf16[2560,768]{1,0:T(8,128)(2,1)} async-done(((bf16[320,768]{1,0:T(8,128)(2,1)}), bf16[2560,768]{1,0:T(8,128)(2,1)}) %all-gather.9.cloned.1.call-update) | async-done | bytes 3932176 | tf_op jit(solution)/shard_map/all_gather | solution.py:91
  85.2 12.6 %multiply_reduce_fusion = (f32[8,256]{1,0:T(8,128)S(1)}, f32[8,256,768]{2,1,0:T(8,128)S(1)}) fusion(bf16[2560,768]{1,0:T(8,128)(2,1)} %all-gather.9.cloned.1.call-done, bf16[8,256,2560]{2,1,0:T(8,128)(2,1)} %param.11, f32[2560]{0:T(1024)S(1)} %convert_element_type.48, f32[8,256]{1,0:T(8,128)S(1)} %add_rsqrt_fusion.2), kind=kOutput, calls=%fused_computation.51 | convolution fusion | flops 8077178880 | bytes 20736000 | tf_op jit(solution)/shard_map/btd,dr->btr/dot_general | solution.py:40
  100.1 46.7 %all-gather.11.cloned.1.call-done = bf16[768,3840]{1,0:T(8,128)(2,1)} async-done(((bf16[96,3840]{1,0:T(8,128)(2,1)}), bf16[768,3840]{1,0:T(8,128)(2,1)}) %all-gather.11.cloned.1.call-update) | async-done | bytes 5898256 | tf_op jit(solution)/shard_map/all_gather | solution.py:96
  146.8 8.4 %copy.24 = bf16[768,3840]{0,1:T(8,128)(2,1)} copy(bf16[768,3840]{1,0:T(8,128)(2,1)} %all-gather.11.cloned.1.call-done) | data formatting | bytes 11796480
  155.2 25.4 %all-gather.7.cloned.1.call-done = bf16[256,5120]{1,0:T(8,128)(2,1)} async-done(((bf16[32,5120]{1,0:T(8,128)(2,1)}), bf16[256,5120]{1,0:T(8,128)(2,1)}) %all-gather.7.cloned.1.call-update) | async-done | bytes 2621456 | tf_op jit(solution)/shard_map/all_gather | solution.py:97
  180.6 121.4 %all-gather.13.cloned.1.call-done = bf16[2560,2560]{1,0:T(8,128)(2,1)} async-done(((bf16[320,2560]{1,0:T(8,128)(2,1)}), bf16[2560,2560]{1,0:T(8,128)(2,1)}) %all-gather.13.cloned.1.call-update) | async-done | bytes 13107216 | tf_op jit(solution)/shard_map/all_gather | solution.py:98
  302.0 217.6 %while.13 = (s32[]{:T(128)}, f32[8,256,2560]{2,1,0:T(8,128)}, bf16[8,256,256]{2,1,0:T(8,128)(2,1)}, bf16[256,5120]{1,0:T(8,128)(2,1)}, bf16[8,256,768]{2,1,0:T(8...) while((s32[]{:T(128)}, f32[8,256,2560]{2,1,0:T(8,128)}, ...), condition=%wide.region_6.7_spmd.clone.clone.clone, body=%wide.region_3.6_spmd.clone.clone.clone.sunk | while | flops 6403571712 | bytes 109078216 | solution.py:76
  307.3 4.7 convolution_bitcast_fusion.3
  321.1 8.2 %fusion.79 = f32[8,256,2560]{2,1,0:T(8,128)} fusion(f32[8,256,2560]{2,1,0:T(8,128)} %get-tuple-element.272, s32[]{:T(128)} %get-tuple-element.271, bf16[256,2560]{0,1:T(8,128)(2,1)S(1)} %bitcast.108, bf16[2560,2560]{1,0:T(8,128)(2,1)} %get-tuple-element.288), kind=kOutput, calls=%fused_computation.12.clone.1 | convolution fusion | flops 3355443200 | bytes 17039872 | tf_op jit(solution)/shard_map/while/body/eval_jaxpr/btc,cd->btd/dot_general | solution.py:68
  329.2 2.7 convolution_convert_fusion.2
  334.5 4.7 convolution_bitcast_fusion.3
  348.3 8.2 %fusion.79 = f32[8,256,2560]{2,1,0:T(8,128)} fusion(f32[8,256,2560]{2,1,0:T(8,128)} %get-tuple-element.272, s32[]{:T(128)} %get-tuple-element.271, bf16[256,2560]{0,1:T(8,128)(2,1)S(1)} %bitcast.108, bf16[2560,2560]{1,0:T(8,128)(2,1)} %get-tuple-element.288), kind=kOutput, calls=%fused_computation.12.clone.1 | convolution fusion | flops 3355443200 | bytes 17039872 | tf_op jit(solution)/shard_map/while/body/eval_jaxpr/btc,cd->btd/dot_general | solution.py:68
  356.5 2.7 convolution_convert_fusion.2
  361.7 4.7 convolution_bitcast_fusion.3
  375.5 8.2 %fusion.79 = f32[8,256,2560]{2,1,0:T(8,128)} fusion(f32[8,256,2560]{2,1,0:T(8,128)} %get-tuple-element.272, s32[]{:T(128)} %get-tuple-element.271, bf16[256,2560]{0,1:T(8,128)(2,1)S(1)} %bitcast.108, bf16[2560,2560]{1,0:T(8,128)(2,1)} %get-tuple-element.288), kind=kOutput, calls=%fused_computation.12.clone.1 | convolution fusion | flops 3355443200 | bytes 17039872 | tf_op jit(solution)/shard_map/while/body/eval_jaxpr/btc,cd->btd/dot_general | solution.py:68
  383.7 2.7 convolution_convert_fusion.2
  388.9 4.7 convolution_bitcast_fusion.3
  402.7 8.2 %fusion.79 = f32[8,256,2560]{2,1,0:T(8,128)} fusion(f32[8,256,2560]{2,1,0:T(8,128)} %get-tuple-element.272, s32[]{:T(128)} %get-tuple-element.271, bf16[256,2560]{0,1:T(8,128)(2,1)S(1)} %bitcast.108, bf16[2560,2560]{1,0:T(8,128)(2,1)} %get-tuple-element.288), kind=kOutput, calls=%fused_computation.12.clone.1 | convolution fusion | flops 3355443200 | bytes 17039872 | tf_op jit(solution)/shard_map/while/body/eval_jaxpr/btc,cd->btd/dot_general | solution.py:68
  410.9 2.7 convolution_convert_fusion.2
  416.2 4.7 convolution_bitcast_fusion.3
  429.9 8.2 %fusion.79 = f32[8,256,2560]{2,1,0:T(8,128)} fusion(f32[8,256,2560]{2,1,0:T(8,128)} %get-tuple-element.272, s32[]{:T(128)} %get-tuple-element.271, bf16[256,2560]{0,1:T(8,128)(2,1)S(1)} %bitcast.108, bf16[2560,2560]{1,0:T(8,128)(2,1)} %get-tuple-element.288), kind=kOutput, calls=%fused_computation.12.clone.1 | convolution fusion | flops 3355443200 | bytes 17039872 | tf_op jit(solution)/shard_map/while/body/eval_jaxpr/btc,cd->btd/dot_general | solution.py:68
  438.1 2.7 convolution_convert_fusion.2
  443.4 4.7 convolution_bitcast_fusion.3
  457.2 8.1 %fusion.79 = f32[8,256,2560]{2,1,0:T(8,128)} fusion(f32[8,256,2560]{2,1,0:T(8,128)} %get-tuple-element.272, s32[]{:T(128)} %get-tuple-element.271, bf16[256,2560]{0,1:T(8,128)(2,1)S(1)} %bitcast.108, bf16[2560,2560]{1,0:T(8,128)(2,1)} %get-tuple-element.288), kind=kOutput, calls=%fused_computation.12.clone.1 | convolution fusion | flops 3355443200 | bytes 17039872 | tf_op jit(solution)/shard_map/while/body/eval_jaxpr/btc,cd->btd/dot_general | solution.py:68
  470.6 4.7 convolution_bitcast_fusion.3
  484.3 8.1 %fusion.79 = f32[8,256,2560]{2,1,0:T(8,128)} fusion(f32[8,256,2560]{2,1,0:T(8,128)} %get-tuple-element.272, s32[]{:T(128)} %get-tuple-element.271, bf16[256,2560]{0,1:T(8,128)(2,1)S(1)} %bitcast.108, bf16[2560,2560]{1,0:T(8,128)(2,1)} %get-tuple-element.288), kind=kOutput, calls=%fused_computation.12.clone.1 | convolution fusion | flops 3355443200 | bytes 17039872 | tf_op jit(solution)/shard_map/while/body/eval_jaxpr/btc,cd->btd/dot_general | solution.py:68
  497.8 4.7 convolution_bitcast_fusion.3
  511.5 8.1 %fusion.79 = f32[8,256,2560]{2,1,0:T(8,128)} fusion(f32[8,256,2560]{2,1,0:T(8,128)} %get-tuple-element.272, s32[]{:T(128)} %get-tuple-element.271, bf16[256,2560]{0,1:T(8,128)(2,1)S(1)} %bitcast.108, bf16[2560,2560]{1,0:T(8,128)(2,1)} %get-tuple-element.288), kind=kOutput, calls=%fused_computation.12.clone.1 | convolution fusion | flops 3355443200 | bytes 17039872 | tf_op jit(solution)/shard_map/while/body/eval_jaxpr/btc,cd->btd/dot_general | solution.py:68
  519.6 15.6 %fusion.36 = bf16[8,256,2560]{2,1,0:T(8,128)(2,1)} fusion(f32[8,256,2560]{2,1,0:T(8,128)} %get-tuple-element.61, bf16[8,256,2560]{2,1,0:T(8,128)(2,1)} %param.11), kind=kLoop, calls=%fused_computation.47 | loop fusion | flops 15728640 | bytes 41943040 | tf_op jit(solution)/shard_map/convert_element_type | solution.py:100
  (120 shorter events, 116.3 us)
Async XLA Ops:
  7.2 35.1 %all-gather.15.cloned.1.call-start = ((), (), s32[]{:S(2)}) async-start(), calls=%async_computation.4 | async-start | bytes 1990656 | tf_op jit(solution)/shard_map/all_gather | solution.py:93
  7.9 77.3 %all-gather.9.cloned.1.call-start = ((), (), s32[]{:S(2)}) async-start(), calls=%async_computation.1 | async-start | bytes 4423680 | tf_op jit(solution)/shard_map/all_gather | solution.py:91
  8.6 138.1 %all-gather.11.cloned.1.call-start = ((), (), s32[]{:S(2)}) async-start(), calls=%async_computation.2 | async-start | bytes 6635520 | tf_op jit(solution)/shard_map/all_gather | solution.py:96
  9.4 171.2 %all-gather.7.cloned.1.call-start = ((), (), s32[]{:S(2)}) async-start(), calls=%async_computation | async-start | bytes 2949120 | tf_op jit(solution)/shard_map/all_gather | solution.py:97
  10.0 292.1 %all-gather.13.cloned.1.call-start = ((), (), s32[]{:S(2)}) async-start(), calls=%async_computation.3 | async-start | bytes 14745600 | tf_op jit(solution)/shard_map/all_gather | solution.py:98
  307.3 4.7 copy-start
  334.5 4.7 copy-start
  361.7 4.7 copy-start
  388.9 4.7 copy-start
  416.2 4.7 copy-start
  443.4 4.7 copy-start
  470.6 4.7 copy-start
  497.7 4.7 copy-start
  519.6 15.6 %copy-start.1 = (bf16[8,256,32]{1,2,0:T(8,128)(2,1)}, bf16[8,256,32]{1,2,0:T(8,128)(2,1)S(1)}, u32[]{:S(2)}) copy-start(bf16[8,256,32]{1,2,0:T(8,128)(2,1)S(1)} %get-tuple-element.307) | copy-start | bytes 393220
Sparse Core Ops, SparseCore 0:
  9.6 30.1 all-gather.14
  41.4 43.7 all-gather.8
  86.9 59.8 all-gather.10
  148.3 32.2 all-gather.6
  182.1 119.8 all-gather.12
where the time goes:
time: 543 us; the launch traced here: 542 us
  waiting for transfers between devices  227 us (42%)
  matrix products  193 us (36%)
  other arithmetic  46.7 us (9%)
  local copies, waits for them, and re-layouts  38.7 us (7%)
  blocking collectives  19.7 us (4%)
  between operations  15.9 us (3%)
    all_gather x1, waiting for transfers between devices, local_block(): w_out_all = lax.all_gather(w_out_s, 'fsdp', tiled=True)  121 us
    dot_general x8, matrix products, attend(): jnp.einsum('btc,cd->btd', attn_out, w_out, preferred_element_type=jnp.flo...  65.3 us
    all_gather x1, waiting for transfers between devices, local_block(): w_uq_all = lax.all_gather(w_uq_s, 'fsdp', tiled=True)  46.7 us
    dot_general x8, matrix products, attend(): jnp.einsum('btr,rc->btc', q_lat, w_uq, preferred_element_type=jnp.float32)  37.9 us
    all_gather x1, waiting for transfers between devices, local_block(): w_dq_all = lax.all_gather(w_dq_s, 'fsdp', tiled=True)  30.1 us
    all_gather x1, waiting for transfers between devices, local_block(): w_ukv_all = lax.all_gather(w_ukv_s, 'fsdp', tiled=True)  25.4 us
    dot_general x8, matrix products, attend(): jnp.einsum('btr,rc->btc', latent, w_ukv, preferred_element_type=jnp.float32)  21.3 us
    reshape x8, local copies, waits for them, and re-layouts, attend(): kv_up = kv_up.reshape(n_prompts, seq_len, n_heads, nope_dim + v_dim)  20.7 us
  transfers between devices with their start and end apart: 5, of which 4 were waited for; matrix products, arithmetic and copies ran while one was open for 9% of the time, Pallas kernels for 0%

commit v1 on v0

v1 whole, which is shorter than its diff:
```python
import functools

import jax
import jax.numpy as jnp
import numpy as np
from jax import lax
from jax.experimental import pallas as pl
from jax.experimental.pallas import tpu as pltpu
from jax.sharding import PartitionSpec as P

EPSILON = 1e-6
ROPE_THETA = 10000.0
LOG2E = 1.4426950408889634
VMEM_LIMIT = 64000 * 1024

NOPE, ROPE, VDIM = 64, 32, 64
HALF = ROPE // 2
GROUP = 8
PE_TILE = 4
LANES = 128


def rope_tiles(seq_len):
    inv_freq = ROPE_THETA ** (-2.0 * np.arange(HALF) / ROPE)
    angles = np.arange(seq_len)[:, None] * inv_freq[None, :]
    cos = np.tile(np.cos(angles), (1, LANES // HALF))
    sin = np.tile(np.sin(angles), (1, PE_TILE))
    return cos.astype(np.float32), np.concatenate([-sin, sin], axis=1).astype(np.float32)


def arrange_q(w):
    rows = w.shape[0]
    w = w.reshape(rows, -1, GROUP, NOPE + ROPE)
    nope = w[..., :NOPE].reshape(rows, -1, GROUP * NOPE)
    pe = w[..., NOPE:].reshape(rows, -1, GROUP // PE_TILE, PE_TILE, 2, HALF)
    pe = pe.transpose(0, 1, 2, 4, 3, 5).reshape(rows, -1, GROUP * ROPE)
    return jnp.concatenate([nope, pe], axis=-1).reshape(rows, -1)


def arrange_kv(w):
    rows = w.shape[0]
    return w.reshape(rows, -1, GROUP, 2, NOPE).transpose(0, 1, 3, 2, 4).reshape(rows, -1)


def arrange_dkv(w, kv_rank):
    lo, hi = w[:, kv_rank:kv_rank + HALF], w[:, kv_rank + HALF:]
    return jnp.concatenate([w[:, :kv_rank]] + [lo] * PE_TILE + [hi] * PE_TILE, axis=1)


def inv_rms(v):
    return lax.rsqrt(jnp.mean(v * v, axis=-1, keepdims=True) + EPSILON)


def rotate(tile, cos, sin):
    return tile * cos + pltpu.roll(tile, LANES // 2, 1) * sin


def down_kernel(x_ref, g1_ref, gq_ref, gkv_ref, wdq_ref, wdkv_ref, cos_ref, sin_ref, cq_ref, c_ref, rt_ref, r_ref):
    kv_rank = c_ref.shape[-1]
    for p in range(x_ref.shape[0]):
        x = x_ref[p].astype(jnp.float32)
        a = (x * inv_rms(x) * g1_ref[...]).astype(jnp.bfloat16)
        qd = jnp.dot(a, wdq_ref[...], preferred_element_type=jnp.float32)
        cq_ref[p] = (qd * inv_rms(qd) * gq_ref[...]).astype(jnp.bfloat16)
        kd = jnp.dot(a, wdkv_ref[...], preferred_element_type=jnp.float32)
        lat = kd[:, :kv_rank]
        c_ref[p] = (lat * inv_rms(lat) * gkv_ref[...]).astype(jnp.bfloat16)
        rt = rotate(kd[:, kv_rank:], cos_ref[...], sin_ref[...]).astype(jnp.bfloat16)
        rt_ref[p] = rt
        r_ref[p] = jnp.concatenate([rt[:, :HALF], rt[:, LANES // 2:LANES // 2 + HALF]], axis=1)


def attend_heads(q, kv, rt_slots, cos, sin, scale):
    seq_len = q.shape[0]
    half = seq_len // 2
    lane = lax.broadcasted_iota(jnp.int32, (1, LANES), 1)
    low = lane < NOPE
    diag = lax.broadcasted_iota(jnp.int32, (half, half), 0) >= lax.broadcasted_iota(jnp.int32, (half, half), 1)
    n_nope = GROUP * NOPE
    qn = q[:, :n_nope].astype(jnp.bfloat16)
    qp = [
        rotate(q[:, n_nope + t * LANES:n_nope + (t + 1) * LANES], cos, sin).astype(jnp.bfloat16)
        for t in range(GROUP // PE_TILE)
    ]
    kn = kv[:, :n_nope].astype(jnp.bfloat16)
    vv = kv[:, n_nope:].astype(jnp.bfloat16)
    zero = jnp.zeros((half, half), jnp.bfloat16)
    outs = []
    for quad in range(GROUP // 4):
        probs, vals = [], []
        for k in range(4):
            j = quad * 4 + k
            t, odd = j // 2, j % 2
            q_tile = jnp.concatenate([qn[:, t * LANES:(t + 1) * LANES], qp[j // PE_TILE]], axis=1)
            keep = low if odd == 0 else jnp.logical_not(low)
            k_tile = jnp.where(keep, kn[:, t * LANES:(t + 1) * LANES], 0)
            k_tile = jnp.concatenate([k_tile, rt_slots[j % PE_TILE]], axis=1)
            s = lax.dot_general(q_tile, k_tile, (((1,), (1,)), ((), ())), preferred_element_type=jnp.float32)
            s = s * scale
            top = jnp.where(diag, s[:half, :half], -1e30)
            left = s[half:, :half]
            right = jnp.where(diag, s[half:, half:], -1e30)
            m_top = jnp.max(top, axis=-1, keepdims=True)
            m_bot = jnp.max(jnp.maximum(left, right), axis=-1, keepdims=True)
            e_top = jnp.exp2(top - m_top)
            e_left = jnp.exp2(left - m_bot)
            e_right = jnp.exp2(right - m_bot)
            r_top = 1.0 / jnp.sum(e_top, axis=-1, keepdims=True)
            r_bot = 1.0 / jnp.sum(e_left + e_right, axis=-1, keepdims=True)
            p_top = jnp.concatenate([(e_top * r_top).astype(jnp.bfloat16), zero], axis=1)
            p_bot = jnp.concatenate([(e_left * r_bot).astype(jnp.bfloat16), (e_right * r_bot).astype(jnp.bfloat16)], axis=1)
            probs.append(jnp.concatenate([p_top, p_bot], axis=0))
            v_tile = jnp.where(keep, vv[:, t * LANES:(t + 1) * LANES], 0)
            blank = jnp.zeros_like(v_tile)
            vals.append(jnp.concatenate([v_tile, blank] if k < 2 else [blank, v_tile], axis=1))
        o = jnp.dot(
            jnp.concatenate(probs, axis=1), jnp.concatenate(vals, axis=0), preferred_element_type=jnp.float32
        )
        outs.append(o.astype(jnp.bfloat16))
    return jnp.concatenate(outs, axis=1)


def slot_masks(rt):
    lane = lax.broadcasted_iota(jnp.int32, (1, LANES), 1)
    slot = lax.rem(lane, LANES // 2) // HALF
    return [jnp.where(slot == j, rt, 0) for j in range(PE_TILE)]


def attend_kernel(cq_ref, c_ref, rt_ref, wuq_ref, wukv_ref, cos_ref, sin_ref, o_ref):
    n_groups = wuq_ref.shape[1] // (GROUP * (NOPE + ROPE))
    q_cols, kv_cols, o_cols = GROUP * (NOPE + ROPE), GROUP * (NOPE + VDIM), GROUP * VDIM
    scale = (NOPE + ROPE) ** -0.5 * LOG2E
    cq = cq_ref[0]
    lat = c_ref[0]
    slots = slot_masks(rt_ref[0])

    def body(g, carry):
        wq = wuq_ref[:, pl.ds(pl.multiple_of(g * q_cols, q_cols), q_cols)]
        wkv = wukv_ref[:, pl.ds(pl.multiple_of(g * kv_cols, kv_cols), kv_cols)]
        q = jnp.dot(cq, wq, preferred_element_type=jnp.float32)
        kv = jnp.dot(lat, wkv, preferred_element_type=jnp.float32)
        o = attend_heads(q, kv, slots, cos_ref[...], sin_ref[...], scale)
        o_ref[0, :, pl.ds(pl.multiple_of(g * o_cols, o_cols), o_cols)] = o
        return carry

    lax.fori_loop(0, n_groups, body, 0)


def out_kernel(x_ref, o_ref, w_ref, y_ref):
    step = 512
    o = o_ref[...]
    for n in range(0, y_ref.shape[1], step):
        acc = jnp.dot(o, w_ref[:, n:n + step], preferred_element_type=jnp.float32)
        y_ref[:, n:n + step] = (x_ref[:, n:n + step].astype(jnp.float32) + acc).astype(jnp.bfloat16)


def whole(shape):
    return pl.BlockSpec(shape, lambda i: (0,) * len(shape))


def solution(mesh):
    n_dp = mesh.shape['dp']
    params = pltpu.CompilerParams(vmem_limit_bytes=VMEM_LIMIT, dimension_semantics=("arbitrary",))

    def gather(w):
        rows = w.shape[0] // n_dp
        part = lax.dynamic_slice_in_dim(w, lax.axis_index('dp') * rows, rows, 0)
        return lax.all_gather(part, ('fsdp', 'dp'), tiled=True)

    def local_block(x, g1, wdq, gq, wuq, wdkv, gkv, wukv, wout):
        n_p, seq_len, d_model = x.shape
        kv_rank = gkv.shape[0] * mesh.shape['fsdp']
        cos_np, sin_np = rope_tiles(seq_len)
        cos, sin = jnp.asarray(cos_np), jnp.asarray(sin_np)
        gains = [lax.all_gather(g, 'fsdp', tiled=True).astype(jnp.float32)[None, :] for g in (g1, gq, gkv)]
        wdq_all = gather(wdq)
        wdkv_all = gather(arrange_dkv(wdkv, kv_rank))
        q_rank = wdq.shape[1]
        per = 2
        blk = lambda cols, n: pl.BlockSpec((n, seq_len, cols), lambda i: (i, 0, 0))
        out = lambda cols: jax.ShapeDtypeStruct((n_p, seq_len, cols), jnp.bfloat16)
        cq, c, rt, r = pl.pallas_call(
            down_kernel,
            grid=(n_p // per,),
            in_specs=[blk(d_model, per)] + [whole(v.shape) for v in (*gains, wdq_all, wdkv_all, cos, sin)],
            out_specs=[blk(q_rank, per), blk(kv_rank, per), blk(LANES, per), blk(ROPE, per)],
            out_shape=[out(q_rank), out(kv_rank), out(LANES), out(ROPE)],
            compiler_params=params,
            cost_estimate=pl.CostEstimate(flops=12_000_000_000, bytes_accessed=20_000_000, transcendentals=0),
            name="down",
        )(x, *gains, wdq_all, wdkv_all, cos, sin)
        wukv_all = gather(arrange_kv(wukv))
        wuq_all = gather(arrange_q(wuq))
        wout_all = gather(wout)
        o_cols = wout_all.shape[0]
        o = pl.pallas_call(
            attend_kernel,
            grid=(n_p,),
            in_specs=[blk(q_rank, 1), blk(kv_rank, 1), blk(LANES, 1)] + [whole(v.shape) for v in (wuq_all, wukv_all, cos, sin)],
            out_specs=blk(o_cols, 1),
            out_shape=out(o_cols),
            compiler_params=params,
            cost_estimate=pl.CostEstimate(flops=60_000_000_000, bytes_accessed=20_000_000, transcendentals=0),
            name="attend",
        )(cq, c, rt, wuq_all, wukv_all, cos, sin)
        rows = 512
        tile = pl.BlockSpec((rows, d_model), lambda i: (i, 0))
        y = pl.pallas_call(
            out_kernel,
            grid=(n_p * seq_len // rows,),
            in_specs=[tile, pl.BlockSpec((rows, o_cols), lambda i: (i, 0)), whole(wout_all.shape)],
            out_specs=tile,
            out_shape=jax.ShapeDtypeStruct((n_p * seq_len, d_model), jnp.bfloat16),
            compiler_params=params,
            cost_estimate=pl.CostEstimate(flops=27_000_000_000, bytes_accessed=45_000_000, transcendentals=0),
            name="project",
        )(x.reshape(n_p * seq_len, d_model), o.reshape(n_p * seq_len, o_cols), wout_all)
        return y.reshape(x.shape), c, r

    batch, row, mat = P(('dp', 'fsdp')), P('fsdp'), P('fsdp', None)
    return jax.shard_map(
        local_block,
        mesh=mesh,
        in_specs=(batch, row, mat, row, mat, mat, row, mat, mat),
        out_specs=(batch, batch, batch),
        check_vma=False,
    )
```

time: 543 us -> 405 us (0.75)
  matrix products: 193 us -> 0 us
  Pallas kernels: 0 us -> 138 us
  other arithmetic: 46.7 us -> 0.79 us
  local copies, waits for them, and re-layouts: 38.7 us -> 15.6 us
  waiting for transfers between devices: 227 us -> 215 us
    dot_general x50 -> x0, matrix products: 193 us -> none  [the longest x8 65.3 us: attend(): jnp.einsum('btc,cd->btd', attn_out, w_out, preferred_element_type=jnp.flo...]
    pallas_call x0 -> x3, Pallas kernels: none -> 138 us  [the longest x1 80.9 us: local_block(): pl.pallas_call(attend_kernel, grid=(n_p,), in_specs=[blk(q_rank, 1), blk(...]
    reduce_sum x10 -> x0, other arithmetic: 25.2 us -> none  [the longest x8 19 us: attend(): attn_probs = jax.nn.softmax(scores, axis=-1).astype(jnp.bfloat16)]
    reshape x8 -> x3, local copies, waits for them, and re-layouts: 20.7 us -> 1.94 us  [arrange_kv(): w.reshape(rows, -1, GROUP, 2, NOPE).transpose(0, 1, 3, 2, 4)]
    convert_element_type x6 -> x0, other arithmetic: 18.1 us -> none  [the longest x1 15.6 us: local_block(): y_blk = (tok_blk.astype(jnp.float32) + proj_out).astype(jnp.bfloat16)]
    unnamed x12 -> x26, local copies, waits for them, and re-layouts: 15.9 us -> 5.22 us
    all_gather x5, waiting for transfers between devices: 224 us -> 215 us  [gather(): return lax.all_gather(part, ('fsdp', 'dp'), tiled=True)]
  transfers between devices with their start and end apart: 5 -> 5, of which waited for: 4 -> 5; matrix products, arithmetic and copies ran while one was open for 9% -> 3% of each run, Pallas kernels for 0% -> 25%
where the time goes in v1:
time: 405 us
  waiting for transfers between devices  215 us (53%)
  Pallas kernels  138 us (34%)
  blocking collectives  18.8 us (5%)
  between operations  15.9 us (4%)
  local copies, waits for them, and re-layouts  15.6 us (4%)
    all_gather x5, waiting for transfers between devices, gather(): return lax.all_gather(part, ('fsdp', 'dp'), tiled=True)  215 us
    pallas_call x1, Pallas kernels, local_block(): pl.pallas_call(attend_kernel, grid=(n_p,), in_specs=[blk(q_rank, 1), blk(...  80.9 us
    pallas_call x1, Pallas kernels, local_block(): pl.pallas_call(out_kernel, grid=(n_p * seq_len // rows,), in_specs=[tile,...  35.6 us
    pallas_call x1, Pallas kernels, local_block(): pl.pallas_call(down_kernel, grid=(n_p // per,), in_specs=[blk(d_model, pe...  21.4 us
    unnamed x1, blocking collectives  18.8 us
  transfers between devices with their start and end apart: 5, of which 5 were waited for; matrix products, arithmetic and copies ran while one was open for 3% of the time, Pallas kernels for 25%

profile of v1, /device:TPU:0, one launch (start us, length us, event | category | flops | bytes accessed | tf_op | source)
XLA Modules:
  0.0 404.6 jit_solution(8277016069299042943)
XLA Ops:
  7.2 0.8 fusion
  8.0 1.0 slice.19
  9.0 0.7 slice.21
  10.0 0.2 copy.36
  10.4 0.3 concatenate.7
  10.6 0.6 constant_dynamic-slice_fusion.3
  11.4 0.7 constant_dynamic-slice_fusion.4
  12.1 1.4 reshape.42
  13.6 0.4 reshape.43
  14.1 0.7 constant_dynamic-slice_fusion.1
  14.8 0.6 copy.31
  15.7 0.2 pad_maximum_fusion
  15.9 0.4 constant_dynamic-slice_fusion.2
  16.2 1.0 copy.38
  17.3 1.8 constant_dynamic-slice_fusion
  19.1 0.6 dynamic-slice
  21.7 0.3 dynamic-update-slice
  21.9 0.2 dynamic-update-slice.1
  22.2 0.2 dynamic-update-slice.2
  22.4 18.8 %all-reduce.3 = (bf16[2560]{0:T(1024)(128)(2,1)S(1)}, bf16[768]{0:T(1024)(128)(2,1)S(1)}, bf16[256]{0:T(256)(128)(2,1)S(1)}) all-reduce(bf16[2560]{0:T(1024)(128)(2,1)S(1)} %dynamic-update-slice, bf16[768]{0:T(1024)(128)(2,1)S(1)} %dynamic-update-slice.1, bf16[256]{0:T(256)(128)(2,1)S(1)} %dynamic-update-slice.2), channel_id=1, replica_groups=mesh['dp'=4,'fsdp'=8] {'fsdp'}, use_global_device_ids=true, to_apply=%add | all-reduce | flops 3584 | bytes 14336
  41.2 0.6 reshape.46.g1_ref
  41.8 0.6 reshape.47.gq_ref
  42.4 0.6 broadcast_in_dim.23
  43.0 27.3 %all-gather.8.cloned.1.call-done.wdkv_ref = bf16[2560,384]{1,0:T(8,128)(2,1)} async-done(((bf16[80,384]{1,0:T(8,128)(2,1)}), bf16[2560,384]{1,0:T(8,128)(2,1)}) %all-gather.8.cloned.1.call-update) | async-done | bytes 1966096 | tf_op jit(solution)/shard_map/all_gather | solution.py:168
  70.3 63.8 %all-gather.6.cloned.1.call-done.wdq_ref = bf16[2560,768]{1,0:T(8,128)(2,1)} async-done(((bf16[80,768]{1,0:T(8,128)(2,1)}), bf16[2560,768]{1,0:T(8,128)(2,1)}) %all-gather.6.cloned.1.call-update) | async-done | bytes 3932176 | tf_op jit(solution)/shard_map/all_gather | solution.py:168
  134.0 21.4 %down.1 = (bf16[8,256,768]{2,1,0:T(8,128)(2,1)}, bf16[8,256,256]{2,1,0:T(8,128)(2,1)}, bf16[8,256,128]{2,1,0:T(8,128)(2,1)}, bf16[8,256,32]{2,1,0:T(8,128)(2,1)}) custom-call(bf16[8,256,2560]{2,1,0:T(8,128)(2,1)} %x_ref.1, f32[1,2560]{1,0:T(1,128)} %reshape.46.g1_ref, f32[1,768]{1,0:T(1,128)} %reshape.47.gq_ref, f32[1,256]{1,0:T(1,128)} %bitcast.29, ...), custom_call_target="tpu_custom_call" | custom-call | flops 12000000000 | bytes 20000000 | tf_op jit(solution)/shard_map/down/pallas_call | solution.py:182
  155.4 1.9 copy.35
  157.3 36.1 %all-gather.12.cloned.1.call-done.wukv_ref = bf16[256,5120]{1,0:T(8,128)(2,1)} async-done(((bf16[8,5120]{1,0:T(8,128)(2,1)}), bf16[256,5120]{1,0:T(8,128)(2,1)}) %all-gather.12.cloned.1.call-update) | async-done | bytes 2621456 | tf_op jit(solution)/shard_map/all_gather | solution.py:168
  193.4 69.7 %all-gather.10.cloned.1.call-done.wuq_ref = bf16[768,3840]{1,0:T(8,128)(2,1)} async-done(((bf16[24,3840]{1,0:T(8,128)(2,1)}), bf16[768,3840]{1,0:T(8,128)(2,1)}) %all-gather.10.cloned.1.call-update) | async-done | bytes 5898256 | tf_op jit(solution)/shard_map/all_gather | solution.py:168
  263.2 80.9 %attend.1 = bf16[8,256,2560]{2,1,0:T(8,128)(2,1)} custom-call(bf16[8,256,768]{2,1,0:T(8,128)(2,1)} %get-tuple-element.7.cq_ref, bf16[8,256,256]{2,1,0:T(8,128)(2,1)} %get-tuple-element.15.c_ref, bf16[8,256,128]{2,1,0:T(8,128)(2,1)} %get-tuple-element.9.rt_ref, bf16[768,3840]{1,0:T(8,128)(2,1)} %all-gather.10.cloned.1.call-done.wuq_ref, ...), custom_call_target="tpu_custom_call" | custom-call | flops 60000002048 | bytes 20000000 | tf_op jit(solution)/shard_map/attend/pallas_call | solution.py:196
  344.0 18.4 %all-gather.14.cloned.1.call-done.w_ref = bf16[2560,2560]{1,0:T(8,128)(2,1)} async-done(((bf16[80,2560]{1,0:T(8,128)(2,1)}), bf16[2560,2560]{1,0:T(8,128)(2,1)}) %all-gather.14.cloned.1.call-update) | async-done | bytes 13107216 | tf_op jit(solution)/shard_map/all_gather | solution.py:168
  362.4 35.6 %project.1 = bf16[2048,2560]{1,0:T(8,128)(2,1)} custom-call(bf16[2048,2560]{1,0:T(8,128)(2,1)} %bitcast.26, bf16[2048,2560]{1,0:T(8,128)(2,1)} %bitcast.28, bf16[2560,2560]{1,0:T(8,128)(2,1)} %all-gather.14.cloned.1.call-done.w_ref), custom_call_target="tpu_custom_call" | custom-call | flops 27000000512 | bytes 45000000 | tf_op jit(solution)/shard_map/project/pallas_call | solution.py:208
  (34 shorter events, 0.9 us)
Async XLA Ops:
  7.2 4.2 %copy-start = (bf16[320,768]{1,0:T(8,128)(2,1)S(1)}, bf16[320,768]{1,0:T(8,128)(2,1)}, u32[]{:S(2)}) copy-start(bf16[320,768]{1,0:T(8,128)(2,1)} %param.13) | copy-start | bytes 1474564
  7.2 63.1 %all-gather.8.cloned.1.call-start = ((), (), s32[]{:S(2)}) async-start(), calls=%async_computation.1 | async-start | bytes 2027520 | tf_op jit(solution)/shard_map/all_gather | solution.py:168
  8.0 6.8 %copy-start.2 = (bf16[96,3840]{1,0:T(8,128)(2,1)S(1)}, bf16[96,3840]{1,0:T(8,128)(2,1)}, u32[]{:S(2)}) copy-start(bf16[96,3840]{1,0:T(8,128)(2,1)} %param.15) | copy-start | bytes 2211844
  11.3 122.8 %all-gather.6.cloned.1.call-start = ((), (), s32[]{:S(2)}) async-start(), calls=%async_computation | async-start | bytes 4055040 | tf_op jit(solution)/shard_map/all_gather | solution.py:168
  12.0 181.4 %all-gather.12.cloned.1.call-start = ((), (), s32[]{:S(2)}) async-start(), calls=%async_computation.3 | async-start | bytes 2703360 | tf_op jit(solution)/shard_map/all_gather | solution.py:168
  14.7 248.4 %all-gather.10.cloned.1.call-start = ((), (), s32[]{:S(2)}) async-start(), calls=%async_computation.2 | async-start | bytes 6082560 | tf_op jit(solution)/shard_map/all_gather | solution.py:168
  15.6 3.5 copy-start.6
  15.6 6.0 %copy-start.3 = (bf16[320]{0:T(512)(128)(2,1)S(1)}, bf16[320]{0:T(512)(128)(2,1)}, u32[]{:S(2)}) copy-start(bf16[320]{0:T(512)(128)(2,1)} %param.12) | copy-start | bytes 1924
  15.6 6.3 %copy-start.4 = (bf16[96]{0:T(256)(128)(2,1)S(1)}, bf16[96]{0:T(256)(128)(2,1)}, u32[]{:S(2)}) copy-start(bf16[96]{0:T(256)(128)(2,1)} %param.14) | copy-start | bytes 580
  15.6 6.5 %copy-start.5 = (bf16[32]{0:T(256)(128)(2,1)S(1)}, bf16[32]{0:T(256)(128)(2,1)}, u32[]{:S(2)}) copy-start(bf16[32]{0:T(256)(128)(2,1)} %param.17) | copy-start | bytes 196
  17.2 345.2 %all-gather.14.cloned.1.call-start = ((), (), s32[]{:S(2)}) async-start(), calls=%async_computation.4 | async-start | bytes 13516800 | tf_op jit(solution)/shard_map/all_gather | solution.py:168
  362.4 35.6 %copy-start.1 = (bf16[320,768]{1,0:T(8,128)(2,1)S(1)}, bf16[320,768]{1,0:T(8,128)(2,1)}, u32[]{:S(2)}) copy-start(bf16[320,768]{1,0:T(8,128)(2,1)} %param.13) | copy-start | bytes 1474564
Sparse Core Ops, SparseCore 0:
  11.6 58.6 all-gather.7
  73.8 60.1 all-gather.5
  136.9 56.4 all-gather.11
  196.3 66.8 all-gather.9
  265.9 96.5 all-gather.13

commit v2 on v1

v2 whole, which is shorter than its diff:
```python
import functools

import jax
import jax.numpy as jnp
import numpy as np
from jax import lax
from jax.experimental import pallas as pl
from jax.experimental.pallas import tpu as pltpu
from jax.sharding import PartitionSpec as P

EPSILON = 1e-6
ROPE_THETA = 10000.0
LOG2E = 1.4426950408889634
VMEM_LIMIT = 64000 * 1024

NOPE, ROPE, VDIM = 64, 32, 64
HALF = ROPE // 2
GROUP = 8
PE_TILE = 4
LANES = 128


def rope_tiles(seq_len):
    inv_freq = ROPE_THETA ** (-2.0 * np.arange(HALF) / ROPE)
    angles = np.arange(seq_len)[:, None] * inv_freq[None, :]
    cos = np.tile(np.cos(angles), (1, LANES // HALF))
    sin = np.tile(np.sin(angles), (1, PE_TILE))
    return cos.astype(np.float32), np.concatenate([-sin, sin], axis=1).astype(np.float32)


def arrange_q(w):
    rows = w.shape[0]
    w = w.reshape(rows, -1, GROUP, NOPE + ROPE)
    nope = w[..., :NOPE].reshape(rows, -1, GROUP * NOPE)
    pe = w[..., NOPE:].reshape(rows, -1, GROUP // PE_TILE, PE_TILE, 2, HALF)
    pe = pe.transpose(0, 1, 2, 4, 3, 5).reshape(rows, -1, GROUP * ROPE)
    return jnp.concatenate([nope, pe], axis=-1).reshape(rows, -1)


def arrange_kv(w):
    rows = w.shape[0]
    return w.reshape(rows, -1, GROUP, 2, NOPE).transpose(0, 1, 3, 2, 4).reshape(rows, -1)


def arrange_dkv(w, kv_rank):
    lo, hi = w[:, kv_rank:kv_rank + HALF], w[:, kv_rank + HALF:]
    return jnp.concatenate([w[:, :kv_rank]] + [lo] * PE_TILE + [hi] * PE_TILE, axis=1)


def inv_rms(v):
    return lax.rsqrt(jnp.mean(v * v, axis=-1, keepdims=True) + EPSILON)


def rotate(tile, cos, sin):
    return tile * cos + pltpu.roll(tile, LANES // 2, 1) * sin


def attend_heads(q, kv, rt_slots, cos, sin, scale):
    seq_len = q.shape[0]
    half = seq_len // 2
    lane = lax.broadcasted_iota(jnp.int32, (1, LANES), 1)
    low = lane < NOPE
    diag = lax.broadcasted_iota(jnp.int32, (half, half), 0) >= lax.broadcasted_iota(jnp.int32, (half, half), 1)
    n_nope = GROUP * NOPE
    qn = q[:, :n_nope].astype(jnp.bfloat16)
    qp = [
        rotate(q[:, n_nope + t * LANES:n_nope + (t + 1) * LANES], cos, sin).astype(jnp.bfloat16)
        for t in range(GROUP // PE_TILE)
    ]
    kn = kv[:, :n_nope].astype(jnp.bfloat16)
    vv = kv[:, n_nope:].astype(jnp.bfloat16)
    zero = jnp.zeros((half, half), jnp.bfloat16)
    outs = []
    for quad in range(GROUP // 4):
        probs, vals = [], []
        for k in range(4):
            j = quad * 4 + k
            t, odd = j // 2, j % 2
            q_tile = jnp.concatenate([qn[:, t * LANES:(t + 1) * LANES], qp[j // PE_TILE]], axis=1)
            keep = low if odd == 0 else jnp.logical_not(low)
            k_tile = jnp.where(keep, kn[:, t * LANES:(t + 1) * LANES], 0)
            k_tile = jnp.concatenate([k_tile, rt_slots[j % PE_TILE]], axis=1)
            s = lax.dot_general(q_tile, k_tile, (((1,), (1,)), ((), ())), preferred_element_type=jnp.float32)
            s = s * scale
            top = jnp.where(diag, s[:half, :half], -1e30)
            left = s[half:, :half]
            right = jnp.where(diag, s[half:, half:], -1e30)
            m_top = jnp.max(top, axis=-1, keepdims=True)
            m_bot = jnp.max(jnp.maximum(left, right), axis=-1, keepdims=True)
            e_top = jnp.exp2(top - m_top)
            e_left = jnp.exp2(left - m_bot)
            e_right = jnp.exp2(right - m_bot)
            r_top = 1.0 / jnp.sum(e_top, axis=-1, keepdims=True)
            r_bot = 1.0 / jnp.sum(e_left + e_right, axis=-1, keepdims=True)
            p_top = jnp.concatenate([(e_top * r_top).astype(jnp.bfloat16), zero], axis=1)
            p_bot = jnp.concatenate([(e_left * r_bot).astype(jnp.bfloat16), (e_right * r_bot).astype(jnp.bfloat16)], axis=1)
            probs.append(jnp.concatenate([p_top, p_bot], axis=0))
            v_tile = jnp.where(keep, vv[:, t * LANES:(t + 1) * LANES], 0)
            blank = jnp.zeros_like(v_tile)
            vals.append(jnp.concatenate([v_tile, blank] if k < 2 else [blank, v_tile], axis=1))
        o = jnp.dot(
            jnp.concatenate(probs, axis=1), jnp.concatenate(vals, axis=0), preferred_element_type=jnp.float32
        )
        outs.append(o.astype(jnp.bfloat16))
    return jnp.concatenate(outs, axis=1)


def slot_masks(rt):
    lane = lax.broadcasted_iota(jnp.int32, (1, LANES), 1)
    slot = lax.rem(lane, LANES // 2) // HALF
    return [jnp.where(slot == j, rt, 0) for j in range(PE_TILE)]


MESH = pl.DeviceIdType.MESH
GROUPS_FIRST = 2
GAIN_ROWS = 32
N_SEND, N_RECV = 19, 19


class Item:
    def __init__(self, index, shard, col, cols, full):
        self.index, self.shard, self.col, self.cols, self.full = index, shard, col, cols, full
        self.rows = shard.shape[0]
        if (self.rows // 4) % 16 == 0:
            self.q_rows, self.q_cols = self.rows // 4, cols
        elif (cols // 4) % LANES == 0 and self.rows == 32:
            self.q_rows, self.q_cols = self.rows, cols // 4
        else:
            self.q_rows, self.q_cols = self.rows // 2, cols // 2
        if self.q_rows == self.rows:
            n = self.q_rows // 2
            self.halves = [(0, n, 0, self.q_cols), (n, n, 0, self.q_cols)]
        else:
            n = -(-self.q_cols // (2 * LANES)) * LANES
            self.halves = [(0, self.q_rows, 0, n), (0, self.q_rows, n, self.q_cols - n)]

    def quarter(self, q):
        per_row = self.cols // self.q_cols
        return (q // per_row) * self.q_rows, lax.rem(q, per_row) * self.q_cols

    def source(self, q):
        r, c = self.quarter(q)
        return self.shard.at[pl.ds(pl.multiple_of(r, 16), self.q_rows), pl.ds(pl.multiple_of(self.col + c, LANES), self.q_cols)]

    def own(self):
        return self.shard.at[:, pl.ds(self.col, self.cols)]

    def place(self, f, q=None, half=None):
        r, c = (0, 0) if q is None else self.quarter(q)
        r = f * self.rows + r
        if q is None:
            n_r, n_c = self.rows, self.cols
        elif half is None:
            n_r, n_c = self.q_rows, self.q_cols
        else:
            dr, n_r, dc, n_c = self.halves[half]
            r, c = r + dr, c + dc
        if n_c == self.cols:
            return self.full.at[pl.ds(pl.multiple_of(r, 16), n_r)]
        return self.full.at[pl.ds(pl.multiple_of(r, 16), n_r), pl.ds(pl.multiple_of(c, LANES), n_c)]


def core_kernel(
    n_prompts, x_ref, gs_ref, dq_s, dkv_s, uq_s, ukv_s, out_s, cos_ref, sin_ref,
    c_ref, r_ref, oa_ref, ob_ref, wout_ref,
    wdq, wdkv, wuqa, wuqb, wukva, wukvb, gains, gvec, cq_all, c_all, rt_all, stage,
    send_sem, recv_sem, g_send, g_recv, local_sem,
):
    i = pl.program_id(0)
    d, f = lax.axis_index('dp'), lax.axis_index('fsdp')
    z, core = f // 2, lax.rem(f, 2)
    dx = lax.rem(d + 2, 4)
    dy = d + 1 - 2 * lax.rem(d, 2)
    dd = lax.rem(dy + 2, 4)
    sib = z * 2 + 1 - core
    n_a = wuqa.shape[1]
    m_a = wukva.shape[1]
    dkv = Item(0, dkv_s, 0, wdkv.shape[1], wdkv)
    dq = Item(1, dq_s, 0, wdq.shape[1], wdq)
    ukva = Item(2, ukv_s, 0, m_a, wukva)
    uqa = Item(3, uq_s, 0, n_a, wuqa)
    ukvb = Item(4, ukv_s, m_a, wukvb.shape[1], wukvb)
    uqb = Item(5, uq_s, n_a, wuqb.shape[1], wuqb)
    wo = Item(6, out_s, 0, wout_ref.shape[1], wout_ref)
    items = [dkv, dq, ukva, uqa, ukvb, uqb, wo]

    def to(k):
        return lax.rem(z + k, 4) * 2 + core

    def origin(k):
        return lax.rem(z + 4 - k, 4) * 2 + core

    def copy(it, src, dst, s, r, dev):
        return pltpu.make_async_remote_copy(
            src_ref=src, dst_ref=dst, send_sem=send_sem.at[it.index, s], recv_sem=recv_sem.at[it.index, r],
            device_id=dev, device_id_type=MESH,
        )

    def along_z(it, k):
        return copy(it, it.source(d), it.place(f, d), k - 1, k - 1, (d, to(k)))

    def to_x(it, k):
        ref = it.place(origin(k), d)
        return copy(it, ref, ref, 2 + k, 2 + k, (dx, f))

    def to_y(it, k):
        ref = it.place(origin(k), d)
        return copy(it, ref, ref, 5 + k, 5 + k, (dy, f))

    def diag_y(it, k):
        ref = it.place(origin(k), dx, 0)
        return copy(it, ref, ref, 8 + k, 8 + k, (dy, f))

    def diag_x(it, k):
        ref = it.place(origin(k), dy, 1)
        return copy(it, ref, ref, 11 + k, 11 + k, (dx, f))

    def to_core(it, k):
        ref = it.place(origin(k))
        return copy(it, ref, ref, 14 + k, 14 + k, (d, sib))

    def own_copy(it):
        return copy(it, it.own(), it.place(f), 18, 18, (d, sib))

    def arrived(it, ref, r):
        return copy(it, ref, ref, 0, r, (d, f)).wait_recv()

    def keep(it):
        return pltpu.make_async_copy(it.own(), stage if it is wo else it.place(f), local_sem.at[it.index])

    def keep_out():
        return pltpu.make_async_copy(stage, wo.place(f), local_sem.at[7])

    def gain_copy(j):
        return pltpu.make_async_remote_copy(
            src_ref=gs_ref, dst_ref=gains.at[f], send_sem=g_send.at[j - 1], recv_sem=g_recv.at[j - 1],
            device_id=(d, lax.rem(f + j, 8)), device_id_type=MESH,
        )

    def a2(it, ks=(1, 2, 3)):
        for k in ks:
            arrived(it, it.place(origin(k), d), k - 1)
            to_x(it, k).start()
            to_y(it, k).start()

    def a3(it, ks=(1, 2, 3)):
        for k in ks:
            arrived(it, it.place(origin(k), dx), 2 + k)
            diag_y(it, k).start()
            arrived(it, it.place(origin(k), dy), 5 + k)
            diag_x(it, k).start()

    def a4(it, ks=(1, 2, 3)):
        for k in ks:
            arrived(it, it.place(origin(k), dd, 0), 8 + k)
            arrived(it, it.place(origin(k), dd, 1), 11 + k)
            to_core(it, k).start()

    def a5(it):
        (keep_out() if it is wo else keep(it)).wait()
        for k in (1, 2, 3):
            arrived(it, it.place(lax.rem(z + 4 - k, 4) * 2 + 1 - core), 14 + k)
        arrived(it, it.place(sib), 18)

    def sent(it):
        for k in (1, 2, 3):
            for make in (along_z, to_x, to_y, diag_y, diag_x, to_core):
                make(it, k).wait_send()

    @pl.when(i == 0)
    def _():
        barrier = pltpu.get_barrier_semaphore()
        peers = [(dx, f), (dy, f)] + [(d, lax.rem(f + j, 8)) for j in range(1, 8)]
        for peer in peers:
            pl.semaphore_signal(barrier, inc=1, device_id=peer, device_id_type=MESH)
        pl.semaphore_wait(barrier, len(peers))
        for j in range(1, 8):
            gain_copy(j).start()
        g_own = pltpu.make_async_copy(gs_ref, gains.at[f], local_sem.at[8])
        g_own.start()
        for it in items:
            for k in (1, 2, 3):
                along_z(it, k).start()
            own_copy(it).start()
            keep(it).start()
        keep(wo).wait()
        keep_out().start()
        for j in range(1, 8):
            gain_copy(j).wait_recv()
        g_own.wait()
        total = jnp.sum(gains[...], axis=0)
        for t in range(gvec.shape[1] // LANES):
            gvec[:, t * LANES:(t + 1) * LANES] = total[t:t + 1, :]
        a2(dkv)
        a2(dq, (1,))
        a3(dkv)
        a2(dq, (2, 3))
        a4(dkv)
        a3(dq)
        a2(ukva)
        a4(dq)
        a3(ukva)
        a5(dkv)
        a5(dq)

    plan = {
        1: lambda: (a2(uqa), a4(ukva)),
        2: lambda: (a2(ukvb), a3(uqa)),
        3: lambda: (a4(uqa), a3(ukvb)),
        5: lambda: (a4(ukvb), a2(uqb)),
        7: lambda: a3(uqb),
        8: lambda: (a5(ukva), a5(uqa), a4(uqb)),
        10: lambda: a2(wo, (1,)),
        12: lambda: a3(wo, (1,)),
        13: lambda: a2(wo, (2,)),
        14: lambda: a4(wo, (1,)),
        15: lambda: a3(wo, (2,)),
        16: lambda: (a5(ukvb), a5(uqb), a2(wo, (3,))),
        17: lambda: (a4(wo, (2,)), a3(wo, (3,))),
        19: lambda: a4(wo, (3,)),
    }
    for step, act in plan.items():
        @pl.when(i == step)
        def _(act=act):
            act()

    d_model, q_rank, kv_rank = x_ref.shape[-1], cq_all.shape[-1], c_all.shape[-1]

    @pl.when(i < n_prompts)
    def _():
        x = x_ref[0].astype(jnp.float32)
        a = (x * inv_rms(x) * gvec[:, :d_model]).astype(jnp.bfloat16)
        qd = jnp.dot(a, wdq[...], preferred_element_type=jnp.float32)
        cq_all[i] = (qd * inv_rms(qd) * gvec[:, d_model:d_model + q_rank]).astype(jnp.bfloat16)
        kd = jnp.dot(a, wdkv[...], preferred_element_type=jnp.float32)
        lat = kd[:, :kv_rank]
        lat = (lat * inv_rms(lat) * gvec[:, d_model + q_rank:]).astype(jnp.bfloat16)
        c_all[i] = lat
        c_ref[0] = lat
        rt = rotate(kd[:, kv_rank:], cos_ref[...], sin_ref[...]).astype(jnp.bfloat16)
        rt_all[i] = rt
        r_ref[0] = jnp.concatenate([rt[:, :HALF], rt[:, LANES // 2:LANES // 2 + HALF]], axis=1)

    q_cols, kv_cols, o_cols = GROUP * (NOPE + ROPE), GROUP * (NOPE + VDIM), GROUP * VDIM
    scale = (NOPE + ROPE) ** -0.5 * LOG2E

    def attend(p, wuq, wukv, o_ref):
        cq = cq_all[p]
        lat = c_all[p]
        slots = slot_masks(rt_all[p])

        def body(g, carry):
            wq = wuq[:, pl.ds(pl.multiple_of(g * q_cols, q_cols), q_cols)]
            wkv = wukv[:, pl.ds(pl.multiple_of(g * kv_cols, kv_cols), kv_cols)]
            q = jnp.dot(cq, wq, preferred_element_type=jnp.float32)
            kv = jnp.dot(lat, wkv, preferred_element_type=jnp.float32)
            o = attend_heads(q, kv, slots, cos_ref[...], sin_ref[...], scale)
            o_ref[0, :, pl.ds(pl.multiple_of(g * o_cols, o_cols), o_cols)] = o
            return carry

        lax.fori_loop(0, wuq.shape[1] // q_cols, body, 0)

    @pl.when(jnp.logical_and(i >= n_prompts, i < 2 * n_prompts))
    def _():
        attend(i - n_prompts, wuqa, wukva, oa_ref)

    @pl.when(i >= 2 * n_prompts)
    def _():
        attend(i - 2 * n_prompts, wuqb, wukvb, ob_ref)

    @pl.when(i == 3 * n_prompts - 1)
    def _():
        a5(wo)
        for j in range(1, 8):
            gain_copy(j).wait_send()
        for it in items:
            sent(it)
            own_copy(it).wait_send()


def slot_masks(rt):
    lane = lax.broadcasted_iota(jnp.int32, (1, LANES), 1)
    slot = lax.rem(lane, LANES // 2) // HALF
    return [jnp.where(slot == j, rt, 0) for j in range(PE_TILE)]


def out_kernel(x_ref, oa_ref, ob_ref, w_ref, c_in, r_in, y_ref, c_out, r_out):
    step = 512
    oa, ob = oa_ref[...], ob_ref[...]
    n_a = oa.shape[1]
    c_out[...] = c_in[...]
    r_out[...] = r_in[...]
    for n in range(0, y_ref.shape[1], step):
        acc = jnp.dot(oa, w_ref[:n_a, n:n + step], preferred_element_type=jnp.float32)
        acc += jnp.dot(ob, w_ref[n_a:, n:n + step], preferred_element_type=jnp.float32)
        y_ref[:, n:n + step] = (x_ref[:, n:n + step].astype(jnp.float32) + acc).astype(jnp.bfloat16)


def whole(shape):
    return pl.BlockSpec(shape, lambda i: (0,) * len(shape))


def solution(mesh):
    n_fsdp = mesh.shape['fsdp']

    def local_block(x, g1, wdq, gq, wuq, wdkv, gkv, wukv, wout):
        n_p, seq_len, d_model = x.shape
        kv_rank, q_rank = gkv.shape[0] * n_fsdp, wdq.shape[1]
        cos_np, sin_np = rope_tiles(seq_len)
        cos, sin = jnp.asarray(cos_np), jnp.asarray(sin_np)
        me = lax.axis_index('fsdp')
        spread = [
            lax.dynamic_update_slice(jnp.zeros(g.shape[0] * n_fsdp, jnp.float32), g.astype(jnp.float32), (me * g.shape[0],))
            for g in (g1, gq, gkv)
        ]
        n_gain = d_model + q_rank + kv_rank
        gs = jnp.concatenate(spread + [jnp.zeros(GAIN_ROWS * LANES - n_gain, jnp.float32)]).reshape(GAIN_ROWS, LANES)
        shards = [wdq, arrange_dkv(wdkv, kv_rank), arrange_q(wuq), arrange_kv(wukv), wout]
        full = lambda w, cols: pltpu.VMEM((w.shape[0] * n_fsdp, cols), jnp.bfloat16)
        q_cols, kv_cols, o_cols = GROUP * (NOPE + ROPE), GROUP * (NOPE + VDIM), GROUP * VDIM
        n_groups = wuq.shape[1] // q_cols
        first, rest = GROUPS_FIRST, n_groups - GROUPS_FIRST
        last = n_p - 1
        blk = lambda cols, lag: pl.BlockSpec((1, seq_len, cols), lambda i: (jnp.clip(i - lag * n_p, 0, last), 0, 0))
        out = lambda cols: jax.ShapeDtypeStruct((n_p, seq_len, cols), jnp.bfloat16)
        hbm = pl.BlockSpec(memory_space=pl.ANY)
        c, r, oa, ob, wout_all = pl.pallas_call(
            functools.partial(core_kernel, n_p),
            grid=(3 * n_p,),
            in_specs=[blk(d_model, 0)] + [hbm] * 6 + [whole(cos.shape)] * 2,
            out_specs=[blk(kv_rank, 0), blk(ROPE, 0), blk(first * o_cols, 1), blk(rest * o_cols, 2), hbm],
            out_shape=[
                out(kv_rank), out(ROPE), out(first * o_cols), out(rest * o_cols),
                jax.ShapeDtypeStruct((wout.shape[0] * n_fsdp, wout.shape[1]), jnp.bfloat16),
            ],
            scratch_shapes=[
                full(wdq, q_rank), full(wdkv, kv_rank + LANES),
                full(wuq, first * q_cols), full(wuq, rest * q_cols),
                full(wukv, first * kv_cols), full(wukv, rest * kv_cols),
                pltpu.VMEM((n_fsdp, GAIN_ROWS, LANES), jnp.float32),
                pltpu.VMEM((1, n_gain), jnp.float32),
                pltpu.VMEM((n_p, seq_len, q_rank), jnp.bfloat16),
                pltpu.VMEM((n_p, seq_len, kv_rank), jnp.bfloat16),
                pltpu.VMEM((n_p, seq_len, LANES), jnp.bfloat16),
                pltpu.VMEM(wout.shape, jnp.bfloat16),
                pltpu.SemaphoreType.DMA((7, N_SEND)),
                pltpu.SemaphoreType.DMA((7, N_RECV)),
                pltpu.SemaphoreType.DMA((7,)),
                pltpu.SemaphoreType.DMA((7,)),
                pltpu.SemaphoreType.DMA((9,)),
            ],
            compiler_params=pltpu.CompilerParams(
                vmem_limit_bytes=VMEM_LIMIT, dimension_semantics=("arbitrary",), collective_id=0, has_side_effects=True,
            ),
            name="core",
        )(x, gs, *shards, cos, sin)
        rows = 512
        tile = lambda cols: pl.BlockSpec((rows, cols), lambda i: (i, 0))
        flat = lambda v: v.reshape(n_p * seq_len, v.shape[-1])
        flat_out = lambda cols: jax.ShapeDtypeStruct((n_p * seq_len, cols), jnp.bfloat16)
        y, c, r = pl.pallas_call(
            out_kernel,
            grid=(n_p * seq_len // rows,),
            in_specs=[tile(d_model), tile(oa.shape[-1]), tile(ob.shape[-1]), whole(wout_all.shape), tile(kv_rank), tile(ROPE)],
            out_specs=[tile(d_model), tile(kv_rank), tile(ROPE)],
            out_shape=[flat_out(d_model), flat_out(kv_rank), flat_out(ROPE)],
            compiler_params=pltpu.CompilerParams(vmem_limit_bytes=VMEM_LIMIT, dimension_semantics=("arbitrary",)),
            name="project",
        )(flat(x), flat(oa), flat(ob), wout_all, flat(c), flat(r))
        back = lambda v: v.reshape(n_p, seq_len, v.shape[-1])
        return back(y), back(c), back(r)

    batch, row, mat = P(('dp', 'fsdp')), P('fsdp'), P('fsdp', None)
    return jax.shard_map(
        local_block,
        mesh=mesh,
        in_specs=(batch, row, mat, row, mat, mat, row, mat, mat),
        out_specs=(batch, batch, batch),
        check_vma=False,
    )
```

time: 405 us -> 234 us (0.58)
  waiting for transfers between devices: 215 us -> 0 us
  Pallas kernels: 138 us -> 217 us
  blocking collectives: 18.8 us -> 0 us
  between operations: 15.9 us -> 0.74 us
  local copies, waits for them, and re-layouts: 15.6 us -> 10.5 us
    all_gather x5 -> x0, waiting for transfers between devices: 215 us -> none  [gather(): return lax.all_gather(part, ('fsdp', 'dp'), tiled=True)]
    pallas_call x3 -> x2, Pallas kernels: 138 us -> 217 us  [the longest x1 180 us: local_block(): pl.pallas_call(functools.partial(core_kernel, n_p), grid=(3 * n_p,), in_s...]
    unnamed x1 -> x0, blocking collectives: 18.8 us -> none
    dynamic_slice x5 -> x0, local copies, waits for them, and re-layouts: 4.09 us -> none  [gather(): part = lax.dynamic_slice_in_dim(w, lax.axis_index('dp') * rows, rows, 0)]
  transfers between devices with their start and end apart: 5 -> 0, of which waited for: 5 -> 0; matrix products, arithmetic and copies ran while one was open for 3% -> 0% of each run, Pallas kernels for 25% -> 0%
where the time goes in v2:
time: 234 us; the launch traced here: 231 us
  Pallas kernels  217 us (93%)
  local copies, waits for them, and re-layouts  10.5 us (4%)
  other arithmetic  3.13 us (1%)
    pallas_call x1, Pallas kernels, local_block(): pl.pallas_call(functools.partial(core_kernel, n_p), grid=(3 * n_p,), in_s...  180 us
    pallas_call x1, Pallas kernels, local_block(): pl.pallas_call(out_kernel, grid=(n_p * seq_len // rows,), in_specs=[tile(...  37 us

profile of v2, /device:TPU:0, one launch (start us, length us, event | category | flops | bytes accessed | tf_op | source)
XLA Modules:
  0.0 231.1 jit_solution(5723684543304608771)
XLA Ops:
  0.6 0.0 copy-start
  0.7 0.8 convert_dynamic-update-slice_fusion.1
  1.5 0.7 convert_dynamic-update-slice_fusion.2
  2.2 0.8 convert_dynamic-update-slice_fusion
  3.0 0.6 maximum_bitcast_fusion.gs_ref
  3.6 0.7 slice.21
  4.3 0.7 fusion
  5.1 0.1 copy.37
  5.2 0.1 copy.28
  5.3 0.1 copy.26
  5.5 1.0 slice.19
  6.4 0.2 copy.36
  6.6 1.0 concatenate.10.dkv_s
  7.6 1.4 reshape.61
  9.0 0.1 copy.39
  9.1 1.2 reshape.62.ukv_s
  10.3 0.0 copy-done
  10.3 0.6 copy.31
  10.9 0.1 slice.25
  11.1 0.2 pad_maximum_fusion
  11.3 1.2 copy.34.uq_s
  12.5 179.8 %core.1 = (bf16[8,256,256]{2,1,0:T(8,128)(2,1)}, bf16[8,256,32]{2,1,0:T(8,128)(2,1)}, bf16[8,256,1024]{2,1,0:T(8,128)(2,1)}, bf16[8,256,1536]{2,1,0:T(8,128)(2,1)}, bf16[2560,2560]{1,0:T(8,128)(2,1)}) custom-call(bf16[8,256,2560]{2,1,0:T(8,128)(2,1)} %x_ref.1, f32[32,128]{1,0:T(8,128)} %maximum_bitcast_fusion.gs_ref, bf16[320,768]{1,0:T(8,128)(2,1)} %dq_s.1, ...), custom_call_target="tpu_custom_call" | custom-call | tf_op jit(solution)/shard_map/core/pallas_call | solution.py:427
  192.3 37.0 %project.1 = (bf16[2048,2560]{1,0:T(8,128)(2,1)}, bf16[2048,256]{1,0:T(8,128)(2,1)}, bf16[2048,32]{1,0:T(8,128)(2,1)}) custom-call(bf16[2048,2560]{1,0:T(8,128)(2,1)} %bitcast.22, bf16[2048,1024]{1,0:T(8,128)(2,1)} %bitcast.24, bf16[2048,1536]{1,0:T(8,128)(2,1)} %bitcast.23, bf16[2560,2560]{1,0:T(8,128)(2,1)} %get-tuple-element.13.w_ref, ...), custom_call_target="tpu_custom_call" | custom-call | tf_op jit(solution)/shard_map/project/pallas_call | solution.py:461
  229.2 1.9 copy.35
  (6 shorter events, 0.1 us)
Async XLA Ops:
  0.6 9.6 %copy-start = (bf16[96,3840]{1,0:T(8,128)(2,1)S(1)}, bf16[96,3840]{1,0:T(8,128)(2,1)}, u32[]{:S(2)}) copy-start(bf16[96,3840]{1,0:T(8,128)(2,1)} %param.15) | copy-start | bytes 2211844

commit v3 on v2

--- a/solution.py
+++ b/solution.py
@@ -162,8 +162,8 @@
 
 def core_kernel(
     n_prompts, x_ref, gs_ref, dq_s, dkv_s, uq_s, ukv_s, out_s, cos_ref, sin_ref,
-    c_ref, r_ref, oa_ref, ob_ref, wout_ref,
-    wdq, wdkv, wuqa, wuqb, wukva, wukvb, gains, gvec, cq_all, c_all, rt_all, stage,
+    c_all, r_ref, oa_ref, ob_ref, wout_ref,
+    wdq, wdkv, wuqa, wuqb, wukva, wukvb, gains, gvec, a_all, acc, cq_all, rt_all, stage,
     send_sem, recv_sem, g_send, g_recv, local_sem,
 ):
     i = pl.program_id(0)
@@ -183,6 +183,7 @@
     uqb = Item(5, uq_s, n_a, wuqb.shape[1], wuqb)
     wo = Item(6, out_s, 0, wout_ref.shape[1], wout_ref)
     items = [dkv, dq, ukva, uqa, ukvb, uqb, wo]
+    down, first, rest, last = (dkv, dq), (ukva, uqa), (ukvb, uqb), (wo,)
 
     def to(k):
         return lax.rem(z + k, 4) * 2 + core
@@ -237,30 +238,37 @@
             device_id=(d, lax.rem(f + j, 8)), device_id_type=MESH,
         )
 
-    def a2(it, ks=(1, 2, 3)):
+    def a2(its, *ks):
         for k in ks:
-            arrived(it, it.place(origin(k), d), k - 1)
-            to_x(it, k).start()
-            to_y(it, k).start()
-
-    def a3(it, ks=(1, 2, 3)):
+            for it in its:
+                arrived(it, it.place(origin(k), d), k - 1)
+                to_x(it, k).start()
+                to_y(it, k).start()
+
+    def a3(its, *ks):
         for k in ks:
-            arrived(it, it.place(origin(k), dx), 2 + k)
-            diag_y(it, k).start()
-            arrived(it, it.place(origin(k), dy), 5 + k)
-            diag_x(it, k).start()
-
-    def a4(it, ks=(1, 2, 3)):
+            for it in its:
+                arrived(it, it.place(origin(k), dx), 2 + k)
+                diag_y(it, k).start()
+                arrived(it, it.place(origin(k), dy), 5 + k)
+                diag_x(it, k).start()
+
+    def a4(its, *ks):
         for k in ks:
-            arrived(it, it.place(origin(k), dd, 0), 8 + k)
-            arrived(it, it.place(origin(k), dd, 1), 11 + k)
-            to_core(it, k).start()
-
-    def a5(it):
-        (keep_out() if it is wo else keep(it)).wait()
-        for k in (1, 2, 3):
-            arrived(it, it.place(lax.rem(z + 4 - k, 4) * 2 + 1 - core), 14 + k)
-        arrived(it, it.place(sib), 18)
+            for it in its:
+                arrived(it, it.place(origin(k), dd, 0), 8 + k)
+                arrived(it, it.place(origin(k), dd, 1), 11 + k)
+                to_core(it, k).start()
+
+    def a5(its, *ks):
+        for k in ks:
+            for it in its:
+                arrived(it, it.place(lax.rem(z + 4 - k, 4) * 2 + 1 - core), 14 + k)
+
+    def a5_own(its):
+        for it in its:
+            (keep_out() if it is wo else keep(it)).wait()
+            arrived(it, it.place(sib), 18)
 
     def sent(it):
         for k in (1, 2, 3):
@@ -278,68 +286,113 @@
             gain_copy(j).start()
         g_own = pltpu.make_async_copy(gs_ref, gains.at[f], local_sem.at[8])
         g_own.start()
-        for it in items:
-            for k in (1, 2, 3):
-                along_z(it, k).start()
+        for it in down:
             own_copy(it).start()
             keep(it).start()
-        keep(wo).wait()
-        keep_out().start()
+        for group in (down, first, rest, last):
+            for k in (1, 2, 3):
+                for it in group:
+                    along_z(it, k).start()
+        for it in items[2:]:
+            own_copy(it).start()
+            keep(it).start()
         for j in range(1, 8):
             gain_copy(j).wait_recv()
         g_own.wait()
         total = jnp.sum(gains[...], axis=0)
         for t in range(gvec.shape[1] // LANES):
             gvec[:, t * LANES:(t + 1) * LANES] = total[t:t + 1, :]
-        a2(dkv)
-        a2(dq, (1,))
-        a3(dkv)
-        a2(dq, (2, 3))
-        a4(dkv)
-        a3(dq)
-        a2(ukva)
-        a4(dq)
-        a3(ukva)
-        a5(dkv)
-        a5(dq)
+        a5_own(down)
+
+    d_model, q_rank, kv_rank = x_ref.shape[-1], cq_all.shape[-1], c_all.shape[-1]
+    k_rows = d_model // 4
+    s2 = n_prompts
+    s3 = s2 + 4
+    s4 = s3 + n_prompts
+    end = s4 + n_prompts - 1
 
     plan = {
-        1: lambda: (a2(uqa), a4(ukva)),
-        2: lambda: (a2(ukvb), a3(uqa)),
-        3: lambda: (a4(uqa), a3(ukvb)),
-        5: lambda: (a4(ukvb), a2(uqb)),
-        7: lambda: a3(uqb),
-        8: lambda: (a5(ukva), a5(uqa), a4(uqb)),
-        10: lambda: a2(wo, (1,)),
-        12: lambda: a3(wo, (1,)),
-        13: lambda: a2(wo, (2,)),
-        14: lambda: a4(wo, (1,)),
-        15: lambda: a3(wo, (2,)),
-        16: lambda: (a5(ukvb), a5(uqb), a2(wo, (3,))),
-        17: lambda: (a4(wo, (2,)), a3(wo, (3,))),
-        19: lambda: a4(wo, (3,)),
+        3: lambda: a2(down, 1),
+        5: lambda: a3(down, 1),
+        7: lambda: (a2(down, 2), a4(down, 1)),
+        s2: lambda: (a3(down, 2), a5(down, 1)),
+        s2 + 1: lambda: (a2(down, 3), a4(down, 2), a5(down, 2)),
+        s2 + 2: lambda: (a3(down, 3), a2(first, 1), a4(down, 3), a2(first, 2), a5(down, 3)),
+        s2 + 3: lambda: (a2(first, 3), a3(first, 1)),
+        s3: lambda: (
+            a3(first, 2), a2(rest, 1), a3(first, 3), a4(first, 1), a2(rest, 2), a4(first, 2, 3), a5_own(first), a5(first, 1, 2, 3)
+        ),
+        s3 + 1: lambda: (a2(rest, 3), a3(rest, 1)),
+        s3 + 2: lambda: (a3(rest, 2), a2(last, 1)),
+        s3 + 3: lambda: (a3(rest, 3), a4(rest, 1)),
+        s3 + 4: lambda: a4(rest, 2),
+        s3 + 5: lambda: (a4(rest, 3), a2(last, 2), a3(last, 1)),
+        s4: lambda: (a5_own(rest), a5(rest, 1, 2, 3), a2(last, 3), a3(last, 2)),
+        s4 + 1: lambda: a4(last, 1),
+        s4 + 2: lambda: (a3(last, 3), a4(last, 2)),
+        s4 + 4: lambda: a4(last, 3),
     }
     for step, act in plan.items():
         @pl.when(i == step)
         def _(act=act):
             act()
 
-    d_model, q_rank, kv_rank = x_ref.shape[-1], cq_all.shape[-1], c_all.shape[-1]
+    @pl.when(i == 1)
+    def _():
+        keep(wo).wait()
+        keep_out().start()
+
+    def partial_sums(p, k):
+        row = lax.rem(z + 4 - k, 4) * k_rows
+        rows = pl.ds(pl.multiple_of(row, LANES), k_rows)
+        a = a_all[p, :, rows]
+        qd = jnp.dot(a, wdq[rows], preferred_element_type=jnp.float32)
+        kd = jnp.dot(a, wdkv[rows], preferred_element_type=jnp.float32)
+        if k > 0:
+            qd += acc[p, :, :q_rank]
+            kd += acc[p, :, q_rank:]
+        return qd, kd
+
+    def add_plane(p, k):
+        qd, kd = partial_sums(p, k)
+        acc[p, :, :q_rank] = qd
+        acc[p, :, q_rank:] = kd
+
+    def finish(p):
+        qd, kd = partial_sums(p, 3)
+        cq_all[p] = (qd * inv_rms(qd) * gvec[:, d_model:d_model + q_rank]).astype(jnp.bfloat16)
+        lat = kd[:, :kv_rank]
+        c_all[p] = (lat * inv_rms(lat) * gvec[:, d_model + q_rank:]).astype(jnp.bfloat16)
+        rt = rotate(kd[:, kv_rank:], cos_ref[...], sin_ref[...]).astype(jnp.bfloat16)
+        rt_all[p] = rt
+        r_ref[p] = jnp.concatenate([rt[:, :HALF], rt[:, LANES // 2:LANES // 2 + HALF]], axis=1)
+
+    def each(first_p, n, fn):
+        def body(p, carry):
+            fn(p)
+            return carry
+        lax.fori_loop(first_p, first_p + n, body, 0)
 
     @pl.when(i < n_prompts)
     def _():
         x = x_ref[0].astype(jnp.float32)
-        a = (x * inv_rms(x) * gvec[:, :d_model]).astype(jnp.bfloat16)
-        qd = jnp.dot(a, wdq[...], preferred_element_type=jnp.float32)
-        cq_all[i] = (qd * inv_rms(qd) * gvec[:, d_model:d_model + q_rank]).astype(jnp.bfloat16)
-        kd = jnp.dot(a, wdkv[...], preferred_element_type=jnp.float32)
-        lat = kd[:, :kv_rank]
-        lat = (lat * inv_rms(lat) * gvec[:, d_model + q_rank:]).astype(jnp.bfloat16)
-        c_all[i] = lat
-        c_ref[0] = lat
-        rt = rotate(kd[:, kv_rank:], cos_ref[...], sin_ref[...]).astype(jnp.bfloat16)
-        rt_all[i] = rt
-        r_ref[0] = jnp.concatenate([rt[:, :HALF], rt[:, LANES // 2:LANES // 2 + HALF]], axis=1)
+        a_all[i] = (x * inv_rms(x) * gvec[:, :d_model]).astype(jnp.bfloat16)
+        add_plane(i, 0)
+
+    @pl.when(jnp.logical_and(i >= s2, i < s2 + 2))
+    def _():
+        @pl.when(i == s2)
+        def _():
+            each(0, n_prompts, lambda p: add_plane(p, 1))
+
+        @pl.when(i == s2 + 1)
+        def _():
+            each(0, n_prompts, lambda p: add_plane(p, 2))
+
+    @pl.when(jnp.logical_and(i >= s2 + 2, i < s3))
+    def _():
+        half = n_prompts // 2
+        each((i - s2 - 2) * half, half, finish)
 
     q_cols, kv_cols, o_cols = GROUP * (NOPE + ROPE), GROUP * (NOPE + VDIM), GROUP * VDIM
     scale = (NOPE + ROPE) ** -0.5 * LOG2E
@@ -360,17 +413,18 @@
 
         lax.fori_loop(0, wuq.shape[1] // q_cols, body, 0)
 
-    @pl.when(jnp.logical_and(i >= n_prompts, i < 2 * n_prompts))
-    def _():
-        attend(i - n_prompts, wuqa, wukva, oa_ref)
-
-    @pl.when(i >= 2 * n_prompts)
-    def _():
-        attend(i - 2 * n_prompts, wuqb, wukvb, ob_ref)
-
-    @pl.when(i == 3 * n_prompts - 1)
-    def _():
-        a5(wo)
+    @pl.when(jnp.logical_and(i >= s3, i < s4))
+    def _():
+        attend(i - s3, wuqa, wukva, oa_ref)
+
+    @pl.when(i >= s4)
+    def _():
+        attend(i - s4, wuqb, wukvb, ob_ref)
+
+    @pl.when(i == end)
+    def _():
+        a5_own(last)
+        a5(last, 1, 2, 3)
         for j in range(1, 8):
             gain_copy(j).wait_send()
         for it in items:
@@ -421,14 +475,17 @@
         n_groups = wuq.shape[1] // q_cols
         first, rest = GROUPS_FIRST, n_groups - GROUPS_FIRST
         last = n_p - 1
-        blk = lambda cols, lag: pl.BlockSpec((1, seq_len, cols), lambda i: (jnp.clip(i - lag * n_p, 0, last), 0, 0))
+        blk = lambda cols, lag: pl.BlockSpec((1, seq_len, cols), lambda i: (jnp.clip(i - lag, 0, last), 0, 0))
         out = lambda cols: jax.ShapeDtypeStruct((n_p, seq_len, cols), jnp.bfloat16)
         hbm = pl.BlockSpec(memory_space=pl.ANY)
         c, r, oa, ob, wout_all = pl.pallas_call(
             functools.partial(core_kernel, n_p),
-            grid=(3 * n_p,),
+            grid=(3 * n_p + 4,),
             in_specs=[blk(d_model, 0)] + [hbm] * 6 + [whole(cos.shape)] * 2,
-            out_specs=[blk(kv_rank, 0), blk(ROPE, 0), blk(first * o_cols, 1), blk(rest * o_cols, 2), hbm],
+            out_specs=[
+                whole((n_p, seq_len, kv_rank)), whole((n_p, seq_len, ROPE)),
+                blk(first * o_cols, n_p + 4), blk(rest * o_cols, 2 * n_p + 4), hbm,
+            ],
             out_shape=[
                 out(kv_rank), out(ROPE), out(first * o_cols), out(rest * o_cols),
                 jax.ShapeDtypeStruct((wout.shape[0] * n_fsdp, wout.shape[1]), jnp.bfloat16),
@@ -439,8 +496,9 @@
                 full(wukv, first * kv_cols), full(wukv, rest * kv_cols),
                 pltpu.VMEM((n_fsdp, GAIN_ROWS, LANES), jnp.float32),
                 pltpu.VMEM((1, n_gain), jnp.float32),
+                pltpu.VMEM((n_p, seq_len, d_model), jnp.bfloat16),
+                pltpu.VMEM((n_p, seq_len, q_rank + kv_rank + LANES), jnp.float32),
                 pltpu.VMEM((n_p, seq_len, q_rank), jnp.bfloat16),
-                pltpu.VMEM((n_p, seq_len, kv_rank), jnp.bfloat16),
                 pltpu.VMEM((n_p, seq_len, LANES), jnp.bfloat16),
                 pltpu.VMEM(wout.shape, jnp.bfloat16),
                 pltpu.SemaphoreType.DMA((7, N_SEND)),

time: 234 us -> 220 us (0.940); the launches traced: 231 us -> 220 us
  Pallas kernels: 217 us -> 206 us
    pallas_call x1, Pallas kernels: 180 us -> 168 us  [local_block(): pl.pallas_call(functools.partial(core_kernel, n_p), grid=(3 * n_p + 4,),...]
where the time goes in v3:
time: 220 us
  Pallas kernels  206 us (94%)
  local copies, waits for them, and re-layouts  10.5 us (5%)
  other arithmetic  3.13 us (1%)
    pallas_call x1, Pallas kernels, local_block(): pl.pallas_call(functools.partial(core_kernel, n_p), grid=(3 * n_p + 4,),...  168 us
    pallas_call x1, Pallas kernels, local_block(): pl.pallas_call(out_kernel, grid=(n_p * seq_len // rows,), in_specs=[tile(...  37.1 us

profile of v3, /device:TPU:0, one launch (start us, length us, event | category | flops | bytes accessed | tf_op | source)
XLA Modules:
  0.0 219.9 jit_solution(10384378783690820970)
XLA Ops:
  0.6 0.0 copy-start
  0.7 0.8 convert_dynamic-update-slice_fusion.1
  1.5 0.7 convert_dynamic-update-slice_fusion.2
  2.2 0.8 convert_dynamic-update-slice_fusion
  3.0 0.6 maximum_bitcast_fusion.gs_ref
  3.6 0.7 slice.21
  4.3 0.7 fusion
  5.1 0.1 copy.37
  5.2 0.1 copy.28
  5.3 0.1 copy.26
  5.5 1.0 slice.19
  6.4 0.2 copy.36
  6.6 1.0 concatenate.10.dkv_s
  7.6 1.4 reshape.61
  9.0 0.1 copy.39
  9.1 1.2 reshape.62.ukv_s
  10.3 0.0 copy-done
  10.3 0.6 copy.31
  10.9 0.1 slice.25
  11.1 0.2 pad_maximum_fusion
  11.3 1.2 copy.34.uq_s
  12.5 168.4 %core.1 = (bf16[8,256,256]{2,1,0:T(8,128)(2,1)}, bf16[8,256,32]{2,1,0:T(8,128)(2,1)}, bf16[8,256,1024]{2,1,0:T(8,128)(2,1)}, bf16[8,256,1536]{2,1,0:T(8,128)(2,1)}, bf16[2560,2560]{1,0:T(8,128)(2,1)}) custom-call(bf16[8,256,2560]{2,1,0:T(8,128)(2,1)} %x_ref.1, f32[32,128]{1,0:T(8,128)} %maximum_bitcast_fusion.gs_ref, bf16[320,768]{1,0:T(8,128)(2,1)} %dq_s.1, ...), custom_call_target="tpu_custom_call" | custom-call | tf_op jit(solution)/shard_map/core/pallas_call | solution.py:481
  180.9 37.1 %project.1 = (bf16[2048,2560]{1,0:T(8,128)(2,1)}, bf16[2048,256]{1,0:T(8,128)(2,1)}, bf16[2048,32]{1,0:T(8,128)(2,1)}) custom-call(bf16[2048,2560]{1,0:T(8,128)(2,1)} %bitcast.22, bf16[2048,1024]{1,0:T(8,128)(2,1)} %bitcast.24, bf16[2048,1536]{1,0:T(8,128)(2,1)} %bitcast.23, bf16[2560,2560]{1,0:T(8,128)(2,1)} %get-tuple-element.13.w_ref, ...), custom_call_target="tpu_custom_call" | custom-call | tf_op jit(solution)/shard_map/project/pallas_call | solution.py:519
  218.0 1.9 copy.35
  (6 shorter events, 0.1 us)
Async XLA Ops:
  0.6 9.6 %copy-start = (bf16[96,3840]{1,0:T(8,128)(2,1)S(1)}, bf16[96,3840]{1,0:T(8,128)(2,1)}, u32[]{:S(2)}) copy-start(bf16[96,3840]{1,0:T(8,128)(2,1)} %param.15) | copy-start | bytes 2211844

commit v4 on v3

--- a/solution.py
+++ b/solution.py
@@ -238,6 +238,11 @@
             device_id=(d, lax.rem(f + j, 8)), device_id_type=MESH,
         )
 
+    def send_z(its, *ks):
+        for k in ks:
+            for it in its:
+                along_z(it, k).start()
+
     def a2(its, *ks):
         for k in ks:
             for it in its:
@@ -289,10 +294,7 @@
         for it in down:
             own_copy(it).start()
             keep(it).start()
-        for group in (down, first, rest, last):
-            for k in (1, 2, 3):
-                for it in group:
-                    along_z(it, k).start()
+        send_z(down, 1, 2, 3)
         for it in items[2:]:
             own_copy(it).start()
             keep(it).start()
@@ -312,18 +314,18 @@
     end = s4 + n_prompts - 1
 
     plan = {
-        3: lambda: a2(down, 1),
+        3: lambda: (a2(down, 1), send_z(first, 1)),
         5: lambda: a3(down, 1),
-        7: lambda: (a2(down, 2), a4(down, 1)),
+        7: lambda: (a2(down, 2), send_z(first, 2, 3), a4(down, 1)),
         s2: lambda: (a3(down, 2), a5(down, 1)),
-        s2 + 1: lambda: (a2(down, 3), a4(down, 2), a5(down, 2)),
-        s2 + 2: lambda: (a3(down, 3), a2(first, 1), a4(down, 3), a2(first, 2), a5(down, 3)),
-        s2 + 3: lambda: (a2(first, 3), a3(first, 1)),
+        s2 + 1: lambda: (a2(down, 3), send_z(rest, 1), a4(down, 2), a5(down, 2)),
+        s2 + 2: lambda: (a3(down, 3), a2(first, 1), send_z(rest, 2), a4(down, 3), a2(first, 2), send_z(rest, 3), a5(down, 3)),
+        s2 + 3: lambda: (a2(first, 3), send_z(last, 1), a3(first, 1)),
         s3: lambda: (
             a3(first, 2), a2(rest, 1), a3(first, 3), a4(first, 1), a2(rest, 2), a4(first, 2, 3), a5_own(first), a5(first, 1, 2, 3)
         ),
-        s3 + 1: lambda: (a2(rest, 3), a3(rest, 1)),
-        s3 + 2: lambda: (a3(rest, 2), a2(last, 1)),
+        s3 + 1: lambda: (a2(rest, 3), send_z(last, 2), a3(rest, 1)),
+        s3 + 2: lambda: (a3(rest, 2), a2(last, 1), send_z(last, 3)),
         s3 + 3: lambda: (a3(rest, 3), a4(rest, 1)),
         s3 + 4: lambda: a4(rest, 2),
         s3 + 5: lambda: (a4(rest, 3), a2(last, 2), a3(last, 1)),

time: 220 us -> 222 us (level)
  the two profiles are of different devices: /device:TPU:0 before, /device:TPU:26 now
where the time goes in v4:
time: 222 us
  Pallas kernels  208 us (94%)
  local copies, waits for them, and re-layouts  10.5 us (5%)
  other arithmetic  3.13 us (1%)
    pallas_call x1, Pallas kernels, local_block(): pl.pallas_call(functools.partial(core_kernel, n_p), grid=(3 * n_p + 4,),...  170 us
    pallas_call x1, Pallas kernels, local_block(): pl.pallas_call(out_kernel, grid=(n_p * seq_len // rows,), in_specs=[tile(...  37.1 us

profile of v4, /device:TPU:26, one launch (start us, length us, event | category | flops | bytes accessed | tf_op | source)
XLA Modules:
  0.0 221.9 jit_solution(11150746503559383043)
XLA Ops:
  0.6 0.0 copy-start
  0.7 0.8 convert_dynamic-update-slice_fusion.1
  1.5 0.7 convert_dynamic-update-slice_fusion.2
  2.2 0.8 convert_dynamic-update-slice_fusion
  3.0 0.6 maximum_bitcast_fusion.gs_ref
  3.6 0.7 slice.21
  4.3 0.7 fusion
  5.1 0.1 copy.37
  5.2 0.1 copy.28
  5.3 0.1 copy.26
  5.5 1.0 slice.19
  6.4 0.2 copy.36
  6.6 1.0 concatenate.10.dkv_s
  7.6 1.4 reshape.61
  9.0 0.1 copy.39
  9.1 1.2 reshape.62.ukv_s
  10.3 0.0 copy-done
  10.3 0.6 copy.31
  10.9 0.1 slice.25
  11.1 0.2 pad_maximum_fusion
  11.3 1.2 copy.34.uq_s
  12.5 170.4 %core.1 = (bf16[8,256,256]{2,1,0:T(8,128)(2,1)}, bf16[8,256,32]{2,1,0:T(8,128)(2,1)}, bf16[8,256,1024]{2,1,0:T(8,128)(2,1)}, bf16[8,256,1536]{2,1,0:T(8,128)(2,1)}, bf16[2560,2560]{1,0:T(8,128)(2,1)}) custom-call(bf16[8,256,2560]{2,1,0:T(8,128)(2,1)} %x_ref.1, f32[32,128]{1,0:T(8,128)} %maximum_bitcast_fusion.gs_ref, bf16[320,768]{1,0:T(8,128)(2,1)} %dq_s.1, ...), custom_call_target="tpu_custom_call" | custom-call | tf_op jit(solution)/shard_map/core/pallas_call | solution.py:483
  182.9 37.1 %project.1 = (bf16[2048,2560]{1,0:T(8,128)(2,1)}, bf16[2048,256]{1,0:T(8,128)(2,1)}, bf16[2048,32]{1,0:T(8,128)(2,1)}) custom-call(bf16[2048,2560]{1,0:T(8,128)(2,1)} %bitcast.22, bf16[2048,1024]{1,0:T(8,128)(2,1)} %bitcast.24, bf16[2048,1536]{1,0:T(8,128)(2,1)} %bitcast.23, bf16[2560,2560]{1,0:T(8,128)(2,1)} %get-tuple-element.13.w_ref, ...), custom_call_target="tpu_custom_call" | custom-call | tf_op jit(solution)/shard_map/project/pallas_call | solution.py:521
  220.0 1.9 copy.35
  (6 shorter events, 0.1 us)
Async XLA Ops:
  0.6 9.6 %copy-start = (bf16[96,3840]{1,0:T(8,128)(2,1)S(1)}, bf16[96,3840]{1,0:T(8,128)(2,1)}, u32[]{:S(2)}) copy-start(bf16[96,3840]{1,0:T(8,128)(2,1)} %param.15) | copy-start | bytes 2211844

commit v5 on v3

--- a/solution.py
+++ b/solution.py
@@ -112,7 +112,364 @@
 
 
 MESH = pl.DeviceIdType.MESH
-GROUPS_FIRST = 2
+GAIN_ROWS = 32
+N_SEND, N_RECV = 19, 19
+
+
+class Item:
+    def __init__(self, index, shard, col, cols, full):
+        self.index, self.shard, self.col, self.cols, self.full = index, shard, col, cols, full
+        self.rows = shard.shape[0]
+        if (self.rows // 4) % 16 == 0:
+            self.q_rows, self.q_cols = self.rows // 4, cols
+        elif (cols // 4) % LANES == 0 and self.rows == 32:
+            self.q_rows, self.q_cols = self.rows, cols // 4
+        else:
+            self.q_rows, self.q_cols = self.rows // 2, cols // 2
+        if self.q_rows == self.rows:
+            n = self.q_rows // 2
+            self.halves = [(0, n, 0, self.q_cols), (n, n, 0, self.q_cols)]
+        else:
+            n = -(-self.q_cols // (2 * LANES)) * LANES
+            self.halves = [(0, self.q_rows, 0, n), (0, self.q_rows, n, self.q_cols - n)]
+
+    def quarter(self, q):
+        per_row = self.cols // self.q_cols
+        return (q // per_row) * self.q_rows, lax.rem(q, per_row) * self.q_cols
+
+    def source(self, q):
+        r, c = self.quarter(q)
+        return self.shard.at[pl.ds(pl.multiple_of(r, 16), self.q_rows), pl.ds(pl.multiple_of(self.col + c, LANES), self.q_cols)]
+
+    def own(self):
+        return self.shard.at[:, pl.ds(self.col, self.cols)]
+
+    def place(self, f, q=None, half=None):
+        r, c = (0, 0) if q is None else self.quarter(q)
+        r = f * self.rows + r
+        if q is None:
+            n_r, n_c = self.rows, self.cols
+        elif half is None:
+            n_r, n_c = self.q_rows, self.q_cols
+        else:
+            dr, n_r, dc, n_c = self.halves[half]
+            r, c = r + dr, c + dc
+        if n_c == self.cols:
+            return self.full.at[pl.ds(pl.multiple_of(r, 16), n_r)]
+        return self.full.at[pl.ds(pl.multiple_of(r, 16), n_r), pl.ds(pl.multiple_of(c, LANES), n_c)]
+
+
+class Net:
+    def __init__(self, send_sem, recv_sem):
+        self.send_sem, self.recv_sem = send_sem, recv_sem
+        self.d, self.f = lax.axis_index('dp'), lax.axis_index('fsdp')
+        self.z, self.core = self.f // 2, lax.rem(self.f, 2)
+        self.dx = lax.rem(self.d + 2, 4)
+        self.dy = self.d + 1 - 2 * lax.rem(self.d, 2)
+        self.dd = lax.rem(self.dy + 2, 4)
+        self.sib = self.z * 2 + 1 - self.core
+
+    def to(self, k):
+        return lax.rem(self.z + k, 4) * 2 + self.core
+
+    def plane(self, k):
+        return lax.rem(self.z + 4 - k, 4)
+
+    def origin(self, k):
+        return self.plane(k) * 2 + self.core
+
+    def copy(self, it, src, dst, s, r, dev):
+        return pltpu.make_async_remote_copy(
+            src_ref=src, dst_ref=dst, send_sem=self.send_sem.at[it.index, s], recv_sem=self.recv_sem.at[it.index, r],
+            device_id=dev, device_id_type=MESH,
+        )
+
+    def along_z(self, it, k):
+        return self.copy(it, it.source(self.d), it.place(self.f, self.d), k - 1, k - 1, (self.d, self.to(k)))
+
+    def to_x(self, it, k):
+        ref = it.place(self.origin(k), self.d)
+        return self.copy(it, ref, ref, 2 + k, 2 + k, (self.dx, self.f))
+
+    def to_y(self, it, k):
+        ref = it.place(self.origin(k), self.d)
+        return self.copy(it, ref, ref, 5 + k, 5 + k, (self.dy, self.f))
+
+    def diag_y(self, it, k):
+        ref = it.place(self.origin(k), self.dx, 0)
+        return self.copy(it, ref, ref, 8 + k, 8 + k, (self.dy, self.f))
+
+    def diag_x(self, it, k):
+        ref = it.place(self.origin(k), self.dy, 1)
+        return self.copy(it, ref, ref, 11 + k, 11 + k, (self.dx, self.f))
+
+    def to_core(self, it, k):
+        ref = it.place(self.origin(k))
+        return self.copy(it, ref, ref, 14 + k, 14 + k, (self.d, self.sib))
+
+    def own_copy(self, it):
+        return self.copy(it, it.own(), it.place(self.f), 18, 18, (self.d, self.sib))
+
+    def arrived(self, it, ref, r):
+        self.copy(it, ref, ref, 0, r, (self.d, self.f)).wait_recv()
+
+    def barrier(self, peers):
+        sem = pltpu.get_barrier_semaphore()
+        for peer in peers:
+            pl.semaphore_signal(sem, inc=1, device_id=peer, device_id_type=MESH)
+        pl.semaphore_wait(sem, len(peers))
+
+    def send_z(self, its, *ks):
+        for k in ks:
+            for it in its:
+                self.along_z(it, k).start()
+
+    def a2(self, its, *ks):
+        for k in ks:
+            for it in its:
+                self.arrived(it, it.place(self.origin(k), self.d), k - 1)
+                self.to_x(it, k).start()
+                self.to_y(it, k).start()
+
+    def a3(self, its, *ks):
+        for k in ks:
+            for it in its:
+                self.arrived(it, it.place(self.origin(k), self.dx), 2 + k)
+                self.diag_y(it, k).start()
+                self.arrived(it, it.place(self.origin(k), self.dy), 5 + k)
+                self.diag_x(it, k).start()
+
+    def a4(self, its, *ks):
+        for k in ks:
+            for it in its:
+                self.arrived(it, it.place(self.origin(k), self.dd, 0), 8 + k)
+                self.arrived(it, it.place(self.origin(k), self.dd, 1), 11 + k)
+                self.to_core(it, k).start()
+
+    def a5(self, its, *ks):
+        for k in ks:
+            for it in its:
+                self.arrived(it, it.place(self.plane(k) * 2 + 1 - self.core), 14 + k)
+
+    def from_core(self, its):
+        for it in its:
+            self.arrived(it, it.place(self.sib), 18)
+
+    def sent(self, its):
+        for it in its:
+            for k in (1, 2, 3):
+                for make in (self.along_z, self.to_x, self.to_y, self.diag_y, self.diag_x, self.to_core):
+                    make(it, k).wait_send()
+            self.own_copy(it).wait_send()
+
+
+def run_plan(i, plan):
+    for step, act in plan.items():
+        @pl.when(i == step)
+        def _(act=act):
+            act()
+
+
+def down_kernel(
+    n_prompts, x_ref, gs_ref, dq_s, dkv_s, uq_s, ukv_s, cos_ref, sin_ref,
+    c_all, r_ref, cq_all, rt_all, wuq_out, wukv_out,
+    wdq, wdkv, wuq, wukv, gains, gvec, a_all, acc,
+    send_sem, recv_sem, g_send, g_recv, local_sem,
+):
+    i = pl.program_id(0)
+    net = Net(send_sem, recv_sem)
+    d, f, z = net.d, net.f, net.z
+    items = [
+        Item(0, dkv_s, 0, wdkv.shape[1], wdkv), Item(1, dq_s, 0, wdq.shape[1], wdq),
+        Item(2, ukv_s, 0, wukv.shape[1], wukv), Item(3, uq_s, 0, wuq.shape[1], wuq),
+    ]
+    down, up = items[:2], items[2:]
+    others = range(1, 8)
+
+    def keep(it):
+        return pltpu.make_async_copy(it.own(), it.place(f), local_sem.at[it.index])
+
+    def keep_gain():
+        return pltpu.make_async_copy(gs_ref, gains.at[f], local_sem.at[4])
+
+    def gain_copy(j):
+        return pltpu.make_async_remote_copy(
+            src_ref=gs_ref, dst_ref=gains.at[f], send_sem=g_send.at[j - 1], recv_sem=g_recv.at[j - 1],
+            device_id=(d, lax.rem(f + j, 8)), device_id_type=MESH,
+        )
+
+    @pl.when(i == 0)
+    def _():
+        net.barrier([(net.dx, f), (net.dy, f)] + [(d, lax.rem(f + j, 8)) for j in others])
+        for j in others:
+            gain_copy(j).start()
+        keep_gain().start()
+        for it in down:
+            net.own_copy(it).start()
+            keep(it).start()
+        net.send_z(down, 1, 2, 3)
+        net.send_z(up, 1, 2, 3)
+        for it in up:
+            net.own_copy(it).start()
+            keep(it).start()
+        for j in others:
+            gain_copy(j).wait_recv()
+        keep_gain().wait()
+        total = jnp.sum(gains[...], axis=0)
+        for t in range(gvec.shape[1] // LANES):
+            gvec[:, t * LANES:(t + 1) * LANES] = total[t:t + 1, :]
+        for it in down:
+            keep(it).wait()
+        net.from_core(down)
+
+    d_model, q_rank, kv_rank = x_ref.shape[-1], cq_all.shape[-1], c_all.shape[-1]
+    k_rows = d_model // 4
+    s2 = n_prompts
+    end = s2 + 3
+
+    run_plan(i, {
+        3: lambda: net.a2(down, 1),
+        5: lambda: net.a3(down, 1),
+        7: lambda: (net.a2(down, 2), net.a4(down, 1)),
+        s2: lambda: (net.a3(down, 2), net.a5(down, 1)),
+        s2 + 1: lambda: (net.a2(down, 3), net.a4(down, 2), net.a5(down, 2)),
+        s2 + 2: lambda: (net.a3(down, 3), net.a2(up, 1), net.a4(down, 3), net.a5(down, 3)),
+        s2 + 3: lambda: (net.a2(up, 2), net.a3(up, 1)),
+    })
+
+    def partial_sums(p, k):
+        rows = pl.ds(pl.multiple_of(net.plane(k) * k_rows, LANES), k_rows)
+        a = a_all[p, :, rows]
+        qd = jnp.dot(a, wdq[rows], preferred_element_type=jnp.float32)
+        kd = jnp.dot(a, wdkv[rows], preferred_element_type=jnp.float32)
+        if k > 0:
+            qd += acc[p, :, :q_rank]
+            kd += acc[p, :, q_rank:]
+        return qd, kd
+
+    def add_plane(p, k):
+        qd, kd = partial_sums(p, k)
+        acc[p, :, :q_rank] = qd
+        acc[p, :, q_rank:] = kd
+
+    def finish(p):
+        qd, kd = partial_sums(p, 3)
+        cq_all[p] = (qd * inv_rms(qd) * gvec[:, d_model:d_model + q_rank]).astype(jnp.bfloat16)
+        lat = kd[:, :kv_rank]
+        c_all[p] = (lat * inv_rms(lat) * gvec[:, d_model + q_rank:]).astype(jnp.bfloat16)
+        rt = rotate(kd[:, kv_rank:], cos_ref[...], sin_ref[...]).astype(jnp.bfloat16)
+        rt_all[p] = rt
+        r_ref[p] = jnp.concatenate([rt[:, :HALF], rt[:, LANES // 2:LANES // 2 + HALF]], axis=1)
+
+    def each(first_p, n, fn):
+        def body(p, carry):
+            fn(p)
+            return carry
+        lax.fori_loop(first_p, first_p + n, body, 0)
+
+    @pl.when(i < n_prompts)
+    def _():
+        x = x_ref[0].astype(jnp.float32)
+        a_all[i] = (x * inv_rms(x) * gvec[:, :d_model]).astype(jnp.bfloat16)
+        add_plane(i, 0)
+
+    @pl.when(i == s2)
+    def _():
+        each(0, n_prompts, lambda p: add_plane(p, 1))
+
+    @pl.when(i == s2 + 1)
+    def _():
+        each(0, n_prompts, lambda p: add_plane(p, 2))
+
+    @pl.when(i >= s2 + 2)
+    def _():
+        half = n_prompts // 2
+        each((i - s2 - 2) * half, half, finish)
+
+    @pl.when(i == end)
+    def _():
+        net.a3(up, 2)
+        net.a2(up, 3)
+        net.a4(up, 1)
+        net.a3(up, 3)
+        net.a4(up, 2, 3)
+        for it in up:
+            keep(it).wait()
+        net.from_core(up)
+        net.a5(up, 1, 2, 3)
+        outs = [pltpu.make_async_copy(it.full, o, local_sem.at[n]) for n, (it, o) in enumerate(zip(up, (wukv_out, wuq_out)))]
+        for out in outs:
+            out.start()
+        for out in outs:
+            out.wait()
+        for j in others:
+            gain_copy(j).wait_send()
+        net.sent(items)
+
+
+def attend_kernel(
+    n_prompts, cq_ref, c_ref, rt_ref, wuq, wukv, cos_ref, sin_ref, out_s,
+    o_ref, wout_ref, stage, send_sem, recv_sem, local_sem,
+):
+    i = pl.program_id(0)
+    net = Net(send_sem, recv_sem)
+    d, f = net.d, net.f
+    last = [Item(0, out_s, 0, wout_ref.shape[1], wout_ref)]
+
+    def take():
+        return pltpu.make_async_copy(last[0].own(), stage, local_sem.at[0])
+
+    def put():
+        return pltpu.make_async_copy(stage, last[0].place(f), local_sem.at[1])
+
+    @pl.when(i == 0)
+    def _():
+        net.barrier([(net.dx, f), (net.dy, f), (d, net.sib)] + [(d, net.to(k)) for k in (1, 2, 3)])
+        net.send_z(last, 1, 2, 3)
+        net.own_copy(last[0]).start()
+        take().start()
+
+    run_plan(i, {
+        1: lambda: (take().wait(), put().start()),
+        2: lambda: net.a2(last, 1),
+        3: lambda: (net.a2(last, 2), net.a3(last, 1)),
+        4: lambda: (net.a2(last, 3), net.a3(last, 2), net.a4(last, 1)),
+        5: lambda: (net.a3(last, 3), net.a4(last, 2)),
+        6: lambda: net.a4(last, 3),
+    })
+
+    q_cols, kv_cols, o_cols = GROUP * (NOPE + ROPE), GROUP * (NOPE + VDIM), GROUP * VDIM
+    scale = (NOPE + ROPE) ** -0.5 * LOG2E
+    cq = cq_ref[0]
+    lat = c_ref[0]
+    slots = slot_masks(rt_ref[0])
+
+    def body(g, carry):
+        wq = wuq[:, pl.ds(pl.multiple_of(g * q_cols, q_cols), q_cols)]
+        wkv = wukv[:, pl.ds(pl.multiple_of(g * kv_cols, kv_cols), kv_cols)]
+        q = jnp.dot(cq, wq, preferred_element_type=jnp.float32)
+        kv = jnp.dot(lat, wkv, preferred_element_type=jnp.float32)
+        o = attend_heads(q, kv, slots, cos_ref[...], sin_ref[...], scale)
+        o_ref[0, :, pl.ds(pl.multiple_of(g * o_cols, o_cols), o_cols)] = o
+        return carry
+
+    lax.fori_loop(0, wuq.shape[1] // q_cols, body, 0)
+
+    @pl.when(i == n_prompts - 1)
+    def _():
+        put().wait()
+        net.from_core(last)
+        net.a5(last, 1, 2, 3)
+        net.sent(last)
+
+
+def slot_masks(rt):
+    lane = lax.broadcasted_iota(jnp.int32, (1, LANES), 1)
+    slot = lax.rem(lane, LANES // 2) // HALF
+    return [jnp.where(slot == j, rt, 0) for j in range(PE_TILE)]
+
+
+MESH = pl.DeviceIdType.MESH
 GAIN_ROWS = 32
 N_SEND, N_RECV = 19, 19
 
@@ -438,15 +795,13 @@
     return [jnp.where(slot == j, rt, 0) for j in range(PE_TILE)]
 
 
-def out_kernel(x_ref, oa_ref, ob_ref, w_ref, c_in, r_in, y_ref, c_out, r_out):
+def out_kernel(x_ref, o_ref, w_ref, c_in, r_in, y_ref, c_out, r_out):
     step = 512
-    oa, ob = oa_ref[...], ob_ref[...]
-    n_a = oa.shape[1]
+    o = o_ref[...]
     c_out[...] = c_in[...]
     r_out[...] = r_in[...]
     for n in range(0, y_ref.shape[1], step):
-        acc = jnp.dot(oa, w_ref[:n_a, n:n + step], preferred_element_type=jnp.float32)
-        acc += jnp.dot(ob, w_ref[n_a:, n:n + step], preferred_element_type=jnp.float32)
+        acc = jnp.dot(o, w_ref[:, n:n + step], preferred_element_type=jnp.float32)
         y_ref[:, n:n + step] = (x_ref[:, n:n + step].astype(jnp.float32) + acc).astype(jnp.bfloat16)
 
 
@@ -469,49 +824,56 @@
         ]
         n_gain = d_model + q_rank + kv_rank
         gs = jnp.concatenate(spread + [jnp.zeros(GAIN_ROWS * LANES - n_gain, jnp.float32)]).reshape(GAIN_ROWS, LANES)
-        shards = [wdq, arrange_dkv(wdkv, kv_rank), arrange_q(wuq), arrange_kv(wukv), wout]
-        full = lambda w, cols: pltpu.VMEM((w.shape[0] * n_fsdp, cols), jnp.bfloat16)
-        q_cols, kv_cols, o_cols = GROUP * (NOPE + ROPE), GROUP * (NOPE + VDIM), GROUP * VDIM
-        n_groups = wuq.shape[1] // q_cols
-        first, rest = GROUPS_FIRST, n_groups - GROUPS_FIRST
+        shards = [wdq, arrange_dkv(wdkv, kv_rank), arrange_q(wuq), arrange_kv(wukv)]
+        full = lambda w, cols: ((w.shape[0] * n_fsdp, cols), jnp.bfloat16)
         last = n_p - 1
-        blk = lambda cols, lag: pl.BlockSpec((1, seq_len, cols), lambda i: (jnp.clip(i - lag, 0, last), 0, 0))
+        blk = lambda cols: pl.BlockSpec((1, seq_len, cols), lambda i: (jnp.minimum(i, last), 0, 0))
         out = lambda cols: jax.ShapeDtypeStruct((n_p, seq_len, cols), jnp.bfloat16)
         hbm = pl.BlockSpec(memory_space=pl.ANY)
-        c, r, oa, ob, wout_all = pl.pallas_call(
-            functools.partial(core_kernel, n_p),
-            grid=(3 * n_p + 4,),
-            in_specs=[blk(d_model, 0)] + [hbm] * 6 + [whole(cos.shape)] * 2,
-            out_specs=[
-                whole((n_p, seq_len, kv_rank)), whole((n_p, seq_len, ROPE)),
-                blk(first * o_cols, n_p + 4), blk(rest * o_cols, 2 * n_p + 4), hbm,
-            ],
-            out_shape=[
-                out(kv_rank), out(ROPE), out(first * o_cols), out(rest * o_cols),
-                jax.ShapeDtypeStruct((wout.shape[0] * n_fsdp, wout.shape[1]), jnp.bfloat16),
-            ],
+        made = [out(kv_rank), out(ROPE), out(q_rank), out(LANES)]
+        made += [jax.ShapeDtypeStruct(*full(w, w.shape[1])) for w in (wuq, wukv)]
+        params = lambda cid: pltpu.CompilerParams(
+            vmem_limit_bytes=VMEM_LIMIT, dimension_semantics=("arbitrary",), collective_id=cid, has_side_effects=True,
+        )
+        vmem = pl.BlockSpec(memory_space=pltpu.VMEM)
+        c, r, cq, rt, wuq_all, wukv_all = pl.pallas_call(
+            functools.partial(down_kernel, n_p),
+            grid=(n_p + 4,),
+            in_specs=[blk(d_model)] + [hbm] * 5 + [whole(cos.shape)] * 2,
+            out_specs=[vmem] * 4 + [hbm] * 2,
+            out_shape=made,
             scratch_shapes=[
-                full(wdq, q_rank), full(wdkv, kv_rank + LANES),
-                full(wuq, first * q_cols), full(wuq, rest * q_cols),
-                full(wukv, first * kv_cols), full(wukv, rest * kv_cols),
+                pltpu.VMEM(*full(wdq, q_rank)), pltpu.VMEM(*full(wdkv, kv_rank + LANES)),
+                pltpu.VMEM(*full(wuq, wuq.shape[1])), pltpu.VMEM(*full(wukv, wukv.shape[1])),
                 pltpu.VMEM((n_fsdp, GAIN_ROWS, LANES), jnp.float32),
                 pltpu.VMEM((1, n_gain), jnp.float32),
                 pltpu.VMEM((n_p, seq_len, d_model), jnp.bfloat16),
                 pltpu.VMEM((n_p, seq_len, q_rank + kv_rank + LANES), jnp.float32),
-                pltpu.VMEM((n_p, seq_len, q_rank), jnp.bfloat16),
-                pltpu.VMEM((n_p, seq_len, LANES), jnp.bfloat16),
-                pltpu.VMEM(wout.shape, jnp.bfloat16),
-                pltpu.SemaphoreType.DMA((7, N_SEND)),
-                pltpu.SemaphoreType.DMA((7, N_RECV)),
+                pltpu.SemaphoreType.DMA((4, N_SEND)),
+                pltpu.SemaphoreType.DMA((4, N_RECV)),
                 pltpu.SemaphoreType.DMA((7,)),
                 pltpu.SemaphoreType.DMA((7,)),
-                pltpu.SemaphoreType.DMA((9,)),
+                pltpu.SemaphoreType.DMA((5,)),
             ],
-            compiler_params=pltpu.CompilerParams(
-                vmem_limit_bytes=VMEM_LIMIT, dimension_semantics=("arbitrary",), collective_id=0, has_side_effects=True,
-            ),
-            name="core",
+            compiler_params=params(0),
+            name="down",
         )(x, gs, *shards, cos, sin)
+        o_cols = wout.shape[0] * n_fsdp
+        o, wout_all = pl.pallas_call(
+            functools.partial(attend_kernel, n_p),
+            grid=(n_p,),
+            in_specs=[blk(q_rank), blk(kv_rank), blk(LANES)] + [whole(v.shape) for v in (wuq_all, wukv_all, cos, sin)] + [hbm],
+            out_specs=[blk(o_cols), hbm],
+            out_shape=[out(o_cols), jax.ShapeDtypeStruct(*full(wout, wout.shape[1]))],
+            scratch_shapes=[
+                pltpu.VMEM(wout.shape, jnp.bfloat16),
+                pltpu.SemaphoreType.DMA((1, N_SEND)),
+                pltpu.SemaphoreType.DMA((1, N_RECV)),
+                pltpu.SemaphoreType.DMA((2,)),
+            ],
+            compiler_params=params(1),
+            name="attend",
+        )(cq, c, rt, wuq_all, wukv_all, cos, sin, wout)
         rows = 512
         tile = lambda cols: pl.BlockSpec((rows, cols), lambda i: (i, 0))
         flat = lambda v: v.reshape(n_p * seq_len, v.shape[-1])
@@ -519,12 +881,12 @@
         y, c, r = pl.pallas_call(
             out_kernel,
             grid=(n_p * seq_len // rows,),
-            in_specs=[tile(d_model), tile(oa.shape[-1]), tile(ob.shape[-1]), whole(wout_all.shape), tile(kv_rank), tile(ROPE)],
+            in_specs=[tile(d_model), tile(o_cols), whole(wout_all.shape), tile(kv_rank), tile(ROPE)],
             out_specs=[tile(d_model), tile(kv_rank), tile(ROPE)],
             out_shape=[flat_out(d_model), flat_out(kv_rank), flat_out(ROPE)],
             compiler_params=pltpu.CompilerParams(vmem_limit_bytes=VMEM_LIMIT, dimension_semantics=("arbitrary",)),
             name="project",
-        )(flat(x), flat(oa), flat(ob), wout_all, flat(c), flat(r))
+        )(flat(x), flat(o), wout_all, flat(c), flat(r))
         back = lambda v: v.reshape(n_p, seq_len, v.shape[-1])
         return back(y), back(c), back(r)
 

time: 220 us -> 245 us (1.11)
  the two profiles are of different devices: /device:TPU:0 before, /device:TPU:24 now
where the time goes in v5:
time: 245 us
  Pallas kernels  230 us (94%)
  local copies, waits for them, and re-layouts  10.5 us (4%)
  other arithmetic  3.13 us (1%)
    pallas_call x1, Pallas kernels, local_block(): pl.pallas_call(functools.partial(attend_kernel, n_p), grid=(n_p,), in_spe...  110 us
    pallas_call x1, Pallas kernels, local_block(): pl.pallas_call(functools.partial(down_kernel, n_p), grid=(n_p + 4,), in_s...  83.2 us
    pallas_call x1, Pallas kernels, local_block(): pl.pallas_call(out_kernel, grid=(n_p * seq_len // rows,), in_specs=[tile(...  37.3 us

profile of v5, /device:TPU:24, one launch (start us, length us, event | category | flops | bytes accessed | tf_op | source)
XLA Modules:
  0.0 244.8 jit_solution(17042161097838032773)
XLA Ops:
  0.6 0.0 copy-start
  0.7 0.8 convert_dynamic-update-slice_fusion.1
  1.5 0.7 convert_dynamic-update-slice_fusion.2
  2.2 0.8 convert_dynamic-update-slice_fusion
  3.0 0.6 maximum_bitcast_fusion.gs_ref
  3.6 0.7 slice.21
  4.3 0.7 fusion
  5.1 0.1 copy.37
  5.2 0.1 copy.28
  5.3 0.1 copy.26
  5.5 1.0 slice.19
  6.4 0.2 copy.36
  6.6 0.9 concatenate.10.dkv_s
  7.6 1.4 reshape.58
  9.0 0.1 copy.39
  9.1 1.2 reshape.59.ukv_s
  10.2 0.0 copy-done
  10.2 0.6 copy.31
  10.9 0.1 slice.25
  11.0 0.2 pad_maximum_fusion
  11.2 1.2 copy.34.uq_s
  12.5 83.2 %down.1 = (bf16[8,256,256]{2,1,0:T(8,128)(2,1)}, bf16[8,256,32]{2,1,0:T(8,128)(2,1)}, bf16[8,256,768]{2,1,0:T(8,128)(2,1)}, bf16[8,256,128]{2,1,0:T(8,128)(2,1)}...) custom-call(bf16[8,256,2560]{2,1,0:T(8,128)(2,1)} %x_ref.1, f32[32,128]{1,0:T(8,128)} %maximum_bitcast_fusion.gs_ref, ...), custom_call_target="tpu_custom_call" | custom-call | tf_op jit(solution)/shard_map/down/pallas_call | solution.py:839
  95.6 109.9 %attend.1 = (bf16[8,256,2560]{2,1,0:T(8,128)(2,1)}, bf16[2560,2560]{1,0:T(8,128)(2,1)}) custom-call(bf16[8,256,768]{2,1,0:T(8,128)(2,1)} %get-tuple-element.14.cq_ref, bf16[8,256,256]{2,1,0:T(8,128)(2,1)} %get-tuple-element.15.c_ref, bf16[8,256,128]{2,1,0:T(8,128)(2,1)} %get-tuple-element.16.rt_ref, bf16[768,3840]{1,0:T(8,128)(2,1)} %get-tuple-element.17.wuq, ...), custom_call_target="tpu_custom_call" | custom-call | tf_op jit(solution)/shard_map/attend/pallas_call | solution.py:862
  205.6 37.3 %project.1 = (bf16[2048,2560]{1,0:T(8,128)(2,1)}, bf16[2048,256]{1,0:T(8,128)(2,1)}, bf16[2048,32]{1,0:T(8,128)(2,1)}) custom-call(bf16[2048,2560]{1,0:T(8,128)(2,1)} %bitcast.21, bf16[2048,2560]{1,0:T(8,128)(2,1)} %bitcast.22, bf16[2560,2560]{1,0:T(8,128)(2,1)} %get-tuple-element.20.w_ref, bf16[2048,256]{1,0:T(8,128)(2,1)} %bitcast.23, ...), custom_call_target="tpu_custom_call" | custom-call | tf_op jit(solution)/shard_map/project/pallas_call | solution.py:881
  242.9 1.9 copy.35
  (6 shorter events, 0.1 us)
Async XLA Ops:
  0.6 9.6 %copy-start = (bf16[96,3840]{1,0:T(8,128)(2,1)S(1)}, bf16[96,3840]{1,0:T(8,128)(2,1)}, u32[]{:S(2)}) copy-start(bf16[96,3840]{1,0:T(8,128)(2,1)} %param.15) | copy-start | bytes 2211844

commit v6 on v1

v6 whole, which is shorter than its diff:
```python
import functools

import jax
import jax.numpy as jnp
import numpy as np
from jax import lax
from jax.experimental import pallas as pl
from jax.experimental.pallas import tpu as pltpu
from jax.sharding import PartitionSpec as P

EPSILON = 1e-6
ROPE_THETA = 10000.0
LOG2E = 1.4426950408889634
VMEM_LIMIT = 64000 * 1024

NOPE, ROPE, VDIM = 64, 32, 64
HALF = ROPE // 2
GROUP = 8
PE_TILE = 4
LANES = 128
Q_COLS, KV_COLS = GROUP * (NOPE + ROPE), GROUP * (NOPE + VDIM)
AHEAD, SPREAD = 2, 6
MASKED = -1e30


def rope_tiles(seq_len):
    inv_freq = ROPE_THETA ** (-2.0 * np.arange(HALF) / ROPE)
    angles = np.arange(seq_len)[:, None] * inv_freq[None, :]
    cos = np.tile(np.cos(angles), (1, LANES // HALF))
    sin = np.tile(np.sin(angles), (1, PE_TILE))
    return cos.astype(np.float32), np.concatenate([-sin, sin], axis=1).astype(np.float32)


def arrange_q(w):
    rows = w.shape[0]
    w = w.reshape(rows, -1, GROUP, NOPE + ROPE)
    nope = w[..., :NOPE].reshape(rows, -1, GROUP * NOPE)
    pe = w[..., NOPE:].reshape(rows, -1, GROUP // PE_TILE, PE_TILE, 2, HALF)
    pe = pe.transpose(0, 1, 2, 4, 3, 5).reshape(rows, -1, GROUP * ROPE)
    return jnp.concatenate([nope, pe], axis=-1).reshape(rows, -1)


def arrange_kv(w):
    rows = w.shape[0]
    return w.reshape(rows, -1, GROUP, 2, NOPE).transpose(0, 1, 3, 2, 4).reshape(rows, -1)


def arrange_dkv(w, kv_rank):
    lo, hi = w[:, kv_rank:kv_rank + HALF], w[:, kv_rank + HALF:]
    return jnp.concatenate([w[:, :kv_rank]] + [lo] * PE_TILE + [hi] * PE_TILE, axis=1)


def inv_rms(v):
    return lax.rsqrt(jnp.mean(v * v, axis=-1, keepdims=True) + EPSILON)


def rotate(tile, cos, sin):
    return tile * cos + pltpu.roll(tile, LANES // 2, 1) * sin


MESH = pl.DeviceIdType.MESH
GAIN_ROWS = 32
GROUPS_FIRST = 2
N_COPIES = 19
PLANES = (1, 2, 3)


class Item:
    def __init__(self, index, shard, col, cols, full):
        self.index, self.shard, self.col, self.cols, self.full = index, shard, col, cols, full
        self.rows = shard.shape[0]
        if (self.rows // 4) % 16 == 0:
            self.q_rows, self.q_cols = self.rows // 4, cols
        elif (cols // 4) % LANES == 0 and self.rows == 32:
            self.q_rows, self.q_cols = self.rows, cols // 4
        else:
            self.q_rows, self.q_cols = self.rows // 2, cols // 2
        if self.q_rows == self.rows:
            n = self.q_rows // 2
            self.halves = [(0, n, 0, self.q_cols), (n, n, 0, self.q_cols)]
        else:
            n = -(-self.q_cols // (2 * LANES)) * LANES
            self.halves = [(0, self.q_rows, 0, n), (0, self.q_rows, n, self.q_cols - n)]

    def quarter(self, q):
        per_row = self.cols // self.q_cols
        return (q // per_row) * self.q_rows, lax.rem(q, per_row) * self.q_cols

    def source(self, q):
        r, c = self.quarter(q)
        return self.shard.at[pl.ds(pl.multiple_of(r, 16), self.q_rows), pl.ds(pl.multiple_of(self.col + c, LANES), self.q_cols)]

    def own(self):
        return self.shard.at[:, pl.ds(self.col, self.cols)]

    def place(self, f, q=None, half=None):
        r, c = (0, 0) if q is None else self.quarter(q)
        r = f * self.rows + r
        if q is None:
            n_r, n_c = self.rows, self.cols
        elif half is None:
            n_r, n_c = self.q_rows, self.q_cols
        else:
            dr, n_r, dc, n_c = self.halves[half]
            r, c = r + dr, c + dc
        if n_c == self.cols:
            return self.full.at[pl.ds(pl.multiple_of(r, 16), n_r)]
        return self.full.at[pl.ds(pl.multiple_of(r, 16), n_r), pl.ds(pl.multiple_of(c, LANES), n_c)]


class Net:
    def __init__(self, send_sem, recv_sem):
        self.send_sem, self.recv_sem = send_sem, recv_sem
        self.d, self.f = lax.axis_index('dp'), lax.axis_index('fsdp')
        self.z, self.core = self.f // 2, lax.rem(self.f, 2)
        self.dx = lax.rem(self.d + 2, 4)
        self.dy = self.d + 1 - 2 * lax.rem(self.d, 2)
        self.dd = lax.rem(self.dy + 2, 4)
        self.sib = self.z * 2 + 1 - self.core

    def to(self, k):
        return lax.rem(self.z + k, 4) * 2 + self.core

    def plane(self, k):
        return lax.rem(self.z + 4 - k, 4)

    def origin(self, k):
        return self.plane(k) * 2 + self.core

    def copy(self, it, src, dst, s, r, dev):
        return pltpu.make_async_remote_copy(
            src_ref=src, dst_ref=dst, send_sem=self.send_sem.at[it.index, s], recv_sem=self.recv_sem.at[it.index, r],
            device_id=dev, device_id_type=MESH,
        )

    def along_z(self, it, k):
        return self.copy(it, it.source(self.d), it.place(self.f, self.d), k - 1, k - 1, (self.d, self.to(k)))

    def to_x(self, it, k):
        ref = it.place(self.origin(k), self.d)
        return self.copy(it, ref, ref, 2 + k, 2 + k, (self.dx, self.f))

    def to_y(self, it, k):
        ref = it.place(self.origin(k), self.d)
        return self.copy(it, ref, ref, 5 + k, 5 + k, (self.dy, self.f))

    def diag_y(self, it, k):
        ref = it.place(self.origin(k), self.dx, 0)
        return self.copy(it, ref, ref, 8 + k, 8 + k, (self.dy, self.f))

    def diag_x(self, it, k):
        ref = it.place(self.origin(k), self.dy, 1)
        return self.copy(it, ref, ref, 11 + k, 11 + k, (self.dx, self.f))

    def to_core(self, it, k):
        ref = it.place(self.origin(k))
        return self.copy(it, ref, ref, 14 + k, 14 + k, (self.d, self.sib))

    def own_copy(self, it):
        return self.copy(it, it.own(), it.place(self.f), 18, 18, (self.d, self.sib))

    def arrived(self, it, ref, r):
        self.copy(it, ref, ref, 0, r, (self.d, self.f)).wait_recv()

    def barrier(self, peers):
        sem = pltpu.get_barrier_semaphore()
        for peer in peers:
            pl.semaphore_signal(sem, inc=1, device_id=peer, device_id_type=MESH)
        pl.semaphore_wait(sem, len(peers))

    def send_z(self, its, ks=PLANES):
        for k in ks:
            for it in its:
                self.along_z(it, k).start()

    def a2(self, its, ks=PLANES):
        for k in ks:
            for it in its:
                self.arrived(it, it.place(self.origin(k), self.d), k - 1)
                self.to_x(it, k).start()
                self.to_y(it, k).start()

    def a3(self, its, ks=PLANES):
        for k in ks:
            for it in its:
                self.arrived(it, it.place(self.origin(k), self.dx), 2 + k)
                self.diag_y(it, k).start()
                self.arrived(it, it.place(self.origin(k), self.dy), 5 + k)
                self.diag_x(it, k).start()

    def a4(self, its, ks=PLANES):
        for k in ks:
            for it in its:
                self.arrived(it, it.place(self.origin(k), self.dd, 0), 8 + k)
                self.arrived(it, it.place(self.origin(k), self.dd, 1), 11 + k)
                self.to_core(it, k).start()

    def a5(self, its, ks=PLANES):
        for k in ks:
            for it in its:
                self.arrived(it, it.place(self.plane(k) * 2 + 1 - self.core), 14 + k)

    def from_core(self, its):
        for it in its:
            self.arrived(it, it.place(self.sib), 18)

    def sent(self, its):
        for it in its:
            for k in PLANES:
                for make in (self.along_z, self.to_x, self.to_y, self.diag_y, self.diag_x, self.to_core):
                    make(it, k).wait_send()
            self.own_copy(it).wait_send()


def scores(tiles, slots, low, j):
    qn, qp, kn, _ = tiles
    t = j // 2
    keep = low if j % 2 == 0 else jnp.logical_not(low)
    q_tile = jnp.concatenate([qn[t], qp[j // PE_TILE]], axis=1)
    k_tile = jnp.concatenate([jnp.where(keep, kn[t], 0), slots[j % PE_TILE]], axis=1)
    return lax.dot_general(k_tile, q_tile, (((1,), (1,)), ((), ())), preferred_element_type=jnp.float32)


def softmax(s, diag, zero, scale):
    half = s.shape[0] // 2
    left = jnp.where(diag, s[:half, :half], MASKED)
    up = s[:half, half:]
    right = jnp.where(diag, s[half:, half:], MASKED)
    m_l = jnp.max(left, axis=0, keepdims=True) * scale
    m_r = jnp.max(jnp.maximum(up, right), axis=0, keepdims=True) * scale
    e_l = jnp.exp2(left * scale - m_l)
    e_u = jnp.exp2(up * scale - m_r)
    e_r = jnp.exp2(right * scale - m_r)
    r_l = 1.0 / jnp.sum(e_l, axis=0, keepdims=True)
    r_r = 1.0 / jnp.sum(e_u + e_r, axis=0, keepdims=True)
    p_top = jnp.concatenate([(e_l * r_l).astype(jnp.bfloat16), (e_u * r_r).astype(jnp.bfloat16)], axis=1)
    p_bot = jnp.concatenate([zero, (e_r * r_r).astype(jnp.bfloat16)], axis=1)
    return jnp.concatenate([p_top, p_bot], axis=0)


def pieces(cq, lat, wuq, wukv, g, cos, sin):
    w = 2 * LANES

    def tiles(x, weights, cols, n, pe=False):
        r = jnp.dot(x, weights[:, g * cols + n * w:g * cols + (n + 1) * w], preferred_element_type=jnp.float32)
        both = [r[:, :LANES], r[:, LANES:]]
        return [(rotate(t, cos, sin) if pe else t).astype(jnp.bfloat16) for t in both]

    n_q, n_kv = Q_COLS // w, KV_COLS // w
    return [functools.partial(tiles, cq, wuq, Q_COLS, n, n == n_q - 1) for n in range(n_q)] + [
        functools.partial(tiles, lat, wukv, KV_COLS, n) for n in range(n_kv)
    ]


def arrange_tiles(made):
    flat = [t for pair in made for t in pair]
    n = GROUP // 2
    m = n + GROUP // PE_TILE
    return flat[:n], flat[n:m], flat[m:m + n], [t.T for t in flat[m + n:]]


def attend(cq, lat, rt, cq_next, lat_next, start, wuq, wukv, cos, sin, hold, o_ref):
    n_groups = wuq.shape[1] // Q_COLS
    scale = (NOPE + ROPE) ** -0.5 * LOG2E
    seq_len = cq.shape[0]
    half = seq_len // 2
    low = lax.broadcasted_iota(jnp.int32, (1, LANES), 1) < NOPE
    diag = lax.broadcasted_iota(jnp.int32, (half, half), 0) <= lax.broadcasted_iota(jnp.int32, (half, half), 1)
    zero = jnp.zeros((half, half), jnp.bfloat16)
    slots = slot_masks(rt)
    n_pieces = hold.shape[0] // 2

    def put(n, made):
        for m, t in enumerate(made):
            hold[2 * n + m] = t

    @pl.when(start)
    def _():
        for n, make in enumerate(pieces(cq, lat, wuq, wukv, 0, cos, sin)):
            put(n, make())

    tiles = {0: arrange_tiles([[hold[2 * n], hold[2 * n + 1]] for n in range(n_pieces)])}
    total = n_groups * GROUP
    s, p, outs = {}, {}, {}
    for u in range(-AHEAD, total + 1):
        g, j = divmod(u, GROUP)
        if u >= 0 and u < total:
            p[u] = softmax(s.pop(u), diag, zero, scale)
            if j == 0:
                made = []
                if g + 1 < n_groups:
                    todo = pieces(cq, lat, wuq, wukv, g + 1, cos, sin)
                else:
                    todo = pieces(cq_next, lat_next, wuq, wukv, 0, cos, sin)
            if j < SPREAD:
                for n in range(j * n_pieces // SPREAD, (j + 1) * n_pieces // SPREAD):
                    made.append(todo[n]())
                if len(made) == n_pieces and g + 1 < n_groups:
                    tiles[g + 1] = arrange_tiles(made)
                elif len(made) == n_pieces:
                    for n, m in enumerate(made):
                        put(n, m)
        if u + AHEAD < total:
            v = u + AHEAD
            s[v] = scores(tiles[v // GROUP], slots, low, v % GROUP)
        if u >= 1:
            h = u - 1
            hj = h % GROUP
            vt = tiles[h // GROUP][3][hj // 2][hj % 2 * VDIM:(hj % 2 + 1) * VDIM]
            outs[h] = jnp.dot(vt, p.pop(h), preferred_element_type=jnp.float32).astype(jnp.bfloat16)
            if h % 2 == 1:
                pair = jnp.concatenate([outs.pop(h - 1), outs.pop(h)], axis=0)
                o_ref[0, :, h // 2 * LANES:(h // 2 + 1) * LANES] = pair.T


def slot_masks(rt):
    lane = lax.broadcasted_iota(jnp.int32, (1, LANES), 1)
    slot = lax.rem(lane, LANES // 2) // HALF
    return [jnp.where(slot == j, rt, 0) for j in range(PE_TILE)]


def core_kernel(
    n_prompts, x_ref, gs_ref, dq_s, dkv_s, uq_s, ukv_s, out_s, cos_ref, sin_ref,
    c_all, r_ref, oa_ref, ob_ref, wout_ref,
    wdq, wdkv, wuqa, wuqb, wukva, wukvb, gains, gvec, a_all, acc, cq_all, rt_all, stage, hold,
    send_sem, recv_sem, g_send, g_recv, local_sem,
):
    i = pl.program_id(0)
    net = Net(send_sem, recv_sem)
    d, f = net.d, net.f
    n_a, m_a = wuqa.shape[1], wukva.shape[1]
    todo = [
        (dkv_s, 0, wdkv), (dq_s, 0, wdq), (ukv_s, 0, wukva), (uq_s, 0, wuqa),
        (ukv_s, m_a, wukvb), (uq_s, n_a, wuqb), (out_s, 0, wout_ref),
    ]
    items = [Item(n, shard, col, full.shape[1], full) for n, (shard, col, full) in enumerate(todo)]
    down, first, rest, last = items[:2], items[2:4], items[4:6], items[6:]
    wo = items[6]
    others = range(1, 8)

    def keep(it):
        return pltpu.make_async_copy(it.own(), stage if it is wo else it.place(f), local_sem.at[it.index])

    def keep_out():
        return pltpu.make_async_copy(stage, wo.place(f), local_sem.at[7])

    def keep_gain():
        return pltpu.make_async_copy(gs_ref, gains.at[f], local_sem.at[8])

    def gain_copy(j):
        return pltpu.make_async_remote_copy(
            src_ref=gs_ref, dst_ref=gains.at[f], send_sem=g_send.at[j - 1], recv_sem=g_recv.at[j - 1],
            device_id=(d, lax.rem(f + j, 8)), device_id_type=MESH,
        )

    @pl.when(i == 0)
    def _():
        net.barrier([(net.dx, f), (net.dy, f)] + [(d, lax.rem(f + j, 8)) for j in others])
        for j in others:
            gain_copy(j).start()
        keep_gain().start()
        for it in down:
            net.own_copy(it).start()
            keep(it).start()
        for group in (down, first, rest, last):
            net.send_z(group)
        for it in items[2:]:
            net.own_copy(it).start()
            keep(it).start()
        for j in others:
            gain_copy(j).wait_recv()
        keep_gain().wait()
        total = jnp.sum(gains[...], axis=0)
        for t in range(gvec.shape[1] // LANES):
            gvec[:, t * LANES:(t + 1) * LANES] = total[t:t + 1, :]
        for it in down:
            keep(it).wait()
        net.from_core(down)

    d_model, q_rank, kv_rank = x_ref.shape[-1], cq_all.shape[-1], c_all.shape[-1]
    seq_len = x_ref.shape[1]
    k_rows = d_model // 4
    half = n_prompts // 2
    c1 = n_prompts
    c2 = c1 + half
    fin = c2 + half
    pa = fin + half
    pb = pa + n_prompts
    end = pb + n_prompts - 1
    one, two, three = ((k,) for k in PLANES)

    @pl.when(i == 1)
    def _():
        keep(wo).wait()
        keep_out().start()

    def ready(its):
        for it in its:
            (keep_out() if it is wo else keep(it)).wait()
        net.from_core(its)
        net.a5(its)

    plan = [
        (4, [(net.a2, down, one)]),
        (7, [(net.a2, down, two), (net.a3, down, one)]),
        (c1, [(net.a4, down, one), (net.a2, down, three), (net.a3, down, two), (net.a5, down, one)]),
        (c1 + 2, [(net.a4, down, two)]),
        (c1 + 3, [(net.a3, down, three), (net.a2, first, one)]),
        (c2, [(net.a2, first, two), (net.a5, down, two)]),
        (c2 + 1, [(net.a3, first, one), (net.a2, first, three)]),
        (c2 + 2, [(net.a4, down, three)]),
        (c2 + 3, [(net.a3, first, two), (net.a2, rest, one)]),
        (fin, [(net.a5, down, three), (net.a3, first, three), (net.a4, first, one)]),
        (fin + 1, [(net.a4, first, two)]),
        (fin + 2, [(net.a2, rest, two), (net.a3, rest, one), (net.a4, first, three)]),
        (pa, [(net.a2, rest, three), (net.a3, rest, two), (net.a4, rest, one)]),
        (pa + 1, [(net.a3, rest, three), (net.a4, rest, two)]),
        (pa + 2, [(net.a4, rest, three)]),
        (pa + 4, [(net.a2, last, one)]),
        (pa + 6, [(net.a3, last, one)]),
        (pb, [(net.a4, last, one), (net.a2, last, two)]),
        (pb + 2, [(net.a3, last, two)]),
        (pb + 3, [(net.a2, last, three), (net.a4, last, two)]),
        (pb + 5, [(net.a3, last, three)]),
        (pb + 6, [(net.a4, last, three)]),
    ]
    for step, acts in plan:
        @pl.when(i == step)
        def _(acts=acts):
            for act, its, ks in acts:
                act(its, ks)

    for step, its in ((pa, first), (pb, rest)):
        @pl.when(i == step)
        def _(its=its):
            ready(its)

    def partial_sums(p, n, k):
        rows = pl.ds(pl.multiple_of(net.plane(k) * k_rows, LANES), k_rows)
        a = a_all[pl.ds(p, n), :, rows].reshape(n * seq_len, k_rows)
        qd = jnp.dot(a, wdq[rows], preferred_element_type=jnp.float32)
        kd = jnp.dot(a, wdkv[rows], preferred_element_type=jnp.float32)
        if k > 0:
            old = acc[pl.ds(p, n)].reshape(n * seq_len, q_rank + kv_rank + LANES)
            qd += old[:, :q_rank]
            kd += old[:, q_rank:]
        return qd, kd

    def add_plane(p, n, k):
        qd, kd = partial_sums(p, n, k)
        acc[pl.ds(p, n), :, :q_rank] = qd.reshape(n, seq_len, q_rank)
        acc[pl.ds(p, n), :, q_rank:] = kd.reshape(n, seq_len, kv_rank + LANES)

    @pl.when(i < c1)
    def _():
        x = x_ref[0].astype(jnp.float32)
        a_all[i] = (x * inv_rms(x) * gvec[:, :d_model]).astype(jnp.bfloat16)
        add_plane(i, 1, 0)

    @pl.when(jnp.logical_and(i >= c1, i < c2))
    def _():
        add_plane((i - c1) * 2, 2, 1)

    @pl.when(jnp.logical_and(i >= c2, i < fin))
    def _():
        add_plane((i - c2) * 2, 2, 2)

    @pl.when(jnp.logical_and(i >= fin, i < pa))
    def _():
        p = (i - fin) * 2
        qd, kd = partial_sums(p, 2, 3)
        cq = (qd * inv_rms(qd) * gvec[:, d_model:d_model + q_rank]).astype(jnp.bfloat16)
        cq_all[pl.ds(p, 2)] = cq.reshape(2, seq_len, q_rank)
        lat = kd[:, :kv_rank]
        lat = (lat * inv_rms(lat) * gvec[:, d_model + q_rank:]).astype(jnp.bfloat16)
        c_all[pl.ds(p, 2)] = lat.reshape(2, seq_len, kv_rank)
        for n in range(2):
            pe = kd[n * seq_len:(n + 1) * seq_len, kv_rank:]
            rt = rotate(pe, cos_ref[...], sin_ref[...]).astype(jnp.bfloat16)
            rt_all[p + n] = rt
            rt_t = rt.T
            r_ref[p + n] = jnp.concatenate([rt_t[:HALF], rt_t[LANES // 2:LANES // 2 + HALF]], axis=0)

    def attend_step(p, wuq, wukv, o_ref):
        after = jnp.minimum(p + 1, n_prompts - 1)
        attend(
            cq_all[p], c_all[p], rt_all[p], cq_all[after], c_all[after], p == 0,
            wuq, wukv, cos_ref[...], sin_ref[...], hold, o_ref,
        )

    @pl.when(jnp.logical_and(i >= pa, i < pb))
    def _():
        attend_step(i - pa, wuqa, wukva, oa_ref)

    @pl.when(i >= pb)
    def _():
        attend_step(i - pb, wuqb, wukvb, ob_ref)

    @pl.when(i == end)
    def _():
        ready(last)
        for j in others:
            gain_copy(j).wait_send()
        net.sent(items)


def out_kernel(x_ref, oa_ref, ob_ref, w_hbm, c_in, r_in, y_ref, c_out, r_out, w, sem):
    step = 512
    n_steps = y_ref.shape[1] // step
    first = pl.program_id(0) == 0
    cols = [slice(n * step, (n + 1) * step) for n in range(n_steps)]
    load = [pltpu.make_async_copy(w_hbm.at[:, c], w.at[:, c], sem.at[n]) for n, c in enumerate(cols)]

    @pl.when(first)
    def _():
        for part in load:
            part.start()

    oa, ob = oa_ref[...], ob_ref[...]
    n_a = oa.shape[1]
    c_out[...] = c_in[...]
    r_out[...] = r_in[...]
    for part, c in zip(load, cols):
        @pl.when(first)
        def _(part=part):
            part.wait()

        acc = jnp.dot(oa, w[:n_a, c], preferred_element_type=jnp.float32)
        acc += jnp.dot(ob, w[n_a:, c], preferred_element_type=jnp.float32)
        y_ref[:, c] = (x_ref[:, c].astype(jnp.float32) + acc).astype(jnp.bfloat16)


def whole(shape):
    return pl.BlockSpec(shape, lambda i: (0,) * len(shape))


def solution(mesh):
    n_fsdp = mesh.shape['fsdp']

    def local_block(x, g1, wdq, gq, wuq, wdkv, gkv, wukv, wout):
        n_p, seq_len, d_model = x.shape
        kv_rank, q_rank = gkv.shape[0] * n_fsdp, wdq.shape[1]
        cos_np, sin_np = rope_tiles(seq_len)
        cos, sin = jnp.asarray(cos_np), jnp.asarray(sin_np)
        me = lax.axis_index('fsdp')
        spread = [
            lax.dynamic_update_slice(jnp.zeros(g.shape[0] * n_fsdp, jnp.float32), g.astype(jnp.float32), (me * g.shape[0],))
            for g in (g1, gq, gkv)
        ]
        n_gain = d_model + q_rank + kv_rank
        gs = jnp.concatenate(spread + [jnp.zeros(GAIN_ROWS * LANES - n_gain, jnp.float32)]).reshape(GAIN_ROWS, LANES)
        shards = [wdq, arrange_dkv(wdkv, kv_rank), arrange_q(wuq), arrange_kv(wukv), wout]
        full = lambda w, cols: pltpu.VMEM((w.shape[0] * n_fsdp, cols), jnp.bfloat16)
        o_cols = GROUP * VDIM
        n_groups = wuq.shape[1] // Q_COLS
        first, rest = GROUPS_FIRST, n_groups - GROUPS_FIRST
        last = n_p - 1
        pa = 2 * n_p + n_p // 2
        blk = lambda cols, lag: pl.BlockSpec((1, seq_len, cols), lambda i: (jnp.clip(i - lag, 0, last), 0, 0))
        out = lambda cols: jax.ShapeDtypeStruct((n_p, seq_len, cols), jnp.bfloat16)
        r_shape = jax.ShapeDtypeStruct((n_p, ROPE, seq_len), jnp.bfloat16)
        hbm = pl.BlockSpec(memory_space=pl.ANY)
        c, r, oa, ob, wout_all = pl.pallas_call(
            functools.partial(core_kernel, n_p),
            grid=(4 * n_p + n_p // 2,),
            in_specs=[blk(d_model, 0)] + [hbm] * 6 + [whole(cos.shape)] * 2,
            out_specs=[
                whole((n_p, seq_len, kv_rank)), whole((n_p, ROPE, seq_len)),
                blk(first * o_cols, pa), blk(rest * o_cols, pa + n_p), hbm,
            ],
            out_shape=[
                out(kv_rank), r_shape, out(first * o_cols), out(rest * o_cols),
                jax.ShapeDtypeStruct((wout.shape[0] * n_fsdp, wout.shape[1]), jnp.bfloat16),
            ],
            scratch_shapes=[
                full(wdq, q_rank), full(wdkv, kv_rank + LANES),
                full(wuq, first * Q_COLS), full(wuq, rest * Q_COLS),
                full(wukv, first * KV_COLS), full(wukv, rest * KV_COLS),
                pltpu.VMEM((n_fsdp, GAIN_ROWS, LANES), jnp.float32),
                pltpu.VMEM((1, n_gain), jnp.float32),
                pltpu.VMEM((n_p, seq_len, d_model), jnp.bfloat16),
                pltpu.VMEM((n_p, seq_len, q_rank + kv_rank + LANES), jnp.float32),
                pltpu.VMEM((n_p, seq_len, q_rank), jnp.bfloat16),
                pltpu.VMEM((n_p, seq_len, LANES), jnp.bfloat16),
                pltpu.VMEM(wout.shape, jnp.bfloat16),
                pltpu.VMEM(((Q_COLS + KV_COLS) // LANES, seq_len, LANES), jnp.bfloat16),
                pltpu.SemaphoreType.DMA((7, N_COPIES)),
                pltpu.SemaphoreType.DMA((7, N_COPIES)),
                pltpu.SemaphoreType.DMA((7,)),
                pltpu.SemaphoreType.DMA((7,)),
                pltpu.SemaphoreType.DMA((9,)),
            ],
            compiler_params=pltpu.CompilerParams(
                vmem_limit_bytes=VMEM_LIMIT, dimension_semantics=("arbitrary",), collective_id=0, has_side_effects=True,
            ),
            name="core",
        )(x, gs, *shards, cos, sin)
        rows = 512
        tile = lambda cols: pl.BlockSpec((rows, cols), lambda i: (i, 0))
        r_tile = pl.BlockSpec((rows // seq_len, ROPE, seq_len), lambda i: (i, 0, 0))
        flat = lambda v: v.reshape(n_p * seq_len, v.shape[-1])
        flat_out = lambda cols: jax.ShapeDtypeStruct((n_p * seq_len, cols), jnp.bfloat16)
        y, c, r = pl.pallas_call(
            out_kernel,
            grid=(n_p * seq_len // rows,),
            in_specs=[tile(d_model), tile(oa.shape[-1]), tile(ob.shape[-1]), hbm, tile(kv_rank), r_tile],
            out_specs=[tile(d_model), tile(kv_rank), r_tile],
            out_shape=[flat_out(d_model), flat_out(kv_rank), r_shape],
            scratch_shapes=[pltpu.VMEM(wout_all.shape, jnp.bfloat16), pltpu.SemaphoreType.DMA((8,))],
            compiler_params=pltpu.CompilerParams(vmem_limit_bytes=VMEM_LIMIT, dimension_semantics=("arbitrary",)),
            name="project",
        )(flat(x), flat(oa), flat(ob), wout_all, flat(c), r)
        back = lambda v: v.reshape(n_p, seq_len, v.shape[-1])
        return back(y), back(c), jnp.swapaxes(r, 1, 2)

    batch, row, mat = P(('dp', 'fsdp')), P('fsdp'), P('fsdp', None)
    return jax.shard_map(
        local_block,
        mesh=mesh,
        in_specs=(batch, row, mat, row, mat, mat, row, mat, mat),
        out_specs=(batch, batch, batch),
        check_vma=False,
    )
```

time: 405 us -> 198 us (0.49)
  waiting for transfers between devices: 215 us -> 0 us
  Pallas kernels: 138 us -> 185 us
  blocking collectives: 18.8 us -> 0 us
  between operations: 15.9 us -> 0.92 us
  local copies, waits for them, and re-layouts: 15.6 us -> 8.63 us
    all_gather x5 -> x0, waiting for transfers between devices: 215 us -> none  [gather(): return lax.all_gather(part, ('fsdp', 'dp'), tiled=True)]
    pallas_call x3 -> x2, Pallas kernels: 138 us -> 185 us  [the longest x1 147 us: local_block(): pl.pallas_call(functools.partial(core_kernel, n_p), grid=(4 * n_p + n_p /...]
    unnamed x1 -> x0, blocking collectives: 18.8 us -> none
    unnamed x26 -> x5, local copies, waits for them, and re-layouts: 5.22 us -> 0.96 us
    dynamic_slice x5 -> x0, local copies, waits for them, and re-layouts: 4.09 us -> none  [gather(): part = lax.dynamic_slice_in_dim(w, lax.axis_index('dp') * rows, rows, 0)]
  transfers between devices with their start and end apart: 5 -> 0, of which waited for: 5 -> 0; matrix products, arithmetic and copies ran while one was open for 3% -> 0% of each run, Pallas kernels for 25% -> 0%
where the time goes in v6:
time: 198 us; the launch traced here: 197 us
  Pallas kernels  185 us (93%)
  local copies, waits for them, and re-layouts  8.63 us (4%)
  other arithmetic  3.13 us (2%)
    pallas_call x1, Pallas kernels, local_block(): pl.pallas_call(functools.partial(core_kernel, n_p), grid=(4 * n_p + n_p /...  147 us
    pallas_call x1, Pallas kernels, local_block(): pl.pallas_call(out_kernel, grid=(n_p * seq_len // rows,), in_specs=[tile(...  37.8 us

profile of v6, /device:TPU:0, one launch (start us, length us, event | category | flops | bytes accessed | tf_op | source)
XLA Modules:
  0.0 197.3 jit_solution(8441893448816902976)
XLA Ops:
  0.6 0.0 copy-start
  0.7 0.8 convert_dynamic-update-slice_fusion.1
  1.5 0.7 convert_dynamic-update-slice_fusion.2
  2.2 0.8 convert_dynamic-update-slice_fusion
  3.0 0.6 maximum_bitcast_fusion.gs_ref
  3.6 0.7 slice.21
  4.3 0.7 fusion
  5.1 0.1 copy.35
  5.2 0.1 copy.27
  5.3 0.1 copy.25
  5.5 1.0 slice.19
  6.4 0.2 copy.34
  6.6 1.0 concatenate.10.dkv_s
  7.6 1.4 reshape.55
  9.0 0.1 copy.37
  9.1 1.2 reshape.56.ukv_s
  10.3 0.0 copy-done
  10.3 0.6 copy.30
  10.9 0.1 slice.25
  11.1 0.2 pad_maximum_fusion
  11.3 1.2 copy.33.uq_s
  12.5 146.8 %core.1 = (bf16[8,256,256]{2,1,0:T(8,128)(2,1)}, bf16[8,32,256]{2,1,0:T(8,128)(2,1)}, bf16[8,256,1024]{2,1,0:T(8,128)(2,1)}, bf16[8,256,1536]{2,1,0:T(8,128)(2,1)}, bf16[2560,2560]{1,0:T(8,128)(2,1)}) custom-call(bf16[8,256,2560]{2,1,0:T(8,128)(2,1)} %x_ref.1, f32[32,128]{1,0:T(8,128)} %maximum_bitcast_fusion.gs_ref, bf16[320,768]{1,0:T(8,128)(2,1)} %dq_s.1, ...), custom_call_target="tpu_custom_call" | custom-call | tf_op jit(solution)/shard_map/core/pallas_call | solution.py:563
  159.3 37.8 %project.1 = (bf16[2048,2560]{1,0:T(8,128)(2,1)}, bf16[2048,256]{1,0:T(8,128)(2,1)}, bf16[8,32,256]{2,1,0:T(8,128)(2,1)}) custom-call(bf16[2048,2560]{1,0:T(8,128)(2,1)} %bitcast.21, bf16[2048,1024]{1,0:T(8,128)(2,1)} %bitcast.23, bf16[2048,1536]{1,0:T(8,128)(2,1)} %bitcast.22, bf16[2560,2560]{1,0:T(8,128)(2,1)} %get-tuple-element.13.w_hbm, ...), custom_call_target="tpu_custom_call" | custom-call | tf_op jit(solution)/shard_map/project/pallas_call | solution.py:603
  (6 shorter events, 0.1 us)
Async XLA Ops:
  0.6 9.6 %copy-start = (bf16[96,3840]{1,0:T(8,128)(2,1)S(1)}, bf16[96,3840]{1,0:T(8,128)(2,1)}, u32[]{:S(2)}) copy-start(bf16[96,3840]{1,0:T(8,128)(2,1)} %param.15) | copy-start | bytes 2211844

commit v7 on v6

--- a/solution.py
+++ b/solution.py
@@ -362,8 +362,7 @@
         for it in down:
             net.own_copy(it).start()
             keep(it).start()
-        for group in (down, first, rest, last):
-            net.send_z(group)
+        net.send_z(down)
         for it in items[2:]:
             net.own_copy(it).start()
             keep(it).start()
@@ -401,28 +400,35 @@
         net.a5(its)
 
     plan = [
-        (4, [(net.a2, down, one)]),
-        (7, [(net.a2, down, two), (net.a3, down, one)]),
-        (c1, [(net.a4, down, one), (net.a2, down, three), (net.a3, down, two), (net.a5, down, one)]),
-        (c1 + 2, [(net.a4, down, two)]),
-        (c1 + 3, [(net.a3, down, three), (net.a2, first, one)]),
-        (c2, [(net.a2, first, two), (net.a5, down, two)]),
-        (c2 + 1, [(net.a3, first, one), (net.a2, first, three)]),
-        (c2 + 2, [(net.a4, down, three)]),
-        (c2 + 3, [(net.a3, first, two), (net.a2, rest, one)]),
-        (fin, [(net.a5, down, three), (net.a3, first, three), (net.a4, first, one)]),
-        (fin + 1, [(net.a4, first, two)]),
-        (fin + 2, [(net.a2, rest, two), (net.a3, rest, one), (net.a4, first, three)]),
-        (pa, [(net.a2, rest, three), (net.a3, rest, two), (net.a4, rest, one)]),
-        (pa + 1, [(net.a3, rest, three), (net.a4, rest, two)]),
-        (pa + 2, [(net.a4, rest, three)]),
-        (pa + 4, [(net.a2, last, one)]),
-        (pa + 6, [(net.a3, last, one)]),
-        (pb, [(net.a4, last, one), (net.a2, last, two)]),
-        (pb + 2, [(net.a3, last, two)]),
-        (pb + 3, [(net.a2, last, three), (net.a4, last, two)]),
-        (pb + 5, [(net.a3, last, three)]),
-        (pb + 6, [(net.a4, last, three)]),
+        (1, [(net.send_z, first, one)]),
+        (2, [(net.send_z, rest, one)]),
+        (3, [(net.send_z, first, three)]),
+        (5, [(net.a2, down, one), (net.send_z, first, two)]),
+        (6, [(net.a3, down, one)]),
+        (7, [(net.a2, down, two)]),
+        (8, [(net.a4, down, one), (net.a2, down, three), (net.a5, down, one), (net.a3, down, two)]),
+        (9, [(net.a2, first, one)]),
+        (10, [(net.send_z, rest, three), (net.send_z, last, one)]),
+        (11, [(net.a4, down, two), (net.a3, down, three)]),
+        (12, [(net.a2, first, three), (net.a3, first, one), (net.a5, down, two), (net.send_z, rest, two)]),
+        (13, [(net.a2, first, two), (net.a2, rest, one), (net.a4, down, three)]),
+        (15, [(net.a3, first, two), (net.a5, down, three)]),
+        (16, [(net.a4, first, one), (net.a3, first, three), (net.a2, rest, three)]),
+        (17, [(net.a4, first, two)]),
+        (19, [(net.a4, first, three), (net.a3, rest, three)]),
+        (20, [(net.send_z, last, two), (net.a2, rest, two)]),
+        (21, [(net.a3, rest, one)]),
+        (22, [(net.a2, last, one)]),
+        (24, [(net.a4, rest, one), (net.send_z, last, three)]),
+        (25, [(net.a3, rest, two), (net.a4, rest, three)]),
+        (27, [(net.a4, rest, two), (net.a2, last, two)]),
+        (28, [(net.a3, last, one)]),
+        (29, [(net.a2, last, three)]),
+        (31, [(net.a3, last, two)]),
+        (32, [(net.a4, last, one)]),
+        (33, [(net.a3, last, three)]),
+        (34, [(net.a4, last, two)]),
+        (35, [(net.a4, last, three)]),
     ]
     for step, acts in plan:
         @pl.when(i == step)

time: 198 us -> 187 us (0.944); the launches traced: 197 us -> 183 us
  Pallas kernels: 185 us -> 171 us
    pallas_call x1, Pallas kernels: 147 us -> 133 us  [local_block(): pl.pallas_call(functools.partial(core_kernel, n_p), grid=(4 * n_p + n_p /...]
where the time goes in v7:
time: 187 us; the launch traced here: 183 us
  Pallas kernels  171 us (91%)
  local copies, waits for them, and re-layouts  8.63 us (5%)
  other arithmetic  3.13 us (2%)
    pallas_call x1, Pallas kernels, local_block(): pl.pallas_call(functools.partial(core_kernel, n_p), grid=(4 * n_p + n_p /...  133 us
    pallas_call x1, Pallas kernels, local_block(): pl.pallas_call(out_kernel, grid=(n_p * seq_len // rows,), in_specs=[tile(...  37.8 us

profile of v7, /device:TPU:0, one launch (start us, length us, event | category | flops | bytes accessed | tf_op | source)
XLA Modules:
  0.0 183.3 jit_solution(6656781123358246909)
XLA Ops:
  0.6 0.0 copy-start
  0.7 0.8 convert_dynamic-update-slice_fusion.1
  1.5 0.7 convert_dynamic-update-slice_fusion.2
  2.2 0.8 convert_dynamic-update-slice_fusion
  3.0 0.6 maximum_bitcast_fusion.gs_ref
  3.6 0.7 slice.21
  4.3 0.7 fusion
  5.1 0.1 copy.35
  5.2 0.1 copy.27
  5.3 0.1 copy.25
  5.5 1.0 slice.19
  6.4 0.2 copy.34
  6.6 1.0 concatenate.10.dkv_s
  7.6 1.4 reshape.55
  9.0 0.1 copy.37
  9.1 1.2 reshape.56.ukv_s
  10.3 0.0 copy-done
  10.3 0.6 copy.30
  10.9 0.1 slice.25
  11.1 0.2 pad_maximum_fusion
  11.3 1.2 copy.33.uq_s
  12.5 132.8 %core.1 = (bf16[8,256,256]{2,1,0:T(8,128)(2,1)}, bf16[8,32,256]{2,1,0:T(8,128)(2,1)}, bf16[8,256,1024]{2,1,0:T(8,128)(2,1)}, bf16[8,256,1536]{2,1,0:T(8,128)(2,1)}, bf16[2560,2560]{1,0:T(8,128)(2,1)}) custom-call(bf16[8,256,2560]{2,1,0:T(8,128)(2,1)} %x_ref.1, f32[32,128]{1,0:T(8,128)} %maximum_bitcast_fusion.gs_ref, bf16[320,768]{1,0:T(8,128)(2,1)} %dq_s.1, ...), custom_call_target="tpu_custom_call" | custom-call | tf_op jit(solution)/shard_map/core/pallas_call | solution.py:569
  145.3 37.8 %project.1 = (bf16[2048,2560]{1,0:T(8,128)(2,1)}, bf16[2048,256]{1,0:T(8,128)(2,1)}, bf16[8,32,256]{2,1,0:T(8,128)(2,1)}) custom-call(bf16[2048,2560]{1,0:T(8,128)(2,1)} %bitcast.21, bf16[2048,1024]{1,0:T(8,128)(2,1)} %bitcast.23, bf16[2048,1536]{1,0:T(8,128)(2,1)} %bitcast.22, bf16[2560,2560]{1,0:T(8,128)(2,1)} %get-tuple-element.13.w_hbm, ...), custom_call_target="tpu_custom_call" | custom-call | tf_op jit(solution)/shard_map/project/pallas_call | solution.py:609
  (6 shorter events, 0.1 us)
Async XLA Ops:
  0.6 9.6 %copy-start = (bf16[96,3840]{1,0:T(8,128)(2,1)S(1)}, bf16[96,3840]{1,0:T(8,128)(2,1)}, u32[]{:S(2)}) copy-start(bf16[96,3840]{1,0:T(8,128)(2,1)} %param.15) | copy-start | bytes 2211844

commit v8 on v7

--- a/solution.py
+++ b/solution.py
@@ -29,25 +29,6 @@
     cos = np.tile(np.cos(angles), (1, LANES // HALF))
     sin = np.tile(np.sin(angles), (1, PE_TILE))
     return cos.astype(np.float32), np.concatenate([-sin, sin], axis=1).astype(np.float32)
-
-
-def arrange_q(w):
-    rows = w.shape[0]
-    w = w.reshape(rows, -1, GROUP, NOPE + ROPE)
-    nope = w[..., :NOPE].reshape(rows, -1, GROUP * NOPE)
-    pe = w[..., NOPE:].reshape(rows, -1, GROUP // PE_TILE, PE_TILE, 2, HALF)
-    pe = pe.transpose(0, 1, 2, 4, 3, 5).reshape(rows, -1, GROUP * ROPE)
-    return jnp.concatenate([nope, pe], axis=-1).reshape(rows, -1)
-
-
-def arrange_kv(w):
-    rows = w.shape[0]
-    return w.reshape(rows, -1, GROUP, 2, NOPE).transpose(0, 1, 3, 2, 4).reshape(rows, -1)
-
-
-def arrange_dkv(w, kv_rank):
-    lo, hi = w[:, kv_rank:kv_rank + HALF], w[:, kv_rank + HALF:]
-    return jnp.concatenate([w[:, :kv_rank]] + [lo] * PE_TILE + [hi] * PE_TILE, axis=1)
 
 
 def inv_rms(v):
@@ -216,9 +197,9 @@
     qn, qp, kn, _ = tiles
     t = j // 2
     keep = low if j % 2 == 0 else jnp.logical_not(low)
-    q_tile = jnp.concatenate([qn[t], qp[j // PE_TILE]], axis=1)
+    q_tile = jnp.concatenate([qn[t], qp[j // PE_TILE]], axis=0)
     k_tile = jnp.concatenate([jnp.where(keep, kn[t], 0), slots[j % PE_TILE]], axis=1)
-    return lax.dot_general(k_tile, q_tile, (((1,), (1,)), ((), ())), preferred_element_type=jnp.float32)
+    return jnp.dot(k_tile, q_tile, preferred_element_type=jnp.float32)
 
 
 def softmax(s, diag, zero, scale):
@@ -256,7 +237,8 @@
     flat = [t for pair in made for t in pair]
     n = GROUP // 2
     m = n + GROUP // PE_TILE
-    return flat[:n], flat[n:m], flat[m:m + n], [t.T for t in flat[m + n:]]
+    turned = [t.T for t in flat[:m]]
+    return turned[:n], turned[n:], flat[m:m + n], [t.T for t in flat[m + n:]]
 
 
 def attend(cq, lat, rt, cq_next, lat_next, start, wuq, wukv, cos, sin, hold, o_ref):
@@ -510,6 +492,53 @@
         net.sent(items)
 
 
+def one_hot(source, n_rows):
+    rows = lax.broadcasted_iota(jnp.int32, (n_rows, source.shape[1]), 0)
+    return (rows == source).astype(jnp.float32).astype(jnp.bfloat16)
+
+
+def pick(w, matrix):
+    return jnp.dot(w, matrix, preferred_element_type=jnp.float32).astype(jnp.bfloat16)
+
+
+def prepare_kernel(g1_ref, gq_ref, gkv_ref, wuq_ref, wukv_ref, wdkv_ref, gs_ref, uq_ref, ukv_ref, dkv_ref):
+    f = lax.axis_index('fsdp')
+    row = 0
+    gs_ref[...] = jnp.zeros_like(gs_ref)
+    for g in (g1_ref, gq_ref, gkv_ref):
+        n = g.shape[1]
+        for t in range(n * 8 // LANES):
+            index = lax.broadcasted_iota(jnp.int32, (1, LANES), 1) + (t * LANES - f * n)
+            gs_ref[row:row + 1, :] = jnp.dot(g[...], one_hot(index, n), preferred_element_type=jnp.float32)
+            row += 1
+
+    def column(n):
+        return lax.broadcasted_iota(jnp.int32, (1, n), 1)
+
+    c = column(Q_COLS)
+    n_nope = GROUP * NOPE
+    pe = c - n_nope
+    head = pe // LANES * PE_TILE + lax.rem(pe, LANES // 2) // HALF
+    pe = head * (NOPE + ROPE) + NOPE + lax.rem(pe, LANES) // (LANES // 2) * HALF + lax.rem(pe, HALF)
+    order = one_hot(jnp.where(c < n_nope, c // NOPE * (NOPE + ROPE) + lax.rem(c, NOPE), pe), Q_COLS)
+    for g in range(wuq_ref.shape[1] // Q_COLS):
+        cols = slice(g * Q_COLS, (g + 1) * Q_COLS)
+        uq_ref[:, cols] = pick(wuq_ref[:, cols], order)
+
+    c = column(KV_COLS)
+    part = lax.rem(c, n_nope)
+    order = one_hot(part // NOPE * (NOPE + VDIM) + c // n_nope * NOPE + lax.rem(part, NOPE), KV_COLS)
+    for g in range(wukv_ref.shape[1] // KV_COLS):
+        cols = slice(g * KV_COLS, (g + 1) * KV_COLS)
+        ukv_ref[:, cols] = pick(wukv_ref[:, cols], order)
+
+    kv_rank = dkv_ref.shape[1] - LANES
+    c = column(LANES)
+    dkv_ref[:, :kv_rank] = wdkv_ref[:, :kv_rank]
+    order = one_hot(c // (LANES // 2) * HALF + lax.rem(c, HALF), ROPE)
+    dkv_ref[:, kv_rank:] = pick(wdkv_ref[:, kv_rank:], order)
+
+
 def out_kernel(x_ref, oa_ref, ob_ref, w_hbm, c_in, r_in, y_ref, c_out, r_out, w, sem):
     step = 512
     n_steps = y_ref.shape[1] // step
@@ -522,8 +551,7 @@
         for part in load:
             part.start()
 
-    oa, ob = oa_ref[...], ob_ref[...]
-    n_a = oa.shape[1]
+    o = jnp.concatenate([oa_ref[...], ob_ref[...]], axis=1)
     c_out[...] = c_in[...]
     r_out[...] = r_in[...]
     for part, c in zip(load, cols):
@@ -531,8 +559,7 @@
         def _(part=part):
             part.wait()
 
-        acc = jnp.dot(oa, w[:n_a, c], preferred_element_type=jnp.float32)
-        acc += jnp.dot(ob, w[n_a:, c], preferred_element_type=jnp.float32)
+        acc = jnp.dot(o, w[:, c], preferred_element_type=jnp.float32)
         y_ref[:, c] = (x_ref[:, c].astype(jnp.float32) + acc).astype(jnp.bfloat16)
 
 
@@ -548,14 +575,17 @@
         kv_rank, q_rank = gkv.shape[0] * n_fsdp, wdq.shape[1]
         cos_np, sin_np = rope_tiles(seq_len)
         cos, sin = jnp.asarray(cos_np), jnp.asarray(sin_np)
-        me = lax.axis_index('fsdp')
-        spread = [
-            lax.dynamic_update_slice(jnp.zeros(g.shape[0] * n_fsdp, jnp.float32), g.astype(jnp.float32), (me * g.shape[0],))
-            for g in (g1, gq, gkv)
-        ]
         n_gain = d_model + q_rank + kv_rank
-        gs = jnp.concatenate(spread + [jnp.zeros(GAIN_ROWS * LANES - n_gain, jnp.float32)]).reshape(GAIN_ROWS, LANES)
-        shards = [wdq, arrange_dkv(wdkv, kv_rank), arrange_q(wuq), arrange_kv(wukv), wout]
+        like = lambda w, cols: jax.ShapeDtypeStruct((w.shape[0], cols), jnp.bfloat16)
+        gs, uq, ukv, dkv = pl.pallas_call(
+            prepare_kernel,
+            out_shape=[
+                jax.ShapeDtypeStruct((GAIN_ROWS, LANES), jnp.float32),
+                like(wuq, wuq.shape[1]), like(wukv, wukv.shape[1]), like(wdkv, kv_rank + LANES),
+            ],
+            name="prepare",
+        )(g1[None], gq[None], gkv[None], wuq, wukv, wdkv)
+        shards = [wdq, dkv, uq, ukv]
         full = lambda w, cols: pltpu.VMEM((w.shape[0] * n_fsdp, cols), jnp.bfloat16)
         o_cols = GROUP * VDIM
         n_groups = wuq.shape[1] // Q_COLS
@@ -600,7 +630,7 @@
                 vmem_limit_bytes=VMEM_LIMIT, dimension_semantics=("arbitrary",), collective_id=0, has_side_effects=True,
             ),
             name="core",
-        )(x, gs, *shards, cos, sin)
+        )(x, gs, *shards, wout, cos, sin)
         rows = 512
         tile = lambda cols: pl.BlockSpec((rows, cols), lambda i: (i, 0))
         r_tile = pl.BlockSpec((rows // seq_len, ROPE, seq_len), lambda i: (i, 0, 0))

time: 187 us -> 184 us (0.984)
  Pallas kernels: 171 us -> 177 us
  local copies, waits for them, and re-layouts: 8.63 us -> 3.05 us
  other arithmetic: 3.13 us -> 0 us
    pallas_call x0 -> x1, Pallas kernels: none -> 5.07 us  [local_block(): pl.pallas_call(prepare_kernel, out_shape=[jax.ShapeDtypeStruct((GAIN_ROWS...]
    reshape x4 -> x0, local copies, waits for them, and re-layouts: 3.9 us -> none  [the longest x3 2.66 us: arrange_kv(): w.reshape(rows, -1, GROUP, 2, NOPE).transpose(0, 1, 3, 2, 4)]
    slice x7 -> x0, local copies, waits for them, and re-layouts: 2.77 us -> none  [the longest x4 1.72 us: arrange_dkv(): lo, hi = (w[:, kv_rank:kv_rank + HALF], w[:, kv_rank + HALF:])]
    dynamic_update_slice x3 -> x0, other arithmetic: 2.32 us -> none  [local_block(): lax.dynamic_update_slice(jnp.zeros(g.shape[0] * n_fsdp, jnp.float32), g.a...]
where the time goes in v8:
time: 184 us; the launch traced here: 181 us
  Pallas kernels  177 us (96%)
  local copies, waits for them, and re-layouts  3.05 us (2%)
    pallas_call x1, Pallas kernels, local_block(): pl.pallas_call(functools.partial(core_kernel, n_p), grid=(4 * n_p + n_p /...  134 us
    pallas_call x1, Pallas kernels, local_block(): pl.pallas_call(out_kernel, grid=(n_p * seq_len // rows,), in_specs=[tile(...  37.8 us
    pallas_call x1, Pallas kernels, local_block(): pl.pallas_call(prepare_kernel, out_shape=[jax.ShapeDtypeStruct((GAIN_ROWS...  5.07 us

profile of v8, /device:TPU:0, one launch (start us, length us, event | category | flops | bytes accessed | tf_op | source)
XLA Modules:
  0.0 180.6 jit_solution(6944406398835979096)
XLA Ops:
  0.6 1.3 broadcast_in_dim.9.g1_ref
  1.9 1.8 copy.14.wdkv_ref
  3.7 5.1 %prepare.1 = (f32[32,128]{1,0:T(8,128)}, bf16[96,3840]{1,0:T(8,128)(2,1)}, bf16[32,5120]{1,0:T(8,128)(2,1)}, bf16[320,384]{1,0:T(8,128)(2,1)}) custom-call(bf16[1,320]{1,0:T(2,128)(2,1)} %broadcast_in_dim.9.g1_ref, bf16[1,96]{1,0:T(2,128)(2,1)} %bitcast.13, bf16[1,32]{1,0:T(2,128)(2,1)} %bitcast.14, bf16[96,3840]{1,0:T(8,128)(2,1)} %wuq_ref.1, ...), custom_call_target="tpu_custom_call" | custom-call | tf_op jit(solution)/shard_map/prepare/pallas_call | solution.py:580
  8.7 133.8 %core.1 = (bf16[8,256,256]{2,1,0:T(8,128)(2,1)}, bf16[8,32,256]{2,1,0:T(8,128)(2,1)}, bf16[8,256,1024]{2,1,0:T(8,128)(2,1)}, bf16[8,256,1536]{2,1,0:T(8,128)(2,1)}, bf16[2560,2560]{1,0:T(8,128)(2,1)}) custom-call(bf16[8,256,2560]{2,1,0:T(8,128)(2,1)} %x_ref.1, f32[32,128]{1,0:T(8,128)} %get-tuple-element.15.gs_ref, bf16[320,768]{1,0:T(8,128)(2,1)} %dq_s.1, ...), custom_call_target="tpu_custom_call" | custom-call | tf_op jit(solution)/shard_map/core/pallas_call | solution.py:599
  142.6 37.8 %project.1 = (bf16[2048,2560]{1,0:T(8,128)(2,1)}, bf16[2048,256]{1,0:T(8,128)(2,1)}, bf16[8,32,256]{2,1,0:T(8,128)(2,1)}) custom-call(bf16[2048,2560]{1,0:T(8,128)(2,1)} %bitcast.9, bf16[2048,1024]{1,0:T(8,128)(2,1)} %bitcast.11, bf16[2048,1536]{1,0:T(8,128)(2,1)} %bitcast.10, bf16[2560,2560]{1,0:T(8,128)(2,1)} %get-tuple-element.21.w_hbm, ...), custom_call_target="tpu_custom_call" | custom-call | tf_op jit(solution)/shard_map/project/pallas_call | solution.py:639

commit v9 on v8

--- a/solution.py
+++ b/solution.py
@@ -28,11 +28,19 @@
     angles = np.arange(seq_len)[:, None] * inv_freq[None, :]
     cos = np.tile(np.cos(angles), (1, LANES // HALF))
     sin = np.tile(np.sin(angles), (1, PE_TILE))
-    return cos.astype(np.float32), np.concatenate([-sin, sin], axis=1).astype(np.float32)
+    blank = np.zeros_like(angles)
+    twice = lambda *parts: np.tile(np.concatenate(parts + (blank, blank), axis=1), (1, 2))
+    one_cos, one_sin = np.cos(angles), np.sin(angles)
+    key = [twice(one_cos, one_cos), twice(-one_sin, blank), twice(blank, one_sin)]
+    return [v.astype(np.float32) for v in [cos, np.concatenate([-sin, sin], axis=1)] + key]
 
 
 def inv_rms(v):
     return lax.rsqrt(jnp.mean(v * v, axis=-1, keepdims=True) + EPSILON)
+
+
+def rotate_key(tile, cos, ahead, behind):
+    return tile * cos + pltpu.roll(tile, LANES - HALF, 1) * ahead + pltpu.roll(tile, HALF, 1) * behind
 
 
 def rotate(tile, cos, sin):
@@ -193,12 +201,15 @@
             self.own_copy(it).wait_send()
 
 
-def scores(tiles, slots, low, j):
+def scores(tiles, rt, low, j):
     qn, qp, kn, _ = tiles
     t = j // 2
-    keep = low if j % 2 == 0 else jnp.logical_not(low)
-    q_tile = jnp.concatenate([qn[t], qp[j // PE_TILE]], axis=0)
-    k_tile = jnp.concatenate([jnp.where(keep, kn[t], 0), slots[j % PE_TILE]], axis=1)
+    odd, slot, pe = j % 2, j % PE_TILE * HALF, qp[j // PE_TILE]
+    nope = qn[t][odd * NOPE:(odd + 1) * NOPE]
+    rotary = [pe[slot:slot + HALF], pe[LANES // 2 + slot:LANES // 2 + slot + HALF]]
+    rotary.append(jnp.zeros((LANES - NOPE - ROPE, pe.shape[1]), jnp.bfloat16))
+    q_tile = jnp.concatenate(rotary + [nope] if odd else [nope] + rotary, axis=0)
+    k_tile = jnp.where(low, rt, kn[t]) if odd else jnp.where(low, kn[t], rt)
     return jnp.dot(k_tile, q_tile, preferred_element_type=jnp.float32)
 
 
@@ -249,7 +260,6 @@
     low = lax.broadcasted_iota(jnp.int32, (1, LANES), 1) < NOPE
     diag = lax.broadcasted_iota(jnp.int32, (half, half), 0) <= lax.broadcasted_iota(jnp.int32, (half, half), 1)
     zero = jnp.zeros((half, half), jnp.bfloat16)
-    slots = slot_masks(rt)
     n_pieces = hold.shape[0] // 2
 
     def put(n, made):
@@ -284,7 +294,7 @@
                         put(n, m)
         if u + AHEAD < total:
             v = u + AHEAD
-            s[v] = scores(tiles[v // GROUP], slots, low, v % GROUP)
+            s[v] = scores(tiles[v // GROUP], rt, low, v % GROUP)
         if u >= 1:
             h = u - 1
             hj = h % GROUP
@@ -295,19 +305,14 @@
                 o_ref[0, :, h // 2 * LANES:(h // 2 + 1) * LANES] = pair.T
 
 
-def slot_masks(rt):
-    lane = lax.broadcasted_iota(jnp.int32, (1, LANES), 1)
-    slot = lax.rem(lane, LANES // 2) // HALF
-    return [jnp.where(slot == j, rt, 0) for j in range(PE_TILE)]
-
-
 def core_kernel(
-    n_prompts, x_ref, gs_ref, dq_s, dkv_s, uq_s, ukv_s, out_s, cos_ref, sin_ref,
+    n_prompts, x_ref, gs_ref, dq_s, dkv_s, uq_s, ukv_s, out_s, cos_ref, sin_ref, kcos, kahead, kbehind,
     c_all, r_ref, oa_ref, ob_ref, wout_ref,
     wdq, wdkv, wuqa, wuqb, wukva, wukvb, gains, gvec, a_all, acc, cq_all, rt_all, stage, hold,
     send_sem, recv_sem, g_send, g_recv, local_sem,
 ):
     i = pl.program_id(0)
+    key_tables = (kcos, kahead, kbehind)
     net = Net(send_sem, recv_sem)
     d, f = net.d, net.f
     n_a, m_a = wuqa.shape[1], wukva.shape[1]
@@ -382,32 +387,34 @@
         net.a5(its)
 
     plan = [
-        (1, [(net.send_z, first, one)]),
-        (2, [(net.send_z, rest, one)]),
-        (3, [(net.send_z, first, three)]),
-        (5, [(net.a2, down, one), (net.send_z, first, two)]),
-        (6, [(net.a3, down, one)]),
-        (7, [(net.a2, down, two)]),
-        (8, [(net.a4, down, one), (net.a2, down, three), (net.a5, down, one), (net.a3, down, two)]),
-        (9, [(net.a2, first, one)]),
-        (10, [(net.send_z, rest, three), (net.send_z, last, one)]),
-        (11, [(net.a4, down, two), (net.a3, down, three)]),
-        (12, [(net.a2, first, three), (net.a3, first, one), (net.a5, down, two), (net.send_z, rest, two)]),
-        (13, [(net.a2, first, two), (net.a2, rest, one), (net.a4, down, three)]),
-        (15, [(net.a3, first, two), (net.a5, down, three)]),
-        (16, [(net.a4, first, one), (net.a3, first, three), (net.a2, rest, three)]),
+        (0, [(net.send_z, rest, one), (net.send_z, first, two)]),
+        (3, [(net.a2, down, one)]),
+        (5, [(net.a3, down, one), (net.send_z, first, three)]),
+        (6, [(net.a2, down, two)]),
+        (7, [(net.a4, down, one), (net.a2, down, three)]),
+        (8, [(net.send_z, first, one), (net.a5, down, one)]),
+        (9, [(net.a3, down, two)]),
+        (10, [(net.a3, down, three)]),
+        (11, [(net.a4, down, two), (net.a2, first, two)]),
+        (12, [(net.a2, first, three), (net.a4, down, three), (net.a5, down, two), (net.send_z, rest, two)]),
+        (13, [(net.a2, first, one)]),
+        (14, [(net.a5, down, three)]),
+        (15, [(net.a3, first, two), (net.send_z, rest, three), (net.a3, first, three)]),
+        (16, [(net.a3, first, one)]),
         (17, [(net.a4, first, two)]),
-        (19, [(net.a4, first, three), (net.a3, rest, three)]),
-        (20, [(net.send_z, last, two), (net.a2, rest, two)]),
-        (21, [(net.a3, rest, one)]),
-        (22, [(net.a2, last, one)]),
-        (24, [(net.a4, rest, one), (net.send_z, last, three)]),
-        (25, [(net.a3, rest, two), (net.a4, rest, three)]),
-        (27, [(net.a4, rest, two), (net.a2, last, two)]),
-        (28, [(net.a3, last, one)]),
-        (29, [(net.a2, last, three)]),
-        (31, [(net.a3, last, two)]),
-        (32, [(net.a4, last, one)]),
+        (18, [(net.a2, rest, two), (net.send_z, last, one), (net.a4, first, three), (net.a4, first, one)]),
+        (19, [(net.a2, rest, one)]),
+        (20, [(net.send_z, last, two)]),
+        (21, [(net.a2, rest, three), (net.a3, rest, two)]),
+        (22, [(net.a3, rest, one), (net.send_z, last, three)]),
+        (23, [(net.a3, rest, three), (net.a2, last, one)]),
+        (24, [(net.a4, rest, two)]),
+        (25, [(net.a4, rest, one)]),
+        (26, [(net.a4, rest, three)]),
+        (28, [(net.a2, last, two)]),
+        (29, [(net.a3, last, one)]),
+        (30, [(net.a2, last, three)]),
+        (31, [(net.a3, last, two), (net.a4, last, one)]),
         (33, [(net.a3, last, three)]),
         (34, [(net.a4, last, two)]),
         (35, [(net.a4, last, three)]),
@@ -464,10 +471,9 @@
         c_all[pl.ds(p, 2)] = lat.reshape(2, seq_len, kv_rank)
         for n in range(2):
             pe = kd[n * seq_len:(n + 1) * seq_len, kv_rank:]
-            rt = rotate(pe, cos_ref[...], sin_ref[...]).astype(jnp.bfloat16)
+            rt = rotate_key(pe, *[t[...] for t in key_tables]).astype(jnp.bfloat16)
             rt_all[p + n] = rt
-            rt_t = rt.T
-            r_ref[p + n] = jnp.concatenate([rt_t[:HALF], rt_t[LANES // 2:LANES // 2 + HALF]], axis=0)
+            r_ref[p + n] = rt.T[:ROPE]
 
     def attend_step(p, wuq, wukv, o_ref):
         after = jnp.minimum(p + 1, n_prompts - 1)
@@ -534,9 +540,11 @@
 
     kv_rank = dkv_ref.shape[1] - LANES
     c = column(LANES)
-    dkv_ref[:, :kv_rank] = wdkv_ref[:, :kv_rank]
-    order = one_hot(c // (LANES // 2) * HALF + lax.rem(c, HALF), ROPE)
-    dkv_ref[:, kv_rank:] = pick(wdkv_ref[:, kv_rank:], order)
+    wdkv = wdkv_ref[...].T
+    dkv_ref[:, :kv_rank] = wdkv[:, :kv_rank]
+    c = lax.rem(c, LANES // 2)
+    order = one_hot(jnp.where(c < ROPE, c, -1), ROPE)
+    dkv_ref[:, kv_rank:] = pick(wdkv[:, kv_rank:], order)
 
 
 def out_kernel(x_ref, oa_ref, ob_ref, w_hbm, c_in, r_in, y_ref, c_out, r_out, w, sem):
@@ -546,21 +554,26 @@
     cols = [slice(n * step, (n + 1) * step) for n in range(n_steps)]
     load = [pltpu.make_async_copy(w_hbm.at[:, c], w.at[:, c], sem.at[n]) for n, c in enumerate(cols)]
 
-    @pl.when(first)
-    def _():
-        for part in load:
-            part.start()
-
     o = jnp.concatenate([oa_ref[...], ob_ref[...]], axis=1)
     c_out[...] = c_in[...]
     r_out[...] = r_in[...]
-    for part, c in zip(load, cols):
-        @pl.when(first)
-        def _(part=part):
-            part.wait()
-
+
+    def product(c):
         acc = jnp.dot(o, w[:, c], preferred_element_type=jnp.float32)
         y_ref[:, c] = (x_ref[:, c].astype(jnp.float32) + acc).astype(jnp.bfloat16)
+
+    @pl.when(first)
+    def _():
+        for part in load:
+            part.start()
+        for part, c in zip(load, cols):
+            part.wait()
+            product(c)
+
+    @pl.when(jnp.logical_not(first))
+    def _():
+        for c in cols:
+            product(c)
 
 
 def whole(shape):
@@ -573,8 +586,7 @@
     def local_block(x, g1, wdq, gq, wuq, wdkv, gkv, wukv, wout):
         n_p, seq_len, d_model = x.shape
         kv_rank, q_rank = gkv.shape[0] * n_fsdp, wdq.shape[1]
-        cos_np, sin_np = rope_tiles(seq_len)
-        cos, sin = jnp.asarray(cos_np), jnp.asarray(sin_np)
+        tables = [jnp.asarray(t) for t in rope_tiles(seq_len)]
         n_gain = d_model + q_rank + kv_rank
         like = lambda w, cols: jax.ShapeDtypeStruct((w.shape[0], cols), jnp.bfloat16)
         gs, uq, ukv, dkv = pl.pallas_call(
@@ -584,7 +596,7 @@
                 like(wuq, wuq.shape[1]), like(wukv, wukv.shape[1]), like(wdkv, kv_rank + LANES),
             ],
             name="prepare",
-        )(g1[None], gq[None], gkv[None], wuq, wukv, wdkv)
+        )(g1[None], gq[None], gkv[None], wuq, wukv, wdkv.T)
         shards = [wdq, dkv, uq, ukv]
         full = lambda w, cols: pltpu.VMEM((w.shape[0] * n_fsdp, cols), jnp.bfloat16)
         o_cols = GROUP * VDIM
@@ -599,7 +611,7 @@
         c, r, oa, ob, wout_all = pl.pallas_call(
             functools.partial(core_kernel, n_p),
             grid=(4 * n_p + n_p // 2,),
-            in_specs=[blk(d_model, 0)] + [hbm] * 6 + [whole(cos.shape)] * 2,
+            in_specs=[blk(d_model, 0)] + [hbm] * 6 + [whole(tables[0].shape)] * len(tables),
             out_specs=[
                 whole((n_p, seq_len, kv_rank)), whole((n_p, ROPE, seq_len)),
                 blk(first * o_cols, pa), blk(rest * o_cols, pa + n_p), hbm,
@@ -630,7 +642,7 @@
                 vmem_limit_bytes=VMEM_LIMIT, dimension_semantics=("arbitrary",), collective_id=0, has_side_effects=True,
             ),
             name="core",
-        )(x, gs, *shards, wout, cos, sin)
+        )(x, gs, *shards, wout, *tables)
         rows = 512
         tile = lambda cols: pl.BlockSpec((rows, cols), lambda i: (i, 0))
         r_tile = pl.BlockSpec((rows // seq_len, ROPE, seq_len), lambda i: (i, 0, 0))

time: 184 us -> 187 us (1.016)
  the two profiles are of different devices: /device:TPU:0 before, /device:TPU:17 now
where the time goes in v9:
time: 187 us
  Pallas kernels  185 us (99%)
    pallas_call x1, Pallas kernels, local_block(): pl.pallas_call(functools.partial(core_kernel, n_p), grid=(4 * n_p + n_p /...  144 us
    pallas_call x1, Pallas kernels, local_block(): pl.pallas_call(out_kernel, grid=(n_p * seq_len // rows,), in_specs=[tile(...  35.9 us
    pallas_call x1, Pallas kernels, local_block(): pl.pallas_call(prepare_kernel, out_shape=[jax.ShapeDtypeStruct((GAIN_ROWS...  5.07 us

profile of v9, /device:TPU:17, one launch (start us, length us, event | category | flops | bytes accessed | tf_op | source)
XLA Modules:
  0.0 187.2 jit_solution(8417059905577887274)
XLA Ops:
  0.6 1.3 broadcast_in_dim.9.g1_ref
  1.9 5.1 %prepare.1 = (f32[32,128]{1,0:T(8,128)}, bf16[96,3840]{1,0:T(8,128)(2,1)}, bf16[32,5120]{1,0:T(8,128)(2,1)}, bf16[320,384]{1,0:T(8,128)(2,1)}) custom-call(bf16[1,320]{1,0:T(2,128)(2,1)} %broadcast_in_dim.9.g1_ref, bf16[1,96]{1,0:T(2,128)(2,1)} %bitcast.15, bf16[1,32]{1,0:T(2,128)(2,1)} %bitcast.16, bf16[96,3840]{1,0:T(8,128)(2,1)} %wuq_ref.1, ...), custom_call_target="tpu_custom_call" | custom-call | tf_op jit(solution)/shard_map/prepare/pallas_call | solution.py:592
  7.0 144.1 %core.1 = (bf16[8,256,256]{2,1,0:T(8,128)(2,1)}, bf16[8,32,256]{2,1,0:T(8,128)(2,1)}, bf16[8,256,1024]{2,1,0:T(8,128)(2,1)}, bf16[8,256,1536]{2,1,0:T(8,128)(2,1)}, bf16[2560,2560]{1,0:T(8,128)(2,1)}) custom-call(bf16[8,256,2560]{2,1,0:T(8,128)(2,1)} %x_ref.1, f32[32,128]{1,0:T(8,128)} %get-tuple-element.15.gs_ref, bf16[320,768]{1,0:T(8,128)(2,1)} %dq_s.1, ...), custom_call_target="tpu_custom_call" | custom-call | tf_op jit(solution)/shard_map/core/pallas_call | solution.py:611
  151.0 35.9 %project.1 = (bf16[2048,2560]{1,0:T(8,128)(2,1)}, bf16[2048,256]{1,0:T(8,128)(2,1)}, bf16[8,32,256]{2,1,0:T(8,128)(2,1)}) custom-call(bf16[2048,2560]{1,0:T(8,128)(2,1)} %bitcast.10, bf16[2048,1024]{1,0:T(8,128)(2,1)} %bitcast.12, bf16[2048,1536]{1,0:T(8,128)(2,1)} %bitcast.11, bf16[2560,2560]{1,0:T(8,128)(2,1)} %get-tuple-element.21.w_hbm, ...), custom_call_target="tpu_custom_call" | custom-call | tf_op jit(solution)/shard_map/project/pallas_call | solution.py:651

commit v10 on v9

--- a/solution.py
+++ b/solution.py
@@ -387,34 +387,32 @@
         net.a5(its)
 
     plan = [
-        (0, [(net.send_z, rest, one), (net.send_z, first, two)]),
-        (3, [(net.a2, down, one)]),
-        (5, [(net.a3, down, one), (net.send_z, first, three)]),
-        (6, [(net.a2, down, two)]),
-        (7, [(net.a4, down, one), (net.a2, down, three)]),
-        (8, [(net.send_z, first, one), (net.a5, down, one)]),
-        (9, [(net.a3, down, two)]),
-        (10, [(net.a3, down, three)]),
-        (11, [(net.a4, down, two), (net.a2, first, two)]),
-        (12, [(net.a2, first, three), (net.a4, down, three), (net.a5, down, two), (net.send_z, rest, two)]),
-        (13, [(net.a2, first, one)]),
-        (14, [(net.a5, down, three)]),
-        (15, [(net.a3, first, two), (net.send_z, rest, three), (net.a3, first, three)]),
-        (16, [(net.a3, first, one)]),
+        (1, [(net.send_z, first, one)]),
+        (2, [(net.send_z, rest, one)]),
+        (3, [(net.send_z, first, three)]),
+        (5, [(net.a2, down, one), (net.send_z, first, two)]),
+        (6, [(net.a3, down, one)]),
+        (7, [(net.a2, down, two)]),
+        (8, [(net.a4, down, one), (net.a2, down, three), (net.a5, down, one), (net.a3, down, two)]),
+        (9, [(net.a2, first, one)]),
+        (10, [(net.send_z, rest, three), (net.send_z, last, one)]),
+        (11, [(net.a4, down, two), (net.a3, down, three)]),
+        (12, [(net.a2, first, three), (net.a3, first, one), (net.a5, down, two), (net.send_z, rest, two)]),
+        (13, [(net.a2, first, two), (net.a2, rest, one), (net.a4, down, three)]),
+        (15, [(net.a3, first, two), (net.a5, down, three)]),
+        (16, [(net.a4, first, one), (net.a3, first, three), (net.a2, rest, three)]),
         (17, [(net.a4, first, two)]),
-        (18, [(net.a2, rest, two), (net.send_z, last, one), (net.a4, first, three), (net.a4, first, one)]),
-        (19, [(net.a2, rest, one)]),
-        (20, [(net.send_z, last, two)]),
-        (21, [(net.a2, rest, three), (net.a3, rest, two)]),
-        (22, [(net.a3, rest, one), (net.send_z, last, three)]),
-        (23, [(net.a3, rest, three), (net.a2, last, one)]),
-        (24, [(net.a4, rest, two)]),
-        (25, [(net.a4, rest, one)]),
-        (26, [(net.a4, rest, three)]),
-        (28, [(net.a2, last, two)]),
-        (29, [(net.a3, last, one)]),
-        (30, [(net.a2, last, three)]),
-        (31, [(net.a3, last, two), (net.a4, last, one)]),
+        (19, [(net.a4, first, three), (net.a3, rest, three)]),
+        (20, [(net.send_z, last, two), (net.a2, rest, two)]),
+        (21, [(net.a3, rest, one)]),
+        (22, [(net.a2, last, one)]),
+        (24, [(net.a4, rest, one), (net.send_z, last, three)]),
+        (25, [(net.a3, rest, two), (net.a4, rest, three)]),
+        (27, [(net.a4, rest, two), (net.a2, last, two)]),
+        (28, [(net.a3, last, one)]),
+        (29, [(net.a2, last, three)]),
+        (31, [(net.a3, last, two)]),
+        (32, [(net.a4, last, one)]),
         (33, [(net.a3, last, three)]),
         (34, [(net.a4, last, two)]),
         (35, [(net.a4, last, three)]),

time: 187 us -> 180 us (0.963)
  the two profiles are of different devices: /device:TPU:17 before, /device:TPU:0 now
where the time goes in v10:
time: 180 us; the launch traced here: 177 us
  Pallas kernels  175 us (97%)
    pallas_call x1, Pallas kernels, local_block(): pl.pallas_call(functools.partial(core_kernel, n_p), grid=(4 * n_p + n_p /...  134 us
    pallas_call x1, Pallas kernels, local_block(): pl.pallas_call(out_kernel, grid=(n_p * seq_len // rows,), in_specs=[tile(...  35.9 us
    pallas_call x1, Pallas kernels, local_block(): pl.pallas_call(prepare_kernel, out_shape=[jax.ShapeDtypeStruct((GAIN_ROWS...  5.07 us

profile of v10, /device:TPU:0, one launch (start us, length us, event | category | flops | bytes accessed | tf_op | source)
XLA Modules:
  0.0 176.9 jit_solution(8359481760923870301)
XLA Ops:
  0.6 1.3 broadcast_in_dim.9.g1_ref
  1.9 5.1 %prepare.1 = (f32[32,128]{1,0:T(8,128)}, bf16[96,3840]{1,0:T(8,128)(2,1)}, bf16[32,5120]{1,0:T(8,128)(2,1)}, bf16[320,384]{1,0:T(8,128)(2,1)}) custom-call(bf16[1,320]{1,0:T(2,128)(2,1)} %broadcast_in_dim.9.g1_ref, bf16[1,96]{1,0:T(2,128)(2,1)} %bitcast.15, bf16[1,32]{1,0:T(2,128)(2,1)} %bitcast.16, bf16[96,3840]{1,0:T(8,128)(2,1)} %wuq_ref.1, ...), custom_call_target="tpu_custom_call" | custom-call | tf_op jit(solution)/shard_map/prepare/pallas_call | solution.py:590
  7.0 133.8 %core.1 = (bf16[8,256,256]{2,1,0:T(8,128)(2,1)}, bf16[8,32,256]{2,1,0:T(8,128)(2,1)}, bf16[8,256,1024]{2,1,0:T(8,128)(2,1)}, bf16[8,256,1536]{2,1,0:T(8,128)(2,1)}, bf16[2560,2560]{1,0:T(8,128)(2,1)}) custom-call(bf16[8,256,2560]{2,1,0:T(8,128)(2,1)} %x_ref.1, f32[32,128]{1,0:T(8,128)} %get-tuple-element.15.gs_ref, bf16[320,768]{1,0:T(8,128)(2,1)} %dq_s.1, ...), custom_call_target="tpu_custom_call" | custom-call | tf_op jit(solution)/shard_map/core/pallas_call | solution.py:609
  140.8 35.9 %project.1 = (bf16[2048,2560]{1,0:T(8,128)(2,1)}, bf16[2048,256]{1,0:T(8,128)(2,1)}, bf16[8,32,256]{2,1,0:T(8,128)(2,1)}) custom-call(bf16[2048,2560]{1,0:T(8,128)(2,1)} %bitcast.10, bf16[2048,1024]{1,0:T(8,128)(2,1)} %bitcast.12, bf16[2048,1536]{1,0:T(8,128)(2,1)} %bitcast.11, bf16[2560,2560]{1,0:T(8,128)(2,1)} %get-tuple-element.21.w_hbm, ...), custom_call_target="tpu_custom_call" | custom-call | tf_op jit(solution)/shard_map/project/pallas_call | solution.py:649
